TPU v7x, 16 devices: a whole 2x2x2 slice. The times are simulated.
16 devices in a mesh: dp: 4 (over z, y), tp: 4 (over x, core).
Axes of the slice: x: 2, y: 2, z: 2, core: 2. Of those that a mesh axis runs over, the one named last changes fastest.
Arguments:
- hidden: bfloat16 [48, 264, 1408], P('dp'), parts along dimension 0
- inter_feats: bfloat16 [48, 264, 5, 1408], P('dp'), parts along dimension 0
- proj_grad: bfloat16 [48, 257, 2560], P('dp'), parts along dimension 0
- w_query: bfloat16 [1408, 16, 88], P(None, 'tp')
- w_key: bfloat16 [1408, 16, 88], P(None, 'tp')
- w_value: bfloat16 [1408, 16, 88], P(None, 'tp')
- w_out: bfloat16 [16, 88, 1408], P('tp')
- ln_params: float32 [4, 1408], replicated
- gate_params: float32 [2], replicated
- w_fc1: bfloat16 [1408, 6144], P(None, 'tp')
- b_fc1: float32 [6144], P('tp')
- w_fc2: bfloat16 [6144, 1408], P('tp')
- b_fc2: float32 [1408], replicated
- w_proj: bfloat16 [8448, 2560], P('tp')
- b_proj: float32 [2560], replicated
Outputs:
- output 1: bfloat16 [48, 257, 2560], P(('dp', 'tp')), parts along dimension 0
- output 2: bfloat16 [48, 264, 1408], P('dp'), parts along dimension 0
- output 3: bfloat16 [48, 264, 5, 1408], P('dp'), parts along dimension 0
- output 4: float32 [5632, 16, 88], P('dp', 'tp'), parts along dimension 0
- output 5: float32 [5632, 16, 88], P('dp', 'tp'), parts along dimension 0
- output 6: float32 [5632, 16, 88], P('dp', 'tp'), parts along dimension 0
- output 7: float32 [64, 88, 1408], P(('dp', 'tp')), parts along dimension 0
- output 8: float32 [16, 1408], P('dp'), parts along dimension 0
- output 9: float32 [8], P('dp'), parts along dimension 0
- output 10: float32 [5632, 6144], P('dp', 'tp'), parts along dimension 0
- output 11: float32 [24576], P(('dp', 'tp')), parts along dimension 0
- output 12: float32 [24576, 1408], P(('dp', 'tp')), parts along dimension 0
- output 13: float32 [5632], P('dp'), parts along dimension 0
- output 14: float32 [33792, 2560], P(('dp', 'tp')), parts along dimension 0
- output 15: float32 [10240], P('dp'), parts along dimension 0
There are 4 independent parts. A program takes and returns all parts, laid end to end along the dimension named above; an argument that names none is the same for every part.
All inputs are finite; a program needn't handle non-finite values.
Results may differ from a plain program's by a relative error of at most 0.0195166.
Values are sent between devices in bfloat16 or wider.
A program may use at most 1 GiB of HBM per device.

v0:
```python
import functools
import jax
import jax.numpy as jnp
from jax import lax
from jax.sharding import PartitionSpec as P

LN_EPS = 1e-5


def layer_norm(values, ln_gain, ln_bias):
    row_mean = jnp.mean(values, axis=-1, keepdims=True)
    centred = values - row_mean
    row_var = jnp.mean(centred * centred, axis=-1, keepdims=True)
    return (centred * lax.rsqrt(row_var + LN_EPS) * ln_gain + ln_bias).astype(jnp.bfloat16)


def gelu_bf16(pre_act):
    return jax.nn.gelu(pre_act, approximate=False).astype(jnp.bfloat16)


def matmul(eq_form, lhs_in, rhs_in):
    return jnp.einsum(eq_form, lhs_in, rhs_in, preferred_element_type=jnp.float32)


def attend(real_rows, q_act, k_act, v_act):
    tokens = q_act.shape[1]
    score_scale = q_act.shape[3] ** -0.5
    scores = matmul('bqhe,bkhe->bhqk', q_act, k_act) * score_scale
    key_ok = (jnp.arange(tokens) < real_rows)[None, None, None, :]
    attn_probs = jax.nn.softmax(jnp.where(key_ok, scores, -1e30), axis=-1).astype(jnp.bfloat16)
    return matmul('bhqk,bkhe->bqhe', attn_probs, v_act).astype(jnp.bfloat16)


def group_sum(part_sum):
    return lax.psum(part_sum.astype(jnp.bfloat16), 'tp').astype(jnp.float32)


def local_step(hidden, inter_feats, proj_grad, w_query, w_key, w_value, w_out, ln_params, gate_params, w_fc1, b_fc1, w_fc2, b_fc2, w_proj, b_proj):
    tile_count, tokens, width = hidden.shape
    real_rows = proj_grad.shape[1]
    feat_local = w_proj.shape[0]
    x_wide = hidden.astype(jnp.float32)
    normed, norm1_pull = jax.vjp(layer_norm, x_wide, ln_params[0], ln_params[1])
    q_act = matmul('btd,dhe->bthe', normed, w_query).astype(jnp.bfloat16)
    k_act = matmul('btd,dhe->bthe', normed, w_key).astype(jnp.bfloat16)
    v_act = matmul('btd,dhe->bthe', normed, w_value).astype(jnp.bfloat16)
    context, attend_pull = jax.vjp(functools.partial(attend, real_rows), q_act, k_act, v_act)
    attn_out = group_sum(matmul('bthe,hed->btd', context, w_out))
    gate_attn = jnp.tanh(gate_params[0])
    gate_mlp = jnp.tanh(gate_params[1])
    x_one = (x_wide + gate_attn * attn_out).astype(jnp.bfloat16)
    x_one_wide = x_one.astype(jnp.float32)
    normed_two, norm2_pull = jax.vjp(layer_norm, x_one_wide, ln_params[2], ln_params[3])
    pre_act = matmul('btd,df->btf', normed_two, w_fc1) + b_fc1
    mlp_act, gelu_pull = jax.vjp(gelu_bf16, pre_act)
    mlp_out = group_sum(matmul('btf,fd->btd', mlp_act, w_fc2)) + b_fc2
    x_two = (x_one_wide + gate_mlp * mlp_out).astype(jnp.bfloat16)
    features = jnp.concatenate([x_two[:, :real_rows], inter_feats[:, :real_rows].reshape(tile_count, real_rows, -1)], axis=-1)
    feats_local = lax.dynamic_slice_in_dim(features, lax.axis_index('tp') * feat_local, feat_local, axis=2)
    proj_part = matmul('btc,cp->btp', feats_local, w_proj).astype(jnp.bfloat16)
    proj_sum = lax.psum_scatter(proj_part, 'tp', scatter_dimension=0, tiled=True)
    proj_out = (proj_sum.astype(jnp.float32) + b_proj).astype(jnp.bfloat16)

    grad_b_proj = jnp.sum(proj_grad, axis=(0, 1), dtype=jnp.float32)
    grad_w_proj = matmul('btc,btp->cp', feats_local, proj_grad)
    grad_feats_local = matmul('btp,cp->btc', proj_grad, w_proj).astype(jnp.bfloat16)
    grad_feats = lax.all_gather(grad_feats_local, 'tp', axis=2, tiled=True)
    pad_rows = ((0, 0), (0, tokens - real_rows), (0, 0))
    grad_x_two = jnp.pad(grad_feats[:, :, :width], pad_rows).astype(jnp.float32)
    grad_inter = jnp.pad(grad_feats[:, :, width:], pad_rows).reshape(inter_feats.shape)
    grad_mlp = gate_mlp * grad_x_two
    grad_gate_mlp = jnp.sum(grad_x_two * mlp_out) * (1.0 - gate_mlp * gate_mlp)
    grad_b_fc2 = jnp.sum(grad_mlp, axis=(0, 1))
    grad_mlp_low = grad_mlp.astype(jnp.bfloat16)
    grad_w_fc2 = matmul('btf,btd->fd', mlp_act, grad_mlp_low)
    grad_act = matmul('btd,fd->btf', grad_mlp_low, w_fc2).astype(jnp.bfloat16)
    grad_pre = gelu_pull(grad_act)[0]
    grad_b_fc1 = jnp.sum(grad_pre, axis=(0, 1))
    grad_pre_low = grad_pre.astype(jnp.bfloat16)
    grad_w_fc1 = matmul('btd,btf->df', normed_two, grad_pre_low)
    grad_normed_two = group_sum(matmul('btf,df->btd', grad_pre_low, w_fc1)).astype(jnp.bfloat16)
    grad_x_ln_two, grad_gain_two, grad_bias_two = norm2_pull(grad_normed_two)
    grad_x_one = (grad_x_two + grad_x_ln_two).astype(jnp.bfloat16).astype(jnp.float32)
    grad_attn = gate_attn * grad_x_one
    grad_gate_attn = jnp.sum(grad_x_one * attn_out) * (1.0 - gate_attn * gate_attn)
    grad_attn_low = grad_attn.astype(jnp.bfloat16)
    grad_w_out = matmul('bthe,btd->hed', context, grad_attn_low)
    grad_context = matmul('btd,hed->bthe', grad_attn_low, w_out).astype(jnp.bfloat16)
    grad_q, grad_k, grad_v = attend_pull(grad_context)
    grad_w_query = matmul('btd,bthe->dhe', normed, grad_q)
    grad_w_key = matmul('btd,bthe->dhe', normed, grad_k)
    grad_w_value = matmul('btd,bthe->dhe', normed, grad_v)
    grad_normed_sum = matmul('bthe,dhe->btd', grad_q, w_query) + matmul('bthe,dhe->btd', grad_k, w_key) + matmul('bthe,dhe->btd', grad_v, w_value)
    grad_normed = group_sum(grad_normed_sum).astype(jnp.bfloat16)
    grad_x_ln, grad_gain, grad_bias = norm1_pull(grad_normed)
    grad_hidden = (grad_x_one + grad_x_ln).astype(jnp.bfloat16)
    grad_ln = jnp.stack([grad_gain, grad_bias, grad_gain_two, grad_bias_two])
    grad_gates = jnp.stack([grad_gate_attn, grad_gate_mlp])
    return (proj_out, grad_hidden, grad_inter, grad_w_query, grad_w_key, grad_w_value, grad_w_out, grad_ln, grad_gates, grad_w_fc1, grad_b_fc1, grad_w_fc2, grad_b_fc2, grad_w_proj, grad_b_proj)


def solution(mesh):
    tiles_spec = P('dp', None, None)
    inter_spec = P('dp', None, None, None)
    head_cols = P(None, 'tp', None)
    in_specs = (tiles_spec, inter_spec, tiles_spec, head_cols, head_cols, head_cols, P('tp', None, None), P(None, None), P(None), P(None, 'tp'), P('tp'), P('tp', None), P(None), P('tp', None), P(None))
    grad_heads = P('dp', 'tp', None)
    out_specs = (P(('dp', 'tp'), None, None), tiles_spec, inter_spec, grad_heads, grad_heads, grad_heads, P(('dp', 'tp'), None, None), P('dp', None), P('dp'), P('dp', 'tp'), P(('dp', 'tp')), P(('dp', 'tp'), None), P('dp'), P(('dp', 'tp'), None), P('dp'))
    return jax.shard_map(local_step, mesh=mesh, in_specs=in_specs, out_specs=out_specs, check_vma=False)
```

profile of v0, /device:TPU:0, one launch (start us, length us, event | category | flops | bytes accessed | tf_op | source)
XLA Modules:
  0.0 2021.1 jit_solution(12422544017701478836)
XLA Ops:
  82.3 45.3 %convolution_convert_fusion = bf16[12,257,2112]{2,1,0:T(8,128)(2,1)} fusion(bf16[12,257,2560]{2,1,0:T(8,128)(2,1)} %param.17, bf16[2112,2560]{1,0:T(8,128)(2,1)} %param.28), kind=kOutput, calls=%fused_computation.37 | convolution fusion | flops 33355161600 | bytes 39630336 | tf_op jit(solution)/shard_map/btp,cp->btc/dot_general | solution.py:22
  127.6 31.6 %copy.62 = bf16[12,257,2112]{1,0,2:T(8,128)(2,1)} copy(bf16[12,257,2112]{2,1,0:T(8,128)(2,1)} %convolution_convert_fusion) | data formatting | bytes 26053632 | tf_op jit(solution)/shard_map/convert_element_type | solution.py:66
  161.8 81.6 %all-reduce.8.cloned.1.call-done = bf16[12,264,1408]{2,1,0:T(8,128)(2,1)} async-done(((bf16[12,264,1408]{2,1,0:T(8,128)(2,1)}), bf16[12,264,1408]{2,1,0:T(8,128)(2,1)}) %all-reduce.8.cloned.1.call-update) | async-done | bytes 8921104 | tf_op jit(solution)/shard_map/psum | solution.py:35
  254.2 28.4 %fusion.53 = (u16[264,1536]{1,0:T(8,128)(2,1)S(1)}, u16[264,1536]{1,0:T(8,128)(2,1)S(1)}, f32[12,264,1536]{2,1,0:T(8,128)}) fusion(f32[1536]{0:T(1024)S(1)} %copy-done.56, bf16[1408,1536]{1,0:T(8,128)(2,1)} %param.24, bf16[12,264,1408]{2,1,0:T(8,128)(2,1)S(1)} %get-tuple-element.81, f32[1408]{0:T(1024)S(1)} %copy-done.46, f32[1408]{0:T(1024)S(1)} %copy-done.37, ...), kind=kOutput, calls=%fused_computation.111 | convolution fusion | flops 13796868096 | bytes 34375424 | tf_op jit(solution)/shard_map/btd,df->btf/dot_general | solution.py:22
  282.6 45.9 %multiply_convert_fusion = (bf16[12,264,1536]{2,1,0:T(8,128)(2,1)}, f32[12,264,1536]{2,1,0:T(8,128)}) fusion(f32[12,264,1536]{2,1,0:T(8,128)} %get-tuple-element.87, u16[264,1536]{1,0:T(8,128)(2,1)S(1)} %get-tuple-element.61, u16[264,1536]{1,0:T(8,128)(2,1)S(1)} %get-tuple-element.60), kind=kLoop, calls=%fused_computation.57 | loop fusion | flops 340623360 | bytes 50282496 | tf_op jit(solution)/shard_map/jvp()/convert_element_type | solution.py:18
  328.6 517.6 %all-gather.2.cloned.1.call-done = bf16[12,257,8448]{1,0,2:T(8,128)(2,1)} async-done(((bf16[12,257,2112]{1,0,2:T(8,128)(2,1)}), bf16[12,257,8448]{1,0,2:T(8,128)(2,1)}) %all-gather.2.cloned.1.call-update) | async-done | bytes 52107280 | tf_op jit(solution)/shard_map/all_gather | solution.py:67
  860.8 20.5 %copy.97 = bf16[12,257,1408]{2,1,0:T(8,128)(2,1)} copy(bf16[12,257,1408]{1,0,2:T(8,128)(2,1)} %slice.42) | data formatting | bytes 17369088
  881.3 30.4 %fusion.130 = (f32[1536]{0:T(1024)}, bf16[12,264,1536]{2,1,0:T(8,128)(2,1)}) fusion(f32[12,264,1536]{2,1,0:T(8,128)} %get-tuple-element.79, f32[12,264,1536]{2,1,0:T(8,128)} %get-tuple-element.87, bf16[1536,1408]{1,0:T(8,128)(2,1)} %param.26, f32[]{:T(128)} %bitcast.11, bf16[12,257,1408]{2,1,0:T(8,128)(2,1)} %copy.97), kind=kOutput, calls=%fused_computation.190 | convolution fusion | flops 13798893568 | bytes 61676548 | tf_op jit(solution)/shard_map/btd,fd->btf/dot_general | solution.py:22
  911.7 20.7 %convolution_convert_fusion.2 = bf16[12,264,1408]{2,1,0:T(8,128)(2,1)} fusion(bf16[12,264,1536]{2,1,0:T(8,128)(2,1)} %get-tuple-element.91, bf16[1408,1536]{1,0:T(8,128)(2,1)} %param.24), kind=kOutput, calls=%fused_computation.101 | convolution fusion | flops 13707251712 | bytes 22978560 | tf_op jit(solution)/shard_map/btf,df->btd/dot_general | solution.py:22
  932.5 20.8 %convolution_convert_fusion.4 = bf16[12,264,1408]{2,1,0:T(8,128)(2,1)} fusion(bf16[12,264,1536]{2,1,0:T(8,128)(2,1)} %get-tuple-element.78, bf16[1536,1408]{1,0:T(8,128)(2,1)} %param.26), kind=kOutput, calls=%fused_computation.103 | convolution fusion | flops 13707251712 | bytes 22978560 | tf_op jit(solution)/shard_map/btf,fd->btd/dot_general | solution.py:22
  953.3 137.4 %all-reduce.10.cloned.1.call-done = bf16[12,264,1408]{2,1,0:T(8,128)(2,1)} async-done(((bf16[12,264,1408]{2,1,0:T(8,128)(2,1)}), bf16[12,264,1408]{2,1,0:T(8,128)(2,1)}) %all-reduce.10.cloned.1.call-update) | async-done | bytes 8921104 | tf_op jit(solution)/shard_map/psum | solution.py:35
  1113.3 16.3 fusion.40
  1215.5 18.6 fusion.43
  1234.1 37.8 %copy.61 = bf16[12,257,5,1408]{3,2,1,0:T(8,128)(2,1)} copy(bf16[12,257,5,1408]{3,1,2,0:T(8,128)(2,1)} %bitcast.168) | data formatting | bytes 86845440 | tf_op jit(solution)/shard_map/slice | solution.py:58
  1272.0 121.1 %reshape.125 = bf16[12,257,7040]{2,1,0:T(8,128)(2,1)} reshape(bf16[12,257,5,1408]{3,2,1,0:T(8,128)(2,1)} %copy.61) | data formatting | bytes 86845440 | tf_op jit(solution)/shard_map/reshape | solution.py:58
  1404.3 131.7 %all-reduce.12.cloned.1.call-done = (bf16[12,264,1408]{2,1,0:T(8,128)(2,1)}, bf16[12,264,1408]{2,1,0:T(8,128)(2,1)}) async-done(((bf16[12,264,1408]{2,1,0:T(8,128)(2,1)}, bf16[12,264,1408]{2,1,0:T(8,128)(2,1)}), (bf16[12,264,1408]{2,1,0:T(8,128)(2,1)}, bf16[12,264,1408]{2,1,0:T(8,128)(2,1)})) %all-reduce.12.cloned.1.call-update) | async-done | bytes 17842192 | tf_op jit(solution)/shard_map/psum | solution.py:35
  1536.0 20.7 %fusion.5 = (f32[1408]{0:T(1024)}, f32[]{:T(128)}, f32[12,264,1408]{2,1,0:T(8,128)}, f32[12,264]{1,0:T(8,128)}) fusion(f32[]{:T(128)} %bitcast.11, bf16[12,257,1408]{2,1,0:T(8,128)(2,1)} %copy.97, f32[1408]{0:T(1024)S(1)} %copy-done.48, bf16[12,264,1408]{2,1,0:T(8,128)(2,1)} %get-tuple-element.74, f32[1408]{0:T(1024)S(1)} %copy-done.35, ...), kind=kLoop, calls=%fused_computation.31 | loop fusion | flops 57982496 | bytes 53332232 | tf_op jit(solution)/shard_map/reduce_sum | solution.py:73
  1569.6 47.1 %convolution_convert_fusion.1 = bf16[12,257,2560]{2,1,0:T(8,128)(2,1)} fusion(bf16[2112,2560]{1,0:T(8,128)(2,1)} %param.28, s32[]{:T(128)S(6)} %select_n.12, bf16[12,257,1408]{2,1,0:T(8,128)(2,1)S(1)} %fusion.42, bf16[12,257,7040]{2,1,0:T(8,128)(2,1)} %reshape.125), kind=kOutput, calls=%fused_computation.38 | convolution fusion | flops 33382598656 | bytes 78710784 | tf_op jit(solution)/shard_map/btc,cp->btp/dot_general | solution.py:22
  1624.1 56.7 %slice.43 = bf16[12,257,7040]{1,0,2:T(8,128)(2,1)} slice(bf16[12,257,8448]{1,0,2:T(8,128)(2,1)} %all-gather.2.cloned.1.call-done), slice={[0:12], [0:257], [1408:8448]} | slice | bytes 86845440 | tf_op jit(solution)/shard_map/slice | solution.py:70
  1680.9 57.0 %pad.9 = bf16[12,264,7040]{1,0,2:T(8,128)(2,1)} pad(bf16[12,257,7040]{1,0,2:T(8,128)(2,1)} %slice.43, bf16[]{:T(256)} %constant.99.clone.1), padding=0_0x0_7x0_0 | pad | bytes 88028160 | tf_op jit(solution)/shard_map/jit(_pad)/pad | solution.py:70
  1737.9 97.7 %copy.73 = bf16[12,264,5,1408]{3,1,2,0:T(8,128)(2,1)} copy(bf16[12,264,5,1408]{1,0,3,2:T(8,128)(2,1)} %bitcast.27) | data formatting | bytes 89210880
  1835.7 23.9 %convolution_bitcast_fusion.2 = f32[1408,1536]{1,0:T(8,128)} fusion(bf16[12,264,1536]{2,1,0:T(8,128)(2,1)} %get-tuple-element.91, bf16[12,264,1408]{2,1,0:T(8,128)(2,1)} %copy-done.3, f32[1408]{0:T(1024)S(1)} %copy-done.47, f32[1408]{0:T(1024)S(1)} %copy-done.38, f32[12,264]{1,0:T(8,128)S(1)} %copy-done.33, f32[12,264]{1,0:T(8,128)S(1)} %copy-done.25), kind=kOutput, calls=%fused_computation.116 | convolution fusion | flops 13729554432 | bytes 27340544 | tf_op jit(solution)/shard_map/btd,btf->df/dot_general | solution.py:22
  1859.6 23.3 %convolution_bitcast_fusion.1 = f32[1536,1408]{1,0:T(8,128)} fusion(bf16[12,264,1536]{2,1,0:T(8,128)(2,1)} %get-tuple-element.78, f32[]{:T(128)} %bitcast.11, bf16[12,257,1408]{2,1,0:T(8,128)(2,1)} %copy.97), kind=kOutput, calls=%fused_computation.115 | convolution fusion | flops 13716172800 | bytes 27067396 | tf_op jit(solution)/shard_map/btf,btd->fd/dot_general | solution.py:22
  1937.6 71.9 %convolution_bitcast_fusion = f32[2112,2560]{1,0:T(8,128)} fusion(bf16[12,257,2560]{2,1,0:T(8,128)(2,1)} %param.17, s32[]{:T(128)S(6)} %select_n.12, bf16[12,257,1408]{2,1,0:T(8,128)(2,1)} %copy-done.14, bf16[12,257,7040]{2,1,0:T(8,128)(2,1)} %reshape.125), kind=kOutput, calls=%fused_computation.73 | convolution fusion | flops 33374703616 | bytes 89524224 | tf_op jit(solution)/shard_map/btc,btp->cp/dot_general | solution.py:22
  (202 shorter events, 299.8 us)
Async XLA Ops:
  7.2 67.5 %copy-start = (bf16[4,88,1408]{2,1,0:T(8,128)(2,1)S(1)}, bf16[4,88,1408]{2,1,0:T(8,128)(2,1)}, u32[]{:S(2)}) copy-start(bf16[4,88,1408]{2,1,0:T(8,128)(2,1)} %param.21) | copy-start | bytes 2973700
  7.2 236.2 %all-reduce.8.cloned.1.call-start = ((), (), s32[]{:S(2)}) async-start(), calls=%async_computation.1 | async-start | bytes 17842176 | tf_op jit(solution)/shard_map/psum | solution.py:35
  7.3 37.0 %copy-start.50 = (pred[264]{0:T(512)(128)(4,1)}, pred[264]{0:T(512)(128)(4,1)S(1)}, u32[]{:S(2)}) copy-start(pred[264]{0:T(512)(128)(4,1)S(1)} %iota_compare_fusion) | copy-start | bytes 796
  82.3 763.9 %all-gather.2.cloned.1.call-start = ((), (), s32[]{:S(2)}) async-start(), calls=%async_computation.2 | async-start | bytes 129761280 | tf_op jit(solution)/shard_map/all_gather | solution.py:67
  159.2 931.5 %all-reduce.10.cloned.1.call-start = ((), (), s32[]{:S(2)}) async-start(), calls=%async_computation.3 | async-start | bytes 17842176 | tf_op jit(solution)/shard_map/psum | solution.py:35
  251.5 31.1 %copy-start.3 = (bf16[12,264,1408]{2,1,0:T(8,128)(2,1)}, bf16[12,264,1408]{2,1,0:T(8,128)(2,1)S(1)}, u32[]{:S(2)}) copy-start(bf16[12,264,1408]{2,1,0:T(8,128)(2,1)S(1)} %get-tuple-element.81) | copy-start | bytes 26763268
  251.6 861.7 %copy-start.24 = (f32[12,264]{1,0:T(8,128)}, f32[12,264]{1,0:T(8,128)S(1)}, u32[]{:S(2)}) copy-start(f32[12,264]{1,0:T(8,128)S(1)} %broadcast_multiply_fusion) | copy-start | bytes 38020
  254.1 28.5 %copy-start.30 = (f32[12,264]{1,0:T(8,128)}, f32[12,264]{1,0:T(8,128)S(1)}, u32[]{:S(2)}) copy-start(f32[12,264]{1,0:T(8,128)S(1)} %multiply_reduce_fusion) | copy-start | bytes 38020
  254.2 859.1 %copy-start.32 = (f32[12,264]{1,0:T(8,128)}, f32[12,264]{1,0:T(8,128)S(1)}, u32[]{:S(2)}) copy-start(f32[12,264]{1,0:T(8,128)S(1)} %fusion.118) | copy-start | bytes 38020
  932.4 603.6 %all-reduce.12.cloned.1.call-start = ((), (), s32[]{:S(2)}) async-start(), calls=%async_computation.5 | async-start | bytes 35684352 | tf_op jit(solution)/shard_map/psum | solution.py:35
  953.3 147.3 %copy-start.31 = (f32[12,264]{1,0:T(8,128)S(1)}, f32[12,264]{1,0:T(8,128)}, u32[]{:S(2)}) copy-start(f32[12,264]{1,0:T(8,128)} %copy-done.30) | copy-start | bytes 38020
  1234.1 775.4 %reduce-scatter.4.cloned.1.call-start = ((), (), s32[]{:S(2)}) async-start(), calls=%async_computation.4 | async-start | bytes 20275200
  1393.1 142.9 %copy-start.20 = (f32[12,264]{1,0:T(8,128)S(1)}, f32[12,264]{1,0:T(8,128)}, u32[]{:S(2)}) copy-start(f32[12,264]{1,0:T(8,128)} %copy-done.19) | copy-start | bytes 38020
  1393.1 142.9 %copy-start.35 = (f32[1408]{0:T(1024)S(1)}, f32[1408]{0:T(1024)}, u32[]{:S(2)}) copy-start(f32[1408]{0:T(1024)} %copy-done.34) | copy-start | bytes 16900
  1393.1 142.9 %copy-start.48 = (f32[1408]{0:T(1024)S(1)}, f32[1408]{0:T(1024)}, u32[]{:S(2)}) copy-start(f32[1408]{0:T(1024)} %param.27) | copy-start | bytes 16900
  1536.0 22.8 %copy-start.6 = (f32[12,264,1408]{2,1,0:T(8,128)S(1)}, f32[12,264,1408]{2,1,0:T(8,128)}, u32[]{:S(2)}) copy-start(f32[12,264,1408]{2,1,0:T(8,128)} %convert_element_type.156) | copy-start | bytes 53526532
  1737.9 97.7 %copy-start.25 = (f32[12,264]{1,0:T(8,128)S(1)}, f32[12,264]{1,0:T(8,128)}, u32[]{:S(2)}) copy-start(f32[12,264]{1,0:T(8,128)} %copy-done.24) | copy-start | bytes 38020
  1737.9 97.7 %copy-start.33 = (f32[12,264]{1,0:T(8,128)S(1)}, f32[12,264]{1,0:T(8,128)}, u32[]{:S(2)}) copy-start(f32[12,264]{1,0:T(8,128)} %copy-done.32) | copy-start | bytes 38020
  1737.9 97.7 %copy-start.38 = (f32[1408]{0:T(1024)S(1)}, f32[1408]{0:T(1024)}, u32[]{:S(2)}) copy-start(f32[1408]{0:T(1024)} %get-tuple-element.70) | copy-start | bytes 16900
  1737.9 97.7 %copy-start.47 = (f32[1408]{0:T(1024)S(1)}, f32[1408]{0:T(1024)}, u32[]{:S(2)}) copy-start(f32[1408]{0:T(1024)} %get-tuple-element.73) | copy-start | bytes 16900
  1859.6 23.3 %copy-start.41 = (f32[1408]{0:T(1024)S(1)}, f32[1408]{0:T(1024)}, u32[]{:S(2)}) copy-start(f32[1408]{0:T(1024)} %get-tuple-element.64) | copy-start | bytes 16900
  1859.6 23.9 %copy-start.40 = (f32[1408]{0:T(1024)S(1)}, f32[1408]{0:T(1024)}, u32[]{:S(2)}) copy-start(f32[1408]{0:T(1024)} %get-tuple-element.69) | copy-start | bytes 16900
  1937.6 71.9 %copy-start.45 = (f32[2560]{0:T(1024)S(1)}, f32[2560]{0:T(1024)}, u32[]{:S(2)}) copy-start(f32[2560]{0:T(1024)} %param.29) | copy-start | bytes 30724
  1937.6 76.7 %copy-start.1 = (bf16[4,88,1408]{2,1,0:T(8,128)(2,1)S(1)}, bf16[4,88,1408]{2,1,0:T(8,128)(2,1)}, u32[]{:S(2)}) copy-start(bf16[4,88,1408]{2,1,0:T(8,128)(2,1)} %param.21) | copy-start | bytes 2973700
  (49 other events, 462.9 us)
Sparse Core Ops, SparseCore 0:
  82.4 160.9 all-reduce.7
  245.5 600.5 all-gather.1
  932.5 158.1 all-reduce.9
  1234.2 301.7 all-reduce.11
  1616.8 118.0 reduce-scatter.3
where the time goes:
time: 2030 us; the launch traced here: 2020 us
  waiting for transfers between devices  868 us (43%)
  matrix products  465 us (23%)
  local copies, waits for them, and re-layouts  462 us (23%)
  other arithmetic  208 us (10%)
    all_gather x1, waiting for transfers between devices, local_step(): grad_feats = lax.all_gather(grad_feats_local, 'tp', axis=2, tiled=True)  518 us
    dot_general x26, matrix products, matmul(): jnp.einsum(eq_form, lhs_in, rhs_in, preferred_element_type=jnp.float32)  452 us
    psum x3, waiting for transfers between devices, group_sum(): return lax.psum(part_sum.astype(jnp.bfloat16), 'tp').astype(jnp.float32)  351 us
    unnamed x138, local copies, waits for them, and re-layouts  141 us
    reshape x1, local copies, waits for them, and re-layouts, local_step(): inter_feats[:, :real_rows].reshape(tile_count, real_rows, -1)  121 us
    pad x1, local copies, waits for them, and re-layouts, local_step(): jnp.pad(grad_feats[:, :, width:], pad_rows).reshape(inter_feats.shape)  57 us
    slice x1, local copies, waits for them, and re-layouts, local_step(): grad_feats[:, :, width:]  56.7 us
    convert_element_type x1, other arithmetic, gelu_bf16(): return jax.nn.gelu(pre_act, approximate=False).astype(jnp.bfloat16)  45.9 us
  transfers between devices with their start and end apart: 5, of which 4 were waited for; matrix products, arithmetic and copies ran while one was open for 37% of the time, Pallas kernels for 0%

commit v1 on v0

v1 whole, which is shorter than its diff:
```python
import jax
import jax.numpy as jnp
from jax import lax
from jax.sharding import PartitionSpec as P

LN_EPS = 1e-5
F32 = jnp.float32
BF16 = jnp.bfloat16
SIB = [(0, 1), (1, 0), (2, 3), (3, 2)]
ACROSS = [(0, 2), (2, 0), (1, 3), (3, 1)]


def layer_norm(values, ln_gain, ln_bias):
    row_mean = jnp.mean(values, axis=-1, keepdims=True)
    centred = values - row_mean
    row_var = jnp.mean(centred * centred, axis=-1, keepdims=True)
    return (centred * lax.rsqrt(row_var + LN_EPS) * ln_gain + ln_bias).astype(BF16)


def mm(eq_form, lhs_in, rhs_in):
    return jnp.einsum(eq_form, lhs_in, rhs_in, preferred_element_type=F32)


def attend(real_rows, q_act, k_act, v_act):
    tokens = q_act.shape[2]
    score_scale = q_act.shape[3] ** -0.5
    scores = mm('bhqe,bhke->bhqk', q_act, k_act) * score_scale
    key_ok = (jnp.arange(tokens) < real_rows)[None, None, None, :]
    attn_probs = jax.nn.softmax(jnp.where(key_ok, scores, -1e30), axis=-1).astype(BF16)
    return mm('bhqk,bhke->bhqe', attn_probs, v_act).astype(BF16)


def sib(value):
    return lax.ppermute(value, 'tp', SIB)


def across(value):
    return lax.ppermute(value, 'tp', ACROSS)


def partner_shard(shard):
    rows = shard.shape[0] // 4
    quarter = lax.dynamic_slice_in_dim(shard, lax.axis_index('dp') * rows, rows, axis=0)
    return lax.all_gather(across(quarter), 'dp', axis=0, tiled=True)


def reduce_own(near, far):
    n = near.shape[0] // 2
    from_sib_own = sib(near[n:])
    from_sib_far = sib(far[n:])
    chip_far = (far[:n].astype(F32) + from_sib_far.astype(F32)).astype(BF16)
    from_far = across(chip_far)
    return near[:n].astype(F32) + from_sib_own.astype(F32) + from_far.astype(F32)


def by_tp(tp, parts, builders):
    return lax.switch(tp, [lambda *p, b=b: b(*p) for b in builders], *parts)


def local_step(hidden, inter_feats, proj_grad, w_query, w_key, w_value, w_out, ln_params, gate_params, w_fc1, b_fc1, w_fc2, b_fc2, w_proj, b_proj):
    tiles, tokens, width = hidden.shape
    real_rows, proj_dim = proj_grad.shape[1:]
    ninter = inter_feats.shape[2]
    own_n = tiles // 4
    tp = lax.axis_index('tp')
    core = tp % 2
    first = tp * own_n
    inter_t = jnp.transpose(inter_feats, (0, 2, 1, 3))
    row_ok = (jnp.arange(tokens) < real_rows)[None, :, None]
    gate_attn = jnp.tanh(gate_params[0])
    gate_mlp = jnp.tanh(gate_params[1])

    def own(value):
        return lax.dynamic_slice_in_dim(value, first, own_n, axis=0)

    def group_of(value, other):
        return lax.dynamic_slice_in_dim(value, (tp ^ other) * own_n, own_n, axis=0)

    att_own = jnp.stack([jnp.transpose(w_query, (1, 2, 0)), jnp.transpose(w_key, (1, 2, 0)), jnp.transpose(w_value, (1, 2, 0)), w_out])
    heads, head_dim = att_own.shape[1:3]
    att_rows = att_own.reshape(4 * heads * head_dim, width)
    att_far = partner_shard(att_rows)
    att_sib = sib(att_rows)
    att_far_sib = sib(att_far)
    att_all = jnp.concatenate([v.reshape(4, heads, head_dim, width) for v in (att_rows, att_far, att_sib, att_far_sib)], axis=1)
    wq, wk, wv, wo = att_all[0], att_all[1], att_all[2], att_all[3]

    wp_far = partner_shard(w_proj)
    wp_sib = sib(w_proj)
    wp_far_sib = sib(wp_far)

    def order(a, b, c, d):
        return a[:width], jnp.concatenate([a[width:], b, c, d], axis=0)

    wp_first, wp_rest = by_tp(tp, (w_proj, wp_sib, wp_far, wp_far_sib), [
        lambda o, s, f, fs: order(o, s, f, fs),
        lambda o, s, f, fs: order(s, o, fs, f),
        lambda o, s, f, fs: order(f, fs, o, s),
        lambda o, s, f, fs: order(fs, f, s, o)])
    wp_rest = wp_rest.reshape(ninter, width, proj_dim)

    pg = jnp.pad(proj_grad, ((0, 0), (0, tokens - real_rows), (0, 0)))

    hid_own = own(hidden).astype(F32)
    normed, norm1_pull = jax.vjp(layer_norm, hid_own, ln_params[0], ln_params[1])
    q_act = mm('btd,hed->bhte', normed, wq).astype(BF16)
    k_act = mm('btd,hed->bhte', normed, wk).astype(BF16)
    v_act = mm('btd,hed->bhte', normed, wv).astype(BF16)
    context, attend_pull = jax.vjp(lambda q, k, v: attend(real_rows, q, k, v), q_act, k_act, v_act)
    attn_out = mm('bhte,hed->btd', context, wo)
    x_one = (hid_own + gate_attn * attn_out).astype(BF16)

    x_far = across(x_one)
    x_sib = sib(x_one)
    x_far_sib = sib(x_far)
    x_near2 = jnp.concatenate([x_one, x_sib], axis=0)
    x_far2 = jnp.concatenate([x_far, x_far_sib], axis=0)

    grad_x_two = mm('btp,cp->btc', pg, wp_first).astype(BF16)
    gx_own = own(grad_x_two)
    grad_mlp_low = (gate_mlp * grad_x_two.astype(F32)).astype(BF16)
    gm_near = jnp.concatenate([own(grad_mlp_low), group_of(grad_mlp_low, 1)], axis=0)
    gm_far = jnp.concatenate([group_of(grad_mlp_low, 2), group_of(grad_mlp_low, 3)], axis=0)

    def mlp_part(x_part, gm_part):
        grad_act = mm('btd,fd->btf', gm_part, w_fc2).astype(BF16)
        normed_two = layer_norm(x_part.astype(F32), ln_params[2], ln_params[3])
        pre_act = mm('btd,df->btf', normed_two, w_fc1) + b_fc1
        cdf = 0.5 * (1.0 + lax.erf(pre_act * (0.5 ** 0.5)))
        pdf = jnp.exp(-0.5 * pre_act * pre_act) * 0.3989422804014327
        mlp_act = (pre_act * cdf).astype(BF16)
        grad_pre = grad_act.astype(F32) * (cdf + pre_act * pdf)
        grad_b = jnp.sum(grad_pre, axis=(0, 1))
        grad_pre_low = grad_pre.astype(BF16)
        mlp_sum = mm('btf,fd->btd', mlp_act, w_fc2).astype(BF16)
        grad_n = mm('btf,df->btd', grad_pre_low, w_fc1).astype(BF16)
        return normed_two, mlp_act, grad_pre_low, grad_b, mlp_sum, grad_n

    n2_near, act_near, gp_near, gb_near, m_near, gn_near = mlp_part(x_near2, gm_near)
    n2_far, act_far, gp_far, gb_far, m_far, gn_far = mlp_part(x_far2, gm_far)
    grad_b_fc1 = gb_near + gb_far
    grad_normed_two = reduce_own(gn_near, gn_far).astype(BF16)
    mlp_out = reduce_own(m_near, m_far) + b_fc2
    grad_w_fc1 = mm('btd,btf->df', n2_near, gp_near) + mm('btd,btf->df', n2_far, gp_far)
    grad_w_fc2 = mm('btf,btd->fd', act_near, gm_near) + mm('btf,btd->fd', act_far, gm_far)

    x_one_wide = x_one.astype(F32)
    x_two = jnp.where(row_ok, (x_one_wide + gate_mlp * mlp_out).astype(BF16), 0)
    proj_own = mm('btc,cp->btp', x_two, wp_first) + mm('bntc,ncp->btp', own(inter_t), wp_rest)
    proj_out = (proj_own[:, :real_rows] + b_proj).astype(BF16)
    x_two_far = lax.ppermute(x_two, 'tp', [(2, 0), (3, 1)])
    x_two_sib = lax.ppermute(x_two, 'tp', [(1, 0)])
    x_two_far_sib = lax.ppermute(x_two_far, 'tp', [(1, 0)])
    half = w_proj.shape[0] - width
    feats = by_tp(tp, (inter_t, x_two, x_two_sib, x_two_far, x_two_far_sib), [
        lambda i, o, s, f, fs: jnp.concatenate([jnp.concatenate([o, s, f, fs], axis=0), i[:, 0, :, :half]], axis=2),
        lambda i, o, s, f, fs: jnp.concatenate([i[:, 0, :, half:], i[:, 1]], axis=2),
        lambda i, o, s, f, fs: jnp.concatenate([i[:, 2], i[:, 3, :, :half]], axis=2),
        lambda i, o, s, f, fs: jnp.concatenate([i[:, 3, :, half:], i[:, 4]], axis=2)])
    grad_w_proj = mm('btc,btp->cp', feats, pg)

    pg_half = lax.dynamic_slice_in_dim(pg, core * (tiles // 2), tiles // 2, axis=0)
    gi_half = mm('btp,ncp->bntc', pg_half, wp_rest).astype(BF16)
    gi_sib = sib(gi_half)
    grad_inter = lax.cond(core == 0, lambda a, b: jnp.concatenate([a, b], axis=0), lambda a, b: jnp.concatenate([b, a], axis=0), gi_half, gi_sib)
    grad_inter = jnp.transpose(grad_inter, (0, 2, 1, 3))

    _, norm2_pull = jax.vjp(layer_norm, x_one_wide, ln_params[2], ln_params[3])
    grad_x_ln_two, grad_gain_two, grad_bias_two = norm2_pull(grad_normed_two)
    gx_own_wide = gx_own.astype(F32)
    grad_x_one = (gx_own_wide + grad_x_ln_two).astype(BF16).astype(F32)
    grad_attn_low = (gate_attn * grad_x_one).astype(BF16)
    grad_context = mm('btd,hed->bhte', grad_attn_low, wo).astype(BF16)
    grad_q, grad_k, grad_v = attend_pull(grad_context)
    grad_normed = (mm('bhte,hed->btd', grad_q, wq) + mm('bhte,hed->btd', grad_k, wk) + mm('bhte,hed->btd', grad_v, wv)).astype(BF16)
    grad_x_ln, grad_gain, grad_bias = norm1_pull(grad_normed)
    gh_own = (grad_x_one + grad_x_ln).astype(BF16)
    gh_far = across(gh_own)
    gh_sib = sib(gh_own)
    gh_far_sib = sib(gh_far)
    grad_hidden = by_tp(tp, (gh_own, gh_sib, gh_far, gh_far_sib), [
        lambda o, s, f, fs: jnp.concatenate([o, s, f, fs], axis=0),
        lambda o, s, f, fs: jnp.concatenate([s, o, fs, f], axis=0),
        lambda o, s, f, fs: jnp.concatenate([f, fs, o, s], axis=0),
        lambda o, s, f, fs: jnp.concatenate([fs, f, s, o], axis=0)])

    dw = [mm('bhte,btd->hed', grad_q, normed), mm('bhte,btd->hed', grad_k, normed), mm('bhte,btd->hed', grad_v, normed), mm('bhte,btd->hed', context, grad_attn_low)]
    dw = jnp.stack([d.astype(BF16) for d in dw])
    dw_sib = sib(dw[:, 2 * heads:])
    dw_far = across((dw[:, heads:2 * heads].astype(F32) + dw_sib[:, heads:].astype(F32)).astype(BF16))
    dw_own = dw[:, :heads].astype(F32) + dw_sib[:, :heads].astype(F32) + dw_far.astype(F32)
    grad_w_query = jnp.transpose(dw_own[0], (2, 0, 1))
    grad_w_key = jnp.transpose(dw_own[1], (2, 0, 1))
    grad_w_value = jnp.transpose(dw_own[2], (2, 0, 1))
    grad_w_out = dw_own[3]

    grad_gate_mlp = jnp.sum(gx_own_wide * mlp_out) * (1.0 - gate_mlp * gate_mlp)
    grad_gate_attn = jnp.sum(grad_x_one * attn_out) * (1.0 - gate_attn * gate_attn)
    small = jnp.concatenate([
        grad_gain, grad_bias, grad_gain_two, grad_bias_two,
        jnp.sum(gate_mlp * gx_own_wide, axis=(0, 1)),
        jnp.sum(own(proj_grad), axis=(0, 1), dtype=F32),
        grad_gate_attn[None], grad_gate_mlp[None]])
    small = lax.psum(small, 'tp')
    grad_ln = small[:4 * width].reshape(4, width)
    grad_b_fc2 = small[4 * width:5 * width]
    grad_b_proj = small[5 * width:5 * width + proj_dim]
    grad_gates = small[5 * width + proj_dim:]
    return (proj_out, grad_hidden, grad_inter, grad_w_query, grad_w_key, grad_w_value, grad_w_out, grad_ln, grad_gates, grad_w_fc1, grad_b_fc1, grad_w_fc2, grad_b_fc2, grad_w_proj, grad_b_proj)


def solution(mesh):
    tiles_spec = P('dp', None, None)
    inter_spec = P('dp', None, None, None)
    head_cols = P(None, 'tp', None)
    in_specs = (tiles_spec, inter_spec, tiles_spec, head_cols, head_cols, head_cols, P('tp', None, None), P(None, None), P(None), P(None, 'tp'), P('tp'), P('tp', None), P(None), P('tp', None), P(None))
    grad_heads = P('dp', 'tp', None)
    out_specs = (P(('dp', 'tp'), None, None), tiles_spec, inter_spec, grad_heads, grad_heads, grad_heads, P(('dp', 'tp'), None, None), P('dp', None), P('dp'), P('dp', 'tp'), P(('dp', 'tp')), P(('dp', 'tp'), None), P('dp'), P(('dp', 'tp'), None), P('dp'))
    return jax.shard_map(local_step, mesh=mesh, in_specs=in_specs, out_specs=out_specs, check_vma=False)
```

time: 2030 us -> 1270 us (0.63)
  waiting for transfers between devices: 868 us -> 341 us
  local copies, waits for them, and re-layouts: 462 us -> 79.1 us
  blocking collectives: 0 us -> 72 us
  matrix products: 465 us -> 508 us
  starting transfers between devices: 0.21 us -> 35 us
    all_gather x1 -> x2, waiting for transfers between devices: 518 us -> 48 us  [partner_shard(): return lax.all_gather(across(quarter), 'dp', axis=0, tiled=True)]
    psum x3 -> x0, waiting for transfers between devices: 351 us -> none  [group_sum(): return lax.psum(part_sum.astype(jnp.bfloat16), 'tp').astype(jnp.float32)]
    ppermute x0 -> x24, waiting for transfers between devices: none -> 293 us  [the longest x7 243 us: across(): return lax.ppermute(value, 'tp', ACROSS)]
    unnamed x138 -> x210, local copies, waits for them, and re-layouts: 141 us -> 9.8 us
    reshape x1, local copies, waits for them, and re-layouts: 121 us -> 0.62 us  [local_step(): grad_ln = small[:4 * width].reshape(4, width)]
    slice x4 -> x11, local copies, waits for them, and re-layouts: 110 us -> 15.2 us  [the longest x1 7.24 us: local_step(): dw_sib = sib(dw[:, 2 * heads:])]
    concatenate x0 -> x5, other arithmetic: none -> 83.2 us  [the longest x1 30.6 us: local_step(): jnp.concatenate([a, b], axis=0)]
    psum x0 -> x1, blocking collectives: none -> 72 us  [local_step(): small = lax.psum(small, 'tp')]
  transfers between devices with their start and end apart: 5 -> 26, of which waited for: 4 -> 10; matrix products, arithmetic and copies ran while one was open for 37% -> 40% of each run, Pallas kernels for 0% -> 0%
where the time goes in v1:
time: 1270 us; the launch traced here: 1260 us
  matrix products  508 us (40%)
  waiting for transfers between devices  341 us (27%)
  other arithmetic  203 us (16%)
  local copies, waits for them, and re-layouts  79.1 us (6%)
  blocking collectives  72 us (6%)
  starting transfers between devices  35 us (3%)
  between operations  18.7 us (1%)
    dot_general x35, matrix products, mm(): return jnp.einsum(eq_form, lhs_in, rhs_in, preferred_element_type=F32)  508 us
    ppermute x7, waiting for transfers between devices, across(): return lax.ppermute(value, 'tp', ACROSS)  243 us
    psum x1, blocking collectives, local_step(): small = lax.psum(small, 'tp')  72 us
    ppermute x1, waiting for transfers between devices, local_step(): x_two_far = lax.ppermute(x_two, 'tp', [(2, 0), (3, 1)])  49.1 us
    all_gather x2, waiting for transfers between devices, partner_shard(): return lax.all_gather(across(quarter), 'dp', axis=0, tiled=True)  48 us
    concatenate x1, other arithmetic, local_step(): jnp.concatenate([a, b], axis=0)  30.6 us
    concatenate x1, local copies, waits for them, and re-layouts, local_step(): jnp.concatenate([a, b], axis=0)  30.3 us
    concatenate x1, other arithmetic, order(): return (a[:width], jnp.concatenate([a[width:], b, c, d], axis=0))  25.5 us
  transfers between devices with their start and end apart: 26, of which 10 were waited for; matrix products, arithmetic and copies ran while one was open for 40% of the time, Pallas kernels for 0%

profile of v1, /device:TPU:0, one launch (start us, length us, event | category | flops | bytes accessed | tf_op | source)
XLA Modules:
  0.0 1258.1 jit_solution(8524639955935006683)
XLA Ops:
  14.9 21.9 %collective-permute-done = bf16[352,1408]{1,0:T(8,128)(2,1)S(1)} collective-permute-done((bf16[352,1408]{1,0:T(8,128)(2,1)S(1)}, bf16[352,1408]{1,0:T(8,128)(2,1)S(1)}, u32[]{:S(2)}, u32[]{:S(2)}) %collective-permute-start) | collective-permute-done | bytes 991264 | tf_op jit(solution)/shard_map/ppermute | solution.py:38
  37.9 48.0 %all-gather.3.cloned.1.call-done = bf16[1408,1408]{1,0:T(8,128)(2,1)} async-done(((bf16[352,1408]{1,0:T(8,128)(2,1)}), bf16[1408,1408]{1,0:T(8,128)(2,1)}) %all-gather.3.cloned.1.call-update) | async-done | bytes 3964944 | tf_op jit(solution)/shard_map/all_gather | solution.py:44
  96.7 53.7 %collective-permute-done.10 = bf16[528,2560]{1,0:T(8,128)(2,1)} collective-permute-done((bf16[528,2560]{1,0:T(8,128)(2,1)}, bf16[528,2560]{1,0:T(8,128)(2,1)}, u32[]{:S(2)}, u32[]{:S(2)}) %collective-permute-start.10) | collective-permute-done | bytes 2703392 | tf_op jit(solution)/shard_map/ppermute | solution.py:38
  196.5 20.6 %fusion.207 = (f32[3,16,264]{2,1,0:T(8,128)S(1)}, f32[3,16,264,264]{2,3,1,0:T(8,128)}) fusion(f32[3,16,264,264]{2,3,1,0:T(8,128)} %fusion.140, pred[264]{0:T(512)(128)(4,1)S(1)} %iota_compare_fusion), kind=kOutput, calls=%fused_computation.287 | output fusion | flops 20072712 | bytes 26814216 | tf_op jit(solution)/shard_map/jvp()/sub | solution.py:29
  249.0 48.7 %collective-permute-done.5 = bf16[3,264,1408]{2,1,0:T(8,128)(2,1)S(1)} collective-permute-done((bf16[3,264,1408]{2,1,0:T(8,128)(2,1)S(1)}, bf16[3,264,1408]{2,1,0:T(8,128)(2,1)S(1)}, u32[]{:S(2)}, u32[]{:S(2)}) %collective-permute-start.5) | collective-permute-done | bytes 2230304 | tf_op jit(solution)/shard_map/ppermute | solution.py:38
  317.8 16.4 %multiply_convert_fusion.2 = (bf16[6,264,1536]{2,1,0:T(8,128)(2,1)S(1)}, bf16[6,264,1536]{2,1,0:T(8,128)(2,1)S(1)}, f32[6,264,1536]{2,1,0:T(8,128)}) fusion(f32[1536]{0:T(1024)S(1)} %copy-done.82, f32[6,264,1536]{2,1,0:T(8,128)} %fusion.95, bf16[1408,1536]{1,0:T(8,128)(2,1)S(1)} %bitcast.310, f32[1408]{0:T(1024)S(1)} %get-tuple-element.210, ...), kind=kOutput, calls=%fused_computation.72 | convolution fusion | flops 6896203776 | bytes 38012288 | tf_op jit(solution)/shard_map/btd,df->btf/dot_general | solution.py:21
  357.3 47.9 %collective-permute-done.8 = bf16[3,264,1408]{2,1,0:T(8,128)(2,1)} collective-permute-done((bf16[3,264,1408]{2,1,0:T(8,128)(2,1)}, bf16[3,264,1408]{2,1,0:T(8,128)(2,1)}, u32[]{:S(2)}, u32[]{:S(2)}) %collective-permute-start.8) | collective-permute-done | bytes 2230304 | tf_op jit(solution)/shard_map/ppermute | solution.py:38
  413.6 49.1 %collective-permute-done.22 = bf16[3,264,1408]{2,1,0:T(8,128)(2,1)S(1)} collective-permute-done((bf16[3,264,1408]{2,1,0:T(8,128)(2,1)}, bf16[3,264,1408]{2,1,0:T(8,128)(2,1)S(1)}, u32[]{:S(2)}, u32[]{:S(2)}) %collective-permute-start.22) | collective-permute-done | bytes 2230304 | tf_op jit(solution)/shard_map/ppermute | solution.py:151
  481.8 45.7 %convolution_bitcast_fusion = f32[2112,2560]{1,0:T(8,128)} fusion(bf16[12,264,2112]{2,1,0:T(8,128)(2,1)} %get-tuple-element.259, bf16[12,257,2560]{2,1,0:T(8,128)(2,1)} %param.31), kind=kOutput, calls=%fused_computation.38 | convolution fusion | flops 34256977920 | bytes 50798592 | tf_op jit(solution)/shard_map/btc,btp->cp/dot_general | solution.py:21
  527.5 39.7 %conditional.4 = (bf16[2112,2560]{1,0:T(8,128)(2,1)}, bf16[5,1408,2560]{2,1,0:T(8,128)(2,1)}) conditional(s32[]{:T(128)} %clamp.2, (bf16[2112,2560]{1,0:T(8,128)(2,1)}, bf16[2112,2560]{1,0:T(8,128)(2,1)}, bf16[2112,2560]{1,0:T(8,128)(2,1)}, bf16[2112,2560]{1,0:T(8,128)(2,1)}) %tuple.77, ...), branch_computations={%region_8.9_spmd, %region_9.10_spmd, %region_10.11_spmd, %region_1... | conditional | flops 144179200 | bytes 100925456 | solution.py:57
  531.6 25.5 %pad_maximum_fusion = bf16[7040,2560]{1,0:T(8,128)(2,1)} fusion(bf16[2112,2560]{1,0:T(8,128)(2,1)} %get-tuple-element.130, bf16[2112,2560]{1,0:T(8,128)(2,1)} %get-tuple-element.129, bf16[2112,2560]{1,0:T(8,128)(2,1)} %get-tuple-element.128, bf16[704,2560]{1,0:T(8,128)(2,1)} %slice.54), kind=kLoop, calls=%fused_computation | loop fusion | flops 144179200 | bytes 72089600 | tf_op jit(solution)/shard_map/cond/branch_0_fun/concatenate | solution.py:93
  567.2 37.6 %fusion.64 = f32[3,264,2560]{2,1,0:T(8,128)} fusion(bf16[5,1408,2560]{2,1,0:T(8,128)(2,1)} %get-tuple-element.186, bf16[12,264,5,1408]{3,1,2,0:T(8,128)(2,1)} %param.30, s32[]{:T(128)S(6)} %select_n.44), kind=kOutput, calls=%fused_computation.132 | convolution fusion | flops 28547481600 | bytes 55306244 | tf_op jit(solution)/shard_map/bntc,ncp->btp/dot_general | solution.py:21
  604.8 72.4 %fusion.14 = bf16[6,5,264,1408]{3,2,0,1:T(8,128)(2,1)} fusion(bf16[5,1408,2560]{2,1,0:T(8,128)(2,1)} %get-tuple-element.186, s32[]{:T(128)S(6)} %select_n.54, bf16[12,257,2560]{2,1,0:T(8,128)(2,1)} %param.31), kind=kOutput, calls=%fused_computation.39 | convolution fusion | flops 57106112512 | bytes 74137600 | tf_op jit(solution)/shard_map/btp,ncp->bntc/dot_general | solution.py:21
  677.2 31.8 %multiply_convert_fusion = (bf16[12,264,1408]{2,1,0:T(8,128)(2,1)S(1)}, bf16[12,264,1408]{2,1,0:T(8,128)(2,1)}) fusion(f32[]{:T(128)} %bitcast.40, bf16[2112,2560]{1,0:T(8,128)(2,1)} %get-tuple-element.185, bf16[12,257,2560]{2,1,0:T(8,128)(2,1)} %param.31), kind=kOutput, calls=%fused_computation.40 | convolution fusion | flops 22855827456 | bytes 41271808 | tf_op jit(solution)/shard_map/btp,cp->btc/dot_general | solution.py:21
  711.8 16.1 %fusion.209 = (f32[1536]{0:T(1024)}, bf16[6,264,1536]{2,1,0:T(8,128)(2,1)S(1)}) fusion(f32[6,264,1536]{2,1,0:T(8,128)} %fusion.95, f32[1536]{0:T(1024)S(1)} %copy-done.83, bf16[1536,1408]{1,0:T(8,128)(2,1)} %param.40, bf16[3,264,1408]{2,1,0:T(8,128)(2,1)S(1)} %get-tuple-element.219, bf16[3,264,1408]{2,1,0:T(8,128)(2,1)S(1)} %get-tuple-element.220), kind=kOutput, calls=%fused_computation.289 | convolution fusion | flops 6887686656 | bytes 23396352 | tf_op jit(solution)/shard_map/btd,fd->btf/dot_general | solution.py:21
  740.4 18.6 %collective-permute-start.13 = (bf16[3,264,1408]{2,1,0:T(8,128)(2,1)S(1)}, bf16[3,264,1408]{2,1,0:T(8,128)(2,1)}, u32[]{:S(2)}, u32[]{:S(2)}) collective-permute-start(bf16[3,264,1408]{2,1,0:T(8,128)(2,1)S(1)} %slice.190), channel_id=1, source_target_pairs={{0,1},{1,0},{2,3},{3,2},{4,5},{5,4},{6,7},{7,6},{8,9},{9,8},{10,11... | collective-permute-start | bytes 6690824 | tf_op jit(solution)/shard_map/ppermute | solution.py:34
  804.4 36.9 %collective-permute-done.14 = bf16[3,264,1408]{2,1,0:T(8,128)(2,1)S(1)} collective-permute-done((bf16[3,264,1408]{2,1,0:T(8,128)(2,1)}, bf16[3,264,1408]{2,1,0:T(8,128)(2,1)S(1)}, u32[]{:S(2)}, u32[]{:S(2)}) %collective-permute-start.14) | collective-permute-done | bytes 2230304 | tf_op jit(solution)/shard_map/ppermute | solution.py:38
  886.8 15.0 %fusion.11 = bf16[3,16,264,264]{2,3,1,0:T(8,128)(2,1)} fusion(f32[3,16,264,264]{2,3,1,0:T(8,128)} %get-tuple-element.233, bf16[3,16,264,264]{2,3,1,0:T(8,128)(2,1)} %get-tuple-element.239, f32[3,16,264]{2,1,0:T(8,128)S(1)} %neg.13, f32[3,16,264]{2,1,0:T(8,128)S(1)} %copy-done.44, pred[264]{0:T(512)(128)(4,1)S(1)} %copy-done.80), kind=kLoop, calls=%fused_computation.32 | loop fusion | flops 23417856 | bytes 26864904 | tf_op jit(solution)/shard_map/transpose(jvp())/mul | solution.py:27
  969.4 15.8 %bitcast_add_fusion.1 = f32[1408,1536]{1,0:T(8,128)} fusion(f32[1408,1536,1]{1,0,2:T(8,128)} %fusion.147, bf16[6,264,1536]{2,1,0:T(8,128)(2,1)} %copy-done.85, f32[6,264]{1,0:T(8,128)S(1)} %copy-done.70, f32[6,264]{1,0:T(8,128)S(1)} %copy-done.59, f32[1408]{0:T(1024)S(1)} %copy-done.74, f32[1408]{0:T(1024)S(1)} %copy-done.47, ...), kind=kOutput, calls=%fused_computation.86 | convolution fusion | flops 6869170176 | bytes 26652032 | tf_op jit(solution)/shard_map/btd,btf->df/dot_general | solution.py:21
  1045.4 34.4 %collective-permute-done.16 = bf16[3,264,1408]{2,1,0:T(8,128)(2,1)} collective-permute-done((bf16[3,264,1408]{2,1,0:T(8,128)(2,1)S(1)}, bf16[3,264,1408]{2,1,0:T(8,128)(2,1)}, u32[]{:S(2)}, u32[]{:S(2)}) %collective-permute-start.16) | collective-permute-done | bytes 2230304 | tf_op jit(solution)/shard_map/ppermute | solution.py:38
  1098.6 72.0 %psum.7 = f32[9602]{0:T(1024)S(1)} all-reduce(f32[9602]{0:T(1024)S(1)} %concatenate.72), channel_id=1, replica_groups=mesh['dp'=4,'tp'=4] {'tp'}, use_global_device_ids=true, to_apply=%region_33.34 | all-reduce | flops 9602 | bytes 76816 | tf_op jit(solution)/shard_map/psum | solution.py:204
  1190.0 60.9 %conditional.6 = (bf16[12,5,264,1408]{3,2,1,0:T(8,128)(2,1)}) conditional(s32[]{:T(128)} %convert_element_type.291, (bf16[6,5,264,1408]{3,2,0,1:T(8,128)(2,1)}, bf16[6,5,264,1408]{3,2,0,1:T(8,128)(2,1)}) %tuple.85, (bf16[6,5,264,1408]{3,2,0,1:T(8,128)(2,1)}, bf16[6,5,264,1408]{3,2,0,1:T(8,128)(2,1)}) %tuple.86), branch_computations={%region_23.24_spmd, %region_24.25_spmd} | conditional | flops 22302720 | bytes 178421760 | solution.py:165
  1190.0 30.6 %pad_maximum_fusion.9 = bf16[12,5,264,1408]{3,2,0,1:T(8,128)(2,1)} fusion(bf16[6,5,264,1408]{3,2,0,1:T(8,128)(2,1)} %get-tuple-element.190, bf16[6,5,264,1408]{3,2,0,1:T(8,128)(2,1)} %get-tuple-element.189), kind=kLoop, calls=%fused_computation.9 | loop fusion | flops 22302720 | bytes 89210880 | tf_op jit(solution)/shard_map/cond/branch_1_fun/concatenate | solution.py:165
  1220.6 30.3 %copy.82 = bf16[12,5,264,1408]{3,2,1,0:T(8,128)(2,1)} copy(bf16[12,5,264,1408]{3,2,0,1:T(8,128)(2,1)} %pad_maximum_fusion.9) | data formatting | bytes 89210880 | tf_op jit(solution)/shard_map/cond/branch_1_fun/concatenate | solution.py:165
  (352 shorter events, 471.3 us)
Async XLA Ops:
  7.2 78.7 %all-gather.3.cloned.1.call-start = ((), (), s32[]{:S(2)}) async-start(), calls=%async_computation | async-start | bytes 4956160 | tf_op jit(solution)/shard_map/all_gather | solution.py:44
  11.7 25.2 %collective-permute-start = (bf16[352,1408]{1,0:T(8,128)(2,1)S(1)}, bf16[352,1408]{1,0:T(8,128)(2,1)S(1)}, u32[]{:S(2)}, u32[]{:S(2)}) collective-permute-start(bf16[352,1408]{1,0:T(8,128)(2,1)S(1)} %constant_dynamic-slice_fusion.5), channel_id=1, source_target_pairs={{0,2},{2,0},{1,3},{3,1},{4,6},{6,4},{5,7},{7,5},{8,10},{10,8},{9,1... | collective-permute-start | bytes 2973704 | tf_op jit(solution)/shard_map/ppermute | solution.py:38
  37.8 318.2 %all-gather.5.cloned.1.call-start = ((), (), s32[]{:S(2)}) async-start(), calls=%async_computation.1 | async-start | bytes 13516800 | tf_op jit(solution)/shard_map/all_gather | solution.py:44
  37.9 112.5 %collective-permute-start.1 = (bf16[1408,1408]{1,0:T(8,128)(2,1)}, bf16[1408,1408]{1,0:T(8,128)(2,1)}, u32[]{:S(2)}, u32[]{:S(2)}) collective-permute-start(bf16[1408,1408]{1,0:T(8,128)(2,1)} %bitcast.293), channel_id=1, source_target_pairs={{0,1},{1,0},{2,3},{3,2},{4,5},{5,4},{6,7},{7,6},{8,9},{9,8},{10,11... | collective-permute-start | bytes 11894792 | tf_op jit(solution)/shard_map/ppermute | solution.py:34
  85.9 64.5 %collective-permute-start.2 = (bf16[1408,1408]{1,0:T(8,128)(2,1)}, bf16[1408,1408]{1,0:T(8,128)(2,1)}, u32[]{:S(2)}, u32[]{:S(2)}) collective-permute-start(bf16[1408,1408]{1,0:T(8,128)(2,1)} %all-gather.3.cloned.1.call-done), channel_id=1, source_target_pairs={{0,1},{1,0},{2,3},{3,2},{4,5},{5,4},{6,7},{7,6},{8,9},{9,8},{10,11... | collective-permute-start | bytes 11894792 | tf_op jit(solution)/shard_map/ppermute | solution.py:34
  89.4 61.0 %collective-permute-start.10 = (bf16[528,2560]{1,0:T(8,128)(2,1)}, bf16[528,2560]{1,0:T(8,128)(2,1)}, u32[]{:S(2)}, u32[]{:S(2)}) collective-permute-start(bf16[528,2560]{1,0:T(8,128)(2,1)} %constant_dynamic-slice_fusion.4), channel_id=1, source_target_pairs={{0,2},{2,0},{1,3},{3,1},{4,6},{6,4},{5,7},{7,5},{8,10},{10,8},{9,1... | collective-permute-start | bytes 8110088 | tf_op jit(solution)/shard_map/ppermute | solution.py:38
  247.5 50.1 %collective-permute-start.5 = (bf16[3,264,1408]{2,1,0:T(8,128)(2,1)S(1)}, bf16[3,264,1408]{2,1,0:T(8,128)(2,1)S(1)}, u32[]{:S(2)}, u32[]{:S(2)}) collective-permute-start(bf16[3,264,1408]{2,1,0:T(8,128)(2,1)S(1)} %get-tuple-element.215), channel_id=1, source_target_pairs={{0,2},{2,0},{1,3},{3,1},{4,6},{6,4},{5,7},{7,5},{8,10},{10,8},{9,1... | collective-permute-start | bytes 6690824 | tf_op jit(solution)/shard_map/ppermute | solution.py:38
  249.0 48.7 %collective-permute-start.3 = (bf16[3,264,1408]{2,1,0:T(8,128)(2,1)S(1)}, bf16[3,264,1408]{2,1,0:T(8,128)(2,1)S(1)}, u32[]{:S(2)}, u32[]{:S(2)}) collective-permute-start(bf16[3,264,1408]{2,1,0:T(8,128)(2,1)S(1)} %get-tuple-element.215), channel_id=1, source_target_pairs={{0,1},{1,0},{2,3},{3,2},{4,5},{5,4},{6,7},{7,6},{8,9},{9,8},{10,11... | collective-permute-start | bytes 6690824 | tf_op jit(solution)/shard_map/ppermute | solution.py:34
  342.4 10.3 collective-permute-start.7
  354.6 50.5 %collective-permute-start.8 = (bf16[3,264,1408]{2,1,0:T(8,128)(2,1)}, bf16[3,264,1408]{2,1,0:T(8,128)(2,1)}, u32[]{:S(2)}, u32[]{:S(2)}) collective-permute-start(bf16[3,264,1408]{2,1,0:T(8,128)(2,1)} %add_convert_fusion.3), channel_id=1, source_target_pairs={{0,2},{2,0},{1,3},{3,1},{4,6},{6,4},{5,7},{7,5},{8,10},{10,8},{9,1... | collective-permute-start | bytes 6690824 | tf_op jit(solution)/shard_map/ppermute | solution.py:38
  356.0 171.4 %collective-permute-start.9 = (bf16[2112,2560]{1,0:T(8,128)(2,1)}, bf16[2112,2560]{1,0:T(8,128)(2,1)}, u32[]{:S(2)}, u32[]{:S(2)}) collective-permute-start(bf16[2112,2560]{1,0:T(8,128)(2,1)} %param.42), channel_id=1, source_target_pairs={{0,1},{1,0},{2,3},{3,2},{4,5},{5,4},{6,7},{7,6},{8,9},{9,8},{10,11... | collective-permute-start | bytes 32440328 | tf_op jit(solution)/shard_map/ppermute | solution.py:34
  356.1 171.4 %collective-permute-start.11 = (bf16[2112,2560]{1,0:T(8,128)(2,1)}, bf16[2112,2560]{1,0:T(8,128)(2,1)}, u32[]{:S(2)}, u32[]{:S(2)}) collective-permute-start(bf16[2112,2560]{1,0:T(8,128)(2,1)} %all-gather.5.cloned.1.call-done), channel_id=1, source_target_pairs={{0,1},{1,0},{2,3},{3,2},{4,5},{5,4},{6,7},{7,6},{8,9},{9,8},{10,11... | collective-permute-start | bytes 32440328 | tf_op jit(solution)/shard_map/ppermute | solution.py:34
  411.0 51.7 %collective-permute-start.22 = (bf16[3,264,1408]{2,1,0:T(8,128)(2,1)}, bf16[3,264,1408]{2,1,0:T(8,128)(2,1)S(1)}, u32[]{:S(2)}, u32[]{:S(2)}) collective-permute-start(bf16[3,264,1408]{2,1,0:T(8,128)(2,1)} %fusion.174), channel_id=1, source_target_pairs={{2,0},{3,1},{6,4},{7,5},{10,8},{11,9},{14,12},{15,13}} | collective-permute-start | bytes 6690824 | tf_op jit(solution)/shard_map/ppermute | solution.py:151
  412.3 56.3 %collective-permute-start.21 = (bf16[3,264,1408]{2,1,0:T(8,128)(2,1)}, bf16[3,264,1408]{2,1,0:T(8,128)(2,1)}, u32[]{:S(2)}, u32[]{:S(2)}) collective-permute-start(bf16[3,264,1408]{2,1,0:T(8,128)(2,1)} %fusion.174), channel_id=1, source_target_pairs={{1,0},{5,4},{9,8},{13,12}} | collective-permute-start | bytes 6690824 | tf_op jit(solution)/shard_map/ppermute | solution.py:152
  462.6 6.2 collective-permute-start.23
  740.4 46.1 %collective-permute-start.13 = (bf16[3,264,1408]{2,1,0:T(8,128)(2,1)S(1)}, bf16[3,264,1408]{2,1,0:T(8,128)(2,1)}, u32[]{:S(2)}, u32[]{:S(2)}) collective-permute-start(bf16[3,264,1408]{2,1,0:T(8,128)(2,1)S(1)} %slice.190), channel_id=1, source_target_pairs={{0,1},{1,0},{2,3},{3,2},{4,5},{5,4},{6,7},{7,6},{8,9},{9,8},{10,11... | collective-permute-start | bytes 6690824 | tf_op jit(solution)/shard_map/ppermute | solution.py:34
  784.4 20.0 %collective-permute-start.12 = (bf16[3,264,1408]{2,1,0:T(8,128)(2,1)S(1)}, bf16[3,264,1408]{2,1,0:T(8,128)(2,1)S(1)}, u32[]{:S(2)}, u32[]{:S(2)}) collective-permute-start(bf16[3,264,1408]{2,1,0:T(8,128)(2,1)S(1)} %slice.188), channel_id=1, source_target_pairs={{0,1},{1,0},{2,3},{3,2},{4,5},{5,4},{6,7},{7,6},{8,9},{9,8},{10,11... | collective-permute-start | bytes 6690824 | tf_op jit(solution)/shard_map/ppermute | solution.py:34
  786.5 403.5 %collective-permute-start.18 = (bf16[6,5,264,1408]{3,2,0,1:T(8,128)(2,1)}, bf16[6,5,264,1408]{3,2,0,1:T(8,128)(2,1)}, u32[]{:S(2)}, u32[]{:S(2)}) collective-permute-start(bf16[6,5,264,1408]{3,2,0,1:T(8,128)(2,1)} %fusion.14), channel_id=1, source_target_pairs={{0,1},{1,0},{2,3},{3,2},{4,5},{5,4},{6,7},{7,6},{8,9},{9,8},{10,11... | collective-permute-start | bytes 66908168 | tf_op jit(solution)/shard_map/ppermute | solution.py:34
  790.2 51.0 %collective-permute-start.14 = (bf16[3,264,1408]{2,1,0:T(8,128)(2,1)}, bf16[3,264,1408]{2,1,0:T(8,128)(2,1)S(1)}, u32[]{:S(2)}, u32[]{:S(2)}) collective-permute-start(bf16[3,264,1408]{2,1,0:T(8,128)(2,1)} %add_convert_fusion.2), channel_id=1, source_target_pairs={{0,2},{2,0},{1,3},{3,1},{4,6},{6,4},{5,7},{7,5},{8,10},{10,8},{9,1... | collective-permute-start | bytes 6690824 | tf_op jit(solution)/shard_map/ppermute | solution.py:38
  969.4 59.4 %collective-permute-start.19 = (bf16[4,8,88,1408]{3,2,1,0:T(8,128)(2,1)}, bf16[4,8,88,1408]{3,2,1,0:T(8,128)(2,1)}, u32[]{:S(2)}, u32[]{:S(2)}) collective-permute-start(bf16[4,8,88,1408]{3,2,1,0:T(8,128)(2,1)} %slice.191), channel_id=1, source_target_pairs={{0,1},{1,0},{2,3},{3,2},{4,5},{5,4},{6,7},{7,6},{8,9},{9,8},{10,11... | collective-permute-start | bytes 23789576 | tf_op jit(solution)/shard_map/ppermute | solution.py:34
  1028.4 51.4 %collective-permute-start.16 = (bf16[3,264,1408]{2,1,0:T(8,128)(2,1)S(1)}, bf16[3,264,1408]{2,1,0:T(8,128)(2,1)}, u32[]{:S(2)}, u32[]{:S(2)}) collective-permute-start(bf16[3,264,1408]{2,1,0:T(8,128)(2,1)S(1)} %fusion.85), channel_id=1, source_target_pairs={{0,2},{2,0},{1,3},{3,1},{4,6},{6,4},{5,7},{7,5},{8,10},{10,8},{9,1... | collective-permute-start | bytes 6690824 | tf_op jit(solution)/shard_map/ppermute | solution.py:38
  1034.1 147.1 %collective-permute-start.20 = (bf16[4,4,88,1408]{3,2,1,0:T(8,128)(2,1)}, bf16[4,4,88,1408]{3,2,1,0:T(8,128)(2,1)}, u32[]{:S(2)}, u32[]{:S(2)}) collective-permute-start(bf16[4,4,88,1408]{3,2,1,0:T(8,128)(2,1)} %add_convert_fusion), channel_id=1, source_target_pairs={{0,2},{2,0},{1,3},{3,1},{4,6},{6,4},{5,7},{7,5},{8,10},{10,8},{9,1... | collective-permute-start | bytes 11894792 | tf_op jit(solution)/shard_map/ppermute | solution.py:38
  1045.4 127.6 %collective-permute-start.15 = (bf16[3,264,1408]{2,1,0:T(8,128)(2,1)S(1)}, bf16[3,264,1408]{2,1,0:T(8,128)(2,1)}, u32[]{:S(2)}, u32[]{:S(2)}) collective-permute-start(bf16[3,264,1408]{2,1,0:T(8,128)(2,1)S(1)} %fusion.85), channel_id=1, source_target_pairs={{0,1},{1,0},{2,3},{3,2},{4,5},{5,4},{6,7},{7,6},{8,9},{9,8},{10,11... | collective-permute-start | bytes 6690824 | tf_op jit(solution)/shard_map/ppermute | solution.py:34
  1079.8 93.2 %collective-permute-start.17 = (bf16[3,264,1408]{2,1,0:T(8,128)(2,1)}, bf16[3,264,1408]{2,1,0:T(8,128)(2,1)}, u32[]{:S(2)}, u32[]{:S(2)}) collective-permute-start(bf16[3,264,1408]{2,1,0:T(8,128)(2,1)} %collective-permute-done.16), channel_id=1, source_target_pairs={{0,1},{1,0},{2,3},{3,2},{4,5},{5,4},{6,7},{7,6},{8,9},{9,8},{10,11... | collective-permute-start | bytes 6690824 | tf_op jit(solution)/shard_map/ppermute | solution.py:34
  (107 other events, 3622.3 us)
Sparse Core Ops, SparseCore 0:
  38.0 47.8 all-gather.2
  150.5 103.8 all-gather.4

commit v2 on v1

v2 whole, which is shorter than its diff:
```python
import jax
import jax.numpy as jnp
from jax import lax
from jax.experimental import pallas as pl
from jax.sharding import PartitionSpec as P


LN_EPS = 1e-5
F32 = jnp.float32
BF16 = jnp.bfloat16
SIB = [(0, 1), (1, 0), (2, 3), (3, 2)]
ACROSS = [(0, 2), (2, 0), (1, 3), (3, 1)]


def layer_norm(values, ln_gain, ln_bias):
    row_mean = jnp.mean(values, axis=-1, keepdims=True)
    centred = values - row_mean
    row_var = jnp.mean(centred * centred, axis=-1, keepdims=True)
    return (centred * lax.rsqrt(row_var + LN_EPS) * ln_gain + ln_bias).astype(BF16)


def mm(eq_form, lhs_in, rhs_in):
    return jnp.einsum(eq_form, lhs_in, rhs_in, preferred_element_type=F32)


def attend(real_rows, q_act, k_act, v_act):
    tokens = q_act.shape[2]
    score_scale = q_act.shape[3] ** -0.5
    scores = mm('bhqe,bhke->bhqk', q_act, k_act) * score_scale
    key_ok = (jnp.arange(tokens) < real_rows)[None, None, None, :]
    attn_probs = jax.nn.softmax(jnp.where(key_ok, scores, -1e30), axis=-1).astype(BF16)
    return mm('bhqk,bhke->bhqe', attn_probs, v_act).astype(BF16)


def sib(value):
    return lax.ppermute(value, 'tp', SIB)


def across(value):
    return lax.ppermute(value, 'tp', ACROSS)


def partner_shard(shard, start, count):
    rows = count // 4
    quarter = lax.dynamic_slice_in_dim(shard, start + lax.axis_index('dp') * rows, rows, axis=0)
    quarter = across(quarter)
    return lax.all_gather(quarter, 'dp', axis=0, tiled=True)


def reduce_own(near, far):
    n = near.shape[0] // 2
    from_sib_far = sib(far[n:])
    from_sib_own = sib(near[n:])
    chip_far = (far[:n].astype(F32) + from_sib_far.astype(F32)).astype(BF16)
    from_far = across(chip_far)
    return near[:n].astype(F32) + from_sib_own.astype(F32) + from_far.astype(F32)


def by_tp(tp, parts, builders):
    return lax.switch(tp, [lambda *p, b=b: b(*p) for b in builders], *parts)


def unfilled(shape, dtype):
    return pl.pallas_call(
        lambda out_ref: None,
        out_shape=jax.ShapeDtypeStruct(shape, dtype),
        out_specs=pl.BlockSpec(memory_space=pl.ANY),
        name='unfilled')()


def put_rows(buffer, piece, start):
    return lax.dynamic_update_slice_in_dim(buffer, piece, start, axis=0)


def whole_step(hidden, inter_feats, proj_grad, w_query, w_key, w_value, w_out, ln_params, gate_params, w_fc1, b_fc1, w_fc2, b_fc2, w_proj, b_proj):
    tiles, tokens, width = hidden.shape
    real_rows, proj_dim = proj_grad.shape[1:]
    ninter = inter_feats.shape[2]
    own_n = tiles // 4
    tp = lax.axis_index('tp')
    core = tp & 1
    first = tp * own_n
    inter_t = jnp.transpose(inter_feats, (0, 2, 1, 3))
    row_ok = (jnp.arange(tokens) < real_rows)[None, :, None]
    gate_attn = jnp.tanh(gate_params[0])
    gate_mlp = jnp.tanh(gate_params[1])

    def own(value):
        return lax.dynamic_slice_in_dim(value, first, own_n, axis=0)

    def group_of(value, other):
        return lax.dynamic_slice_in_dim(value, (tp ^ other) * own_n, own_n, axis=0)

    att_own = jnp.stack([jnp.transpose(w_query, (1, 2, 0)), jnp.transpose(w_key, (1, 2, 0)), jnp.transpose(w_value, (1, 2, 0)), w_out])
    heads, head_dim = att_own.shape[1:3]
    att_rows = att_own.reshape(4 * heads * head_dim, width)
    att_sib = sib(att_rows)
    att_far = partner_shard(att_rows, 0, att_rows.shape[0])
    att_far_sib = sib(att_far)

    def head_group(*shards):
        return jnp.concatenate([v.reshape(4, heads, head_dim, width) for v in shards], axis=1)

    shard_rows = w_proj.shape[0]
    wp_sib = sib(w_proj)
    wp_far_head = partner_shard(w_proj, 0, width)
    wp_far_tail = partner_shard(w_proj, width, shard_rows - width)
    wp_far_sib_head = sib(wp_far_head)
    wp_far_sib_tail = sib(wp_far_tail)
    wp_all = unfilled((4 * shard_rows, proj_dim), BF16)
    wp_all = put_rows(wp_all, w_proj, tp * shard_rows)
    wp_all = put_rows(wp_all, wp_sib, (tp ^ 1) * shard_rows)
    wp_all = put_rows(wp_all, wp_far_head, (tp ^ 2) * shard_rows)
    wp_all = put_rows(wp_all, wp_far_sib_head, (tp ^ 3) * shard_rows)
    wp_all = put_rows(wp_all, wp_far_tail, (tp ^ 2) * shard_rows + width)
    wp_all = put_rows(wp_all, wp_far_sib_tail, (tp ^ 3) * shard_rows + width)
    wp_planes = wp_all.reshape(ninter + 1, width, proj_dim)
    wp_first = by_tp(tp, (w_proj, wp_sib, wp_far_head, wp_far_sib_head), [
        lambda o, s, f, fs: o[:width],
        lambda o, s, f, fs: s[:width],
        lambda o, s, f, fs: f,
        lambda o, s, f, fs: fs])

    pg = jnp.pad(proj_grad, ((0, 0), (0, tokens - real_rows), (0, 0)))

    hid_own = own(hidden).astype(F32)
    normed, norm1_pull = jax.vjp(layer_norm, hid_own, ln_params[0], ln_params[1])

    def attention(weights):
        wq, wk, wv, wo = weights[0], weights[1], weights[2], weights[3]
        q_act = mm('btd,hed->bhte', normed, wq).astype(BF16)
        k_act = mm('btd,hed->bhte', normed, wk).astype(BF16)
        v_act = mm('btd,hed->bhte', normed, wv).astype(BF16)
        context, pull = jax.vjp(lambda q, k, v: attend(real_rows, q, k, v), q_act, k_act, v_act)
        return mm('bhte,hed->btd', context, wo), context, pull

    w_near = head_group(att_rows, att_sib)
    attn_near, context_near, pull_near = attention(w_near)
    w_far = head_group(att_far, att_far_sib)
    attn_far, context_far, pull_far = attention(w_far)
    attn_out = attn_near + attn_far
    x_one = (hid_own + gate_attn * attn_out).astype(BF16)

    x_far = across(x_one)
    x_sib = sib(x_one)
    x_far_sib = sib(x_far)
    x_near2 = jnp.concatenate([x_one, x_sib], axis=0)
    x_far2 = jnp.concatenate([x_far, x_far_sib], axis=0)

    grad_x_two = mm('btp,cp->btc', pg, wp_first).astype(BF16)
    grad_mlp_low = (gate_mlp * grad_x_two.astype(F32)).astype(BF16)
    gx_own = own(grad_x_two)
    gm_near = jnp.concatenate([own(grad_mlp_low), group_of(grad_mlp_low, 1)], axis=0)
    gm_far = jnp.concatenate([group_of(grad_mlp_low, 2), group_of(grad_mlp_low, 3)], axis=0)

    def mlp_part(x_part, gm_part):
        grad_act = mm('btd,fd->btf', gm_part, w_fc2).astype(BF16)
        normed_two = layer_norm(x_part.astype(F32), ln_params[2], ln_params[3])
        pre_act = mm('btd,df->btf', normed_two, w_fc1) + b_fc1
        cdf = 0.5 * (1.0 + lax.erf(pre_act * (0.5 ** 0.5)))
        pdf = jnp.exp(-0.5 * pre_act * pre_act) * 0.3989422804014327
        mlp_act = (pre_act * cdf).astype(BF16)
        grad_pre = grad_act.astype(F32) * (cdf + pre_act * pdf)
        grad_b = jnp.sum(grad_pre, axis=(0, 1))
        grad_pre_low = grad_pre.astype(BF16)
        grad_n = mm('btf,df->btd', grad_pre_low, w_fc1).astype(BF16)
        mlp_sum = mm('btf,fd->btd', mlp_act, w_fc2).astype(BF16)
        return normed_two, mlp_act, grad_pre_low, grad_b, mlp_sum, grad_n

    n2_near, act_near, gp_near, gb_near, m_near, gn_near = mlp_part(x_near2, gm_near)
    n2_far, act_far, gp_far, gb_far, m_far, gn_far = mlp_part(x_far2, gm_far)
    grad_b_fc1 = gb_near + gb_far
    grad_normed_two = reduce_own(gn_near, gn_far).astype(BF16)
    mlp_out = reduce_own(m_near, m_far) + b_fc2
    grad_w_fc1 = mm('btd,btf->df', n2_near, gp_near) + mm('btd,btf->df', n2_far, gp_far)
    grad_w_fc2 = mm('btf,btd->fd', act_near, gm_near) + mm('btf,btd->fd', act_far, gm_far)

    x_one_wide = x_one.astype(F32)
    x_two = jnp.where(row_ok, (x_one_wide + gate_mlp * mlp_out).astype(BF16), 0)
    feats_own = jnp.concatenate([x_two[:, None], own(inter_t)], axis=1)
    proj_own = mm('bntc,ncp->btp', feats_own, wp_planes)
    proj_out = (proj_own[:, :real_rows] + b_proj).astype(BF16)
    x_two_far = lax.ppermute(x_two, 'tp', [(2, 0), (3, 1)])
    x_two_sib = lax.ppermute(x_two, 'tp', [(1, 0)])
    x_two_far_sib = lax.ppermute(x_two_far, 'tp', [(1, 0)])
    half = shard_rows - width
    feats = by_tp(tp, (inter_t, x_two, x_two_sib, x_two_far, x_two_far_sib), [
        lambda i, o, s, f, fs: jnp.concatenate([jnp.concatenate([o, s, f, fs], axis=0), i[:, 0, :, :half]], axis=2),
        lambda i, o, s, f, fs: jnp.concatenate([i[:, 0, :, half:], i[:, 1]], axis=2),
        lambda i, o, s, f, fs: jnp.concatenate([i[:, 2], i[:, 3, :, :half]], axis=2),
        lambda i, o, s, f, fs: jnp.concatenate([i[:, 3, :, half:], i[:, 4]], axis=2)])
    grad_w_proj = mm('btc,btp->cp', feats, pg)

    half_tiles = tiles // 2
    grad_inter = unfilled((tiles, ninter, tokens, width), BF16)
    gi_sib = []
    for n in range(ninter):
        pg_half = lax.dynamic_slice_in_dim(pg, core * half_tiles, half_tiles, axis=0)
        gi_half = mm('btp,cp->btc', pg_half, wp_planes[n + 1]).astype(BF16)
        grad_inter = lax.dynamic_update_slice(grad_inter, gi_half[:, None], (core * half_tiles, n, 0, 0))
        gi_sib.append(sib(gi_half))
    for n in range(ninter):
        grad_inter = lax.dynamic_update_slice(grad_inter, gi_sib[n][:, None], ((1 - core) * half_tiles, n, 0, 0))
    grad_inter = jnp.transpose(grad_inter, (0, 2, 1, 3))

    _, norm2_pull = jax.vjp(layer_norm, x_one_wide, ln_params[2], ln_params[3])
    grad_x_ln_two, grad_gain_two, grad_bias_two = norm2_pull(grad_normed_two)
    gx_own_wide = gx_own.astype(F32)
    grad_x_one = (gx_own_wide + grad_x_ln_two).astype(BF16).astype(F32)
    grad_attn_low = (gate_attn * grad_x_one).astype(BF16)

    def attention_back(weights, pull):
        grad_context = mm('btd,hed->bhte', grad_attn_low, weights[3]).astype(BF16)
        grad_q, grad_k, grad_v = pull(grad_context)
        partial = mm('bhte,hed->btd', grad_q, weights[0]) + mm('bhte,hed->btd', grad_k, weights[1]) + mm('bhte,hed->btd', grad_v, weights[2])
        return grad_q, grad_k, grad_v, partial

    def attention_dw(grad_q, grad_k, grad_v, context):
        parts = [mm('bhte,btd->hed', grad_q, normed), mm('bhte,btd->hed', grad_k, normed), mm('bhte,btd->hed', grad_v, normed), mm('bhte,btd->hed', context, grad_attn_low)]
        return jnp.stack([d.astype(BF16) for d in parts])

    gq_far, gk_far, gv_far, gnorm_far = attention_back(w_far, pull_far)
    dw_far2 = attention_dw(gq_far, gk_far, gv_far, context_far)
    dw_far_from_sib = sib(dw_far2[:, heads:])
    dw_from_far = across((dw_far2[:, :heads].astype(F32) + dw_far_from_sib.astype(F32)).astype(BF16))
    gq_near, gk_near, gv_near, gnorm_near = attention_back(w_near, pull_near)
    grad_normed = (gnorm_near + gnorm_far).astype(BF16)
    grad_x_ln, grad_gain, grad_bias = norm1_pull(grad_normed)
    gh_own = (grad_x_one + grad_x_ln).astype(BF16)
    gh_far = across(gh_own)
    gh_sib = sib(gh_own)
    gh_far_sib = sib(gh_far)
    dw_near2 = attention_dw(gq_near, gk_near, gv_near, context_near)
    dw_near_from_sib = sib(dw_near2[:, heads:])
    grad_hidden = by_tp(tp, (gh_own, gh_sib, gh_far, gh_far_sib), [
        lambda o, s, f, fs: jnp.concatenate([o, s, f, fs], axis=0),
        lambda o, s, f, fs: jnp.concatenate([s, o, fs, f], axis=0),
        lambda o, s, f, fs: jnp.concatenate([f, fs, o, s], axis=0),
        lambda o, s, f, fs: jnp.concatenate([fs, f, s, o], axis=0)])
    dw_own = dw_near2[:, :heads].astype(F32) + dw_near_from_sib.astype(F32) + dw_from_far.astype(F32)
    grad_w_query = jnp.transpose(dw_own[0], (2, 0, 1))
    grad_w_key = jnp.transpose(dw_own[1], (2, 0, 1))
    grad_w_value = jnp.transpose(dw_own[2], (2, 0, 1))
    grad_w_out = dw_own[3]

    mlp_out_late, _ = lax.optimization_barrier((mlp_out, grad_normed))
    grad_gate_mlp = jnp.sum(gx_own_wide * mlp_out_late) * (1.0 - gate_mlp * gate_mlp)
    grad_gate_attn = jnp.sum(grad_x_one * attn_out) * (1.0 - gate_attn * gate_attn)
    small = jnp.concatenate([
        grad_gain, grad_bias, grad_gain_two, grad_bias_two,
        jnp.sum(gate_mlp * gx_own_wide, axis=(0, 1)),
        jnp.sum(own(proj_grad), axis=(0, 1), dtype=F32),
        grad_gate_attn[None], grad_gate_mlp[None]])
    small = small + sib(small)
    small = small + across(small)
    grad_ln = small[:4 * width].reshape(4, width)
    grad_b_fc2 = small[4 * width:5 * width]
    grad_b_proj = small[5 * width:5 * width + proj_dim]
    grad_gates = small[5 * width + proj_dim:]
    return (proj_out, grad_hidden, grad_inter, grad_w_query, grad_w_key, grad_w_value, grad_w_out, grad_ln, grad_gates, grad_w_fc1, grad_b_fc1, grad_w_fc2, grad_b_fc2, grad_w_proj, grad_b_proj)


def solution(mesh):
    tiles_spec = P('dp', None, None)
    inter_spec = P('dp', None, None, None)
    head_cols = P(None, 'tp', None)
    in_specs = (tiles_spec, inter_spec, tiles_spec, head_cols, head_cols, head_cols, P('tp', None, None), P(None, None), P(None), P(None, 'tp'), P('tp'), P('tp', None), P(None), P('tp', None), P(None))
    grad_heads = P('dp', 'tp', None)
    out_specs = (P(('dp', 'tp'), None, None), tiles_spec, inter_spec, grad_heads, grad_heads, grad_heads, P(('dp', 'tp'), None, None), P('dp', None), P('dp'), P('dp', 'tp'), P(('dp', 'tp')), P(('dp', 'tp'), None), P('dp'), P(('dp', 'tp'), None), P('dp'))
    return jax.shard_map(whole_step, mesh=mesh, in_specs=in_specs, out_specs=out_specs, check_vma=False)
```

time: 1270 us -> 1100 us (0.87)
  waiting for transfers between devices: 341 us -> 243 us
  blocking collectives: 72 us -> 0 us
  other arithmetic: 203 us -> 145 us
  local copies, waits for them, and re-layouts: 79.1 us -> 127 us
  matrix products: 508 us -> 522 us
    psum x1 -> x0, blocking collectives: 72 us -> none  [local_step(): small = lax.psum(small, 'tp')]
    dynamic_update_slice x0 -> x11, local copies, waits for them, and re-layouts: none -> 59.8 us  [the longest x6 36.3 us: put_rows(): return lax.dynamic_update_slice_in_dim(buffer, piece, start, axis=0)]
    concatenate x5 -> x4, other arithmetic: 83.2 us -> 28.4 us  [the longest x1 10.3 us: whole_step(): jnp.concatenate([jnp.concatenate([o, s, f, fs], axis=0), i[:, 0, :, :half...]
    ppermute x3, waiting for transfers between devices: 49.3 us -> 0.01 us  [the longest x1 0.01 us: whole_step(): x_two_sib = lax.ppermute(x_two, 'tp', [(1, 0)])]
    all_gather x2 -> x3, waiting for transfers between devices: 48 us -> 0.04 us  [partner_shard(): return lax.all_gather(quarter, 'dp', axis=0, tiled=True)]
    concatenate x2 -> x1, local copies, waits for them, and re-layouts: 30.3 us -> 0.08 us  [whole_step(): jnp.concatenate([grad_gain, grad_bias, grad_gain_two, grad_bias_two, jnp....]
    dot_general x35 -> x56, matrix products: 508 us -> 522 us  [mm(): return jnp.einsum(eq_form, lhs_in, rhs_in, preferred_element_type=F32)]
    unnamed x210 -> x322, local copies, waits for them, and re-layouts: 9.8 us -> 23.6 us
  transfers between devices with their start and end apart: 26 -> 36, of which waited for: 10 -> 7; matrix products, arithmetic and copies ran while one was open for 40% -> 70% of each run, Pallas kernels for 0% -> 0%
where the time goes in v2:
time: 1100 us; the launch traced here: 1090 us
  matrix products  522 us (47%)
  waiting for transfers between devices  243 us (22%)
  other arithmetic  145 us (13%)
  local copies, waits for them, and re-layouts  127 us (12%)
  starting transfers between devices  33.1 us (3%)
  between operations  19 us (2%)
    dot_general x56, matrix products, mm(): return jnp.einsum(eq_form, lhs_in, rhs_in, preferred_element_type=F32)  522 us
    ppermute x9, waiting for transfers between devices, across(): return lax.ppermute(value, 'tp', ACROSS)  243 us
    dynamic_update_slice x6, local copies, waits for them, and re-layouts, put_rows(): return lax.dynamic_update_slice_in_dim(buffer, piece, start, axis=0)  36.3 us
    unnamed x322, local copies, waits for them, and re-layouts  23.6 us
    dynamic_update_slice x5, local copies, waits for them, and re-layouts, whole_step(): lax.dynamic_update_slice(grad_inter, gi_sib[n][:, None], ((1 - core) * ha...  23.5 us
  transfers between devices with their start and end apart: 36, of which 7 were waited for; matrix products, arithmetic and copies ran while one was open for 70% of the time, Pallas kernels for 0%

profile of v2, /device:TPU:0, one launch (start us, length us, event | category | flops | bytes accessed | tf_op | source)
XLA Modules:
  0.0 1090.3 jit_solution(17037854695621186871)
XLA Ops:
  14.9 21.9 %collective-permute-done.1 = bf16[352,1408]{1,0:T(8,128)(2,1)S(1)} collective-permute-done((bf16[352,1408]{1,0:T(8,128)(2,1)S(1)}, bf16[352,1408]{1,0:T(8,128)(2,1)S(1)}, u32[]{:S(2)}, u32[]{:S(2)}) %collective-permute-start.1) | collective-permute-done | bytes 991264 | tf_op jit(solution)/shard_map/ppermute | solution.py:40
  50.5 32.4 %collective-permute-done.10 = bf16[352,2560]{1,0:T(8,128)(2,1)} collective-permute-done((bf16[352,2560]{1,0:T(8,128)(2,1)}, bf16[352,2560]{1,0:T(8,128)(2,1)}, u32[]{:S(2)}, u32[]{:S(2)}) %collective-permute-start.10) | collective-permute-done | bytes 1802272 | tf_op jit(solution)/shard_map/ppermute | solution.py:40
  188.7 46.8 %collective-permute-done.5 = bf16[3,264,1408]{2,1,0:T(8,128)(2,1)} collective-permute-done((bf16[3,264,1408]{2,1,0:T(8,128)(2,1)S(1)}, bf16[3,264,1408]{2,1,0:T(8,128)(2,1)}, u32[]{:S(2)}, u32[]{:S(2)}) %collective-permute-start.5) | collective-permute-done | bytes 2230304 | tf_op jit(solution)/shard_map/ppermute | solution.py:40
  279.0 14.8 %multiply_convert_fusion.2 = (bf16[6,264,1536]{2,1,0:T(8,128)(2,1)}, bf16[6,264,1536]{2,1,0:T(8,128)(2,1)S(1)}, f32[6,264,1536]{2,1,0:T(8,128)}) fusion(f32[1536]{0:T(1024)S(1)} %copy-done.102, f32[6,264,1536]{2,1,0:T(8,128)S(1)} %fusion.100, bf16[1408,1536]{1,0:T(8,128)(2,1)S(1)} %bitcast.541, f32[1408]{0:T(1024)S(1)} %copy-done.93, ...), kind=kOutput, calls=%fused_computation.72 | convolution fusion | flops 6896203776 | bytes 38012288 | tf_op jit(solution)/shard_map/btd,df->btf/dot_general | solution.py:23
  354.2 34.8 %collective-permute-done.8 = bf16[3,264,1408]{2,1,0:T(8,128)(2,1)} collective-permute-done((bf16[3,264,1408]{2,1,0:T(8,128)(2,1)}, bf16[3,264,1408]{2,1,0:T(8,128)(2,1)}, u32[]{:S(2)}, u32[]{:S(2)}) %collective-permute-start.8) | collective-permute-done | bytes 2230304 | tf_op jit(solution)/shard_map/ppermute | solution.py:40
  405.5 31.8 %multiply_convert_fusion = (bf16[12,264,1408]{2,1,0:T(8,128)(2,1)S(1)}, bf16[12,264,1408]{2,1,0:T(8,128)(2,1)}) fusion(f32[]{:T(128)} %bitcast.52, bf16[1408,2560]{1,0:T(8,128)(2,1)} %get-tuple-element.176, bf16[12,257,2560]{2,1,0:T(8,128)(2,1)} %param.29), kind=kOutput, calls=%fused_computation.18 | convolution fusion | flops 22855827456 | bytes 40841220 | tf_op jit(solution)/shard_map/btp,cp->btc/dot_general | solution.py:23
  440.1 16.5 %fusion.320 = (f32[1536]{0:T(1024)}, bf16[6,264,1536]{2,1,0:T(8,128)(2,1)S(1)}) fusion(f32[6,264,1536]{2,1,0:T(8,128)} %get-tuple-element.150, f32[1536]{0:T(1024)S(1)} %copy-done.103, bf16[1536,1408]{1,0:T(8,128)(2,1)} %param.38, bf16[3,264,1408]{2,1,0:T(8,128)(2,1)} %get-tuple-element.132, bf16[3,264,1408]{2,1,0:T(8,128)(2,1)} %get-tuple-element.129), kind=kOutput, calls=%fused_computation.389 | convolution fusion | flops 6887686656 | bytes 23396352 | tf_op jit(solution)/shard_map/btd,fd->btf/dot_general | solution.py:23
  456.6 11.8 %convolution_convert_fusion.2 = bf16[6,264,1408]{2,1,0:T(8,128)(2,1)S(1)} fusion(bf16[1408,1536]{1,0:T(8,128)(2,1)} %param.36, bf16[6,264,1536]{2,1,0:T(8,128)(2,1)S(1)} %get-tuple-element.169), kind=kOutput, calls=%fused_computation.150 | convolution fusion | flops 6853625856 | bytes 13651968 | tf_op jit(solution)/shard_map/btf,df->btd/dot_general | solution.py:23
  474.5 13.4 %fusion.321 = (f32[1536]{0:T(1024)}, bf16[6,264,1536]{2,1,0:T(8,128)(2,1)S(1)}) fusion(f32[6,264,1536]{2,1,0:T(8,128)} %copy-done.104, f32[1536]{0:T(1024)S(1)} %copy-done.103, bf16[1536,1408]{1,0:T(8,128)(2,1)S(1)} %bitcast.539, bf16[3,264,1408]{2,1,0:T(8,128)(2,1)S(1)} %get-tuple-element.130, bf16[3,264,1408]{2,1,0:T(8,128)(2,1)S(1)} %get-tuple-element.131), kind=kOutput, calls=%fused_computation.390 | convolution fusion | flops 6887686656 | bytes 23396352 | tf_op jit(solution)/shard_map/btd,fd->btf/dot_general | solution.py:23
  512.4 18.8 %bitcast_dynamic-update-slice_fusion.4 = (bf16[12,5,264,1408]{3,2,1,0:T(8,128)(2,1)}, bf16[6,264,1408]{2,1,0:T(8,128)(2,1)}) fusion(bf16[12,5,264,1408]{3,2,1,0:T(8,128)(2,1)} %unfilled.3, s32[]{:T(128)S(6)} %select_n.98, bf16[8448,2560]{1,0:T(8,128)(2,1)} %constant_dynamic-update-slice_fusion, bf16[12,257,2560]{2,1,0:T(8,128)(2,1)} %param.29), kind=kOutput, calls=%fused_computation.182 | convolution fusion | flops 11421222912 | bytes 32351232 | tf_op jit(solution)/shard_map/btp,cp->btc/dot_general | solution.py:23
  531.2 17.1 %bitcast_dynamic-update-slice_fusion.3 = (bf16[12,5,264,1408]{3,2,1,0:T(8,128)(2,1)}, bf16[6,264,1408]{2,1,0:T(8,128)(2,1)}) fusion(bf16[12,5,264,1408]{3,2,1,0:T(8,128)(2,1)} %get-tuple-element.158, s32[]{:T(128)S(6)} %select_n.98, bf16[8448,2560]{1,0:T(8,128)(2,1)} %constant_dynamic-update-slice_fusion, bf16[12,257,2560]{2,1,0:T(8,128)(2,1)S(1)} %bitcast.535), kind=kOutput, calls=%fused_computation.181 | convolution fusion | flops 11421222912 | bytes 31921152 | tf_op jit(solution)/shard_map/btp,cp->btc/dot_general | solution.py:23
  548.4 17.3 %bitcast_dynamic-update-slice_fusion.2 = (bf16[12,5,264,1408]{3,2,1,0:T(8,128)(2,1)}, bf16[6,264,1408]{2,1,0:T(8,128)(2,1)}) fusion(bf16[12,5,264,1408]{3,2,1,0:T(8,128)(2,1)} %get-tuple-element.160, s32[]{:T(128)S(6)} %select_n.98, bf16[8448,2560]{1,0:T(8,128)(2,1)} %constant_dynamic-update-slice_fusion, bf16[12,257,2560]{2,1,0:T(8,128)(2,1)S(1)} %bitcast.535), kind=kOutput, calls=%fused_computation.180 | convolution fusion | flops 11421222912 | bytes 31921152 | tf_op jit(solution)/shard_map/btp,cp->btc/dot_general | solution.py:23
  565.7 18.8 %bitcast_dynamic-update-slice_fusion.1 = (bf16[12,5,264,1408]{3,2,1,0:T(8,128)(2,1)}, bf16[6,264,1408]{2,1,0:T(8,128)(2,1)}) fusion(bf16[12,5,264,1408]{3,2,1,0:T(8,128)(2,1)} %get-tuple-element.162, s32[]{:T(128)S(6)} %select_n.98, bf16[8448,2560]{1,0:T(8,128)(2,1)} %constant_dynamic-update-slice_fusion, bf16[12,257,2560]{2,1,0:T(8,128)(2,1)} %param.29), kind=kOutput, calls=%fused_computation.179 | convolution fusion | flops 11421222912 | bytes 32351232 | tf_op jit(solution)/shard_map/btp,cp->btc/dot_general | solution.py:23
  584.5 18.8 %bitcast_dynamic-update-slice_fusion = (bf16[12,5,264,1408]{3,2,1,0:T(8,128)(2,1)}, bf16[6,264,1408]{2,1,0:T(8,128)(2,1)}) fusion(bf16[12,5,264,1408]{3,2,1,0:T(8,128)(2,1)} %get-tuple-element.164, s32[]{:T(128)S(6)} %select_n.98, bf16[8448,2560]{1,0:T(8,128)(2,1)} %constant_dynamic-update-slice_fusion, bf16[12,257,2560]{2,1,0:T(8,128)(2,1)} %param.29), kind=kOutput, calls=%fused_computation.178 | convolution fusion | flops 11421222912 | bytes 32351232 | tf_op jit(solution)/shard_map/btp,cp->btc/dot_general | solution.py:23
  604.0 41.3 %fusion.59 = f32[3,264,2560]{2,1,0:T(8,128)} fusion(bf16[6,1408,2560,1]{2,1,0,3:T(8,128)(2,1)} %bitcast.492, bf16[3,5,264,1408]{3,2,1,0:T(8,128)(2,1)S(1)} %bitcast.515, bf16[3,1,264,1408]{3,2,1,0:T(8,128)(2,1)} %bitcast.56), kind=kOutput, calls=%fused_computation.139 | convolution fusion | flops 34263668736 | bytes 64745472 | tf_op jit(solution)/shard_map/bntc,ncp->btp/dot_general | solution.py:23
  645.4 13.1 %fusion.117 = f32[1408,1536,1]{1,0,2:T(8,128)} fusion(bf16[6,264,1536]{2,1,0:T(8,128)(2,1)S(1)} %bitcast.545, f32[1408]{0:T(1024)S(1)} %copy-done.94, f32[1408]{0:T(1024)S(1)} %copy-done.73, f32[6,264]{1,0:T(8,128)S(1)} %copy-done.87, f32[6,264]{1,0:T(8,128)S(1)} %copy-done.81, bf16[3,264,1408]{2,1,0:T(8,128)(2,1)} %collective-permute-done.3, ...), kind=kOutput, calls=%fused_computation.233 | convolution fusion | flops 6867007488 | bytes 18001280 | tf_op jit(solution)/shard_map/btd,btf->df/dot_general | solution.py:23
  658.5 15.3 %bitcast_add_fusion.1 = f32[1408,1536]{1,0:T(8,128)} fusion(f32[1408,1536,1]{1,0,2:T(8,128)} %fusion.117, bf16[6,264,1536]{2,1,0:T(8,128)(2,1)S(1)} %copy-done.107, f32[6,264]{1,0:T(8,128)S(1)} %copy-done.89, f32[6,264]{1,0:T(8,128)S(1)} %copy-done.83, f32[1408]{0:T(1024)S(1)} %copy-done.94, f32[1408]{0:T(1024)S(1)} %copy-done.73, ...), kind=kOutput, calls=%fused_computation.89 | convolution fusion | flops 6869170176 | bytes 26652032 | tf_op jit(solution)/shard_map/btd,btf->df/dot_general | solution.py:23
  673.8 12.9 %fusion.112 = f32[1536,1408,1]{1,0,2:T(8,128)} fusion(bf16[6,264,1536]{2,1,0:T(8,128)(2,1)} %get-tuple-element.137, bf16[3,264,1408]{2,1,0:T(8,128)(2,1)S(1)} %copy-done.47, bf16[3,264,1408]{2,1,0:T(8,128)(2,1)S(1)} %copy-done.46), kind=kOutput, calls=%fused_computation.228 | convolution fusion | flops 6853625856 | bytes 17977344 | tf_op jit(solution)/shard_map/btf,btd->fd/dot_general | solution.py:23
  688.4 14.3 %bitcast_add_fusion = f32[1536,1408]{1,0:T(8,128)} fusion(f32[1536,1408,1]{1,0,2:T(8,128)} %fusion.112, bf16[6,264,1536]{2,1,0:T(8,128)(2,1)} %copy-done.108, bf16[3,264,1408]{2,1,0:T(8,128)(2,1)S(1)} %copy-done.43, bf16[3,264,1408]{2,1,0:T(8,128)(2,1)S(1)} %copy-done.45), kind=kOutput, calls=%fused_computation.88 | convolution fusion | flops 6855788544 | bytes 26628096 | tf_op jit(solution)/shard_map/btf,btd->fd/dot_general | solution.py:23
  711.6 13.4 %conditional.5 = (bf16[12,264,2112]{2,1,0:T(8,128)(2,1)}) conditional(s32[]{:T(128)} %clamp.2, (bf16[3,264,1408]{2,1,0:T(8,128)(2,1)}, bf16[3,264,1408]{2,1,0:T(8,128)(2,1)}, bf16[3,264,1408]{2,1,0:T(8,128)(2,1)}, bf16[3,264,1408]{2,1,0:T(8,128)(2,1)S(1)}, bf16[12,5,264,1408]{3,2,1,0:T(8,128)(2,1)}) %tuple.114, ...), branch_computations={%region_36.37_spmd, %region_37.38_spmd, %region_38.39_spmd, %regio... | conditional | flops 66908160 | bytes 89210920 | solution.py:60
  725.1 45.7 %convolution_bitcast_fusion = f32[2112,2560]{1,0:T(8,128)} fusion(bf16[12,264,2112]{2,1,0:T(8,128)(2,1)} %get-tuple-element.178, bf16[12,257,2560]{2,1,0:T(8,128)(2,1)} %param.29), kind=kOutput, calls=%fused_computation.17 | convolution fusion | flops 34256977920 | bytes 50798592 | tf_op jit(solution)/shard_map/btc,btp->cp/dot_general | solution.py:23
  814.9 11.3 %fusion.15 = (bf16[3,8,264,264]{2,3,1,0:T(8,128)(2,1)}, bf16[3,8,264,264]{2,3,1,0:T(8,128)(2,1)}) fusion(f32[3,8,264,264]{2,3,1,0:T(8,128)S(1)} %bitcast.478, bf16[3,8,264,264]{2,3,1,0:T(8,128)(2,1)} %get-tuple-element.154, f32[3,8,264]{2,1,0:T(8,128)S(1)} %neg.19, f32[3,8,264]{2,1,0:T(8,128)S(1)} %copy-done.62, pred[264]{0:T(512)(128)(4,1)S(1)} %copy-done.100, ...), kind=kLoop, calls=%fused_computation.51 | loop fusion | flops 23417856 | bytes 26864904 | tf_op jit(solution)/shard_map/transpose(jvp())/mul | solution.py:29
  949.3 29.3 %collective-permute-done.18 = bf16[3,264,1408]{2,1,0:T(8,128)(2,1)} collective-permute-done((bf16[3,264,1408]{2,1,0:T(8,128)(2,1)S(1)}, bf16[3,264,1408]{2,1,0:T(8,128)(2,1)}, u32[]{:S(2)}, u32[]{:S(2)}) %collective-permute-start.18) | collective-permute-done | bytes 2230304 | tf_op jit(solution)/shard_map/ppermute | solution.py:40
  994.5 69.2 %collective-permute-done.29 = f32[9602]{0:T(1024)S(1)} collective-permute-done((f32[9602]{0:T(1024)S(1)}, f32[9602]{0:T(1024)S(1)}, u32[]{:S(2)}, u32[]{:S(2)}) %collective-permute-start.29) | collective-permute-done | bytes 38440 | tf_op jit(solution)/shard_map/ppermute | solution.py:40
  (540 shorter events, 518.2 us)
Async XLA Ops:
  7.2 91.1 %all-gather.4.cloned.1.call-start = ((), (), s32[]{:S(2)}) async-start(), calls=%async_computation | async-start | bytes 4956160 | tf_op jit(solution)/shard_map/all_gather | solution.py:47
  37.8 217.0 %all-gather.6.cloned.1.call-start = ((), (), s32[]{:S(2)}) async-start(), calls=%async_computation.1 | async-start | bytes 9011200 | tf_op jit(solution)/shard_map/all_gather | solution.py:47
  82.9 237.9 %all-gather.8.cloned.1.call-start = ((), (), s32[]{:S(2)}) async-start(), calls=%async_computation.2 | async-start | bytes 4505600 | tf_op jit(solution)/shard_map/all_gather | solution.py:47
  185.8 69.0 %collective-permute-start.3 = (bf16[3,264,1408]{2,1,0:T(8,128)(2,1)S(1)}, bf16[3,264,1408]{2,1,0:T(8,128)(2,1)}, u32[]{:S(2)}, u32[]{:S(2)}) collective-permute-start(bf16[3,264,1408]{2,1,0:T(8,128)(2,1)S(1)} %get-tuple-element.126), channel_id=1, source_target_pairs={{0,1},{1,0},{2,3},{3,2},{4,5},{5,4},{6,7},{7,6},{8,9},{9,8},{10,11... | collective-permute-start | bytes 6690824 | tf_op jit(solution)/shard_map/ppermute | solution.py:36
  185.8 153.7 %collective-permute-start.9 = (bf16[2112,2560]{1,0:T(8,128)(2,1)}, bf16[2112,2560]{1,0:T(8,128)(2,1)}, u32[]{:S(2)}, u32[]{:S(2)}) collective-permute-start(bf16[2112,2560]{1,0:T(8,128)(2,1)} %param.40), channel_id=1, source_target_pairs={{0,1},{1,0},{2,3},{3,2},{4,5},{5,4},{6,7},{7,6},{8,9},{9,8},{10,11... | collective-permute-start | bytes 32440328 | tf_op jit(solution)/shard_map/ppermute | solution.py:36
  188.5 65.3 %collective-permute-start.12 = (bf16[176,2560]{1,0:T(8,128)(2,1)}, bf16[176,2560]{1,0:T(8,128)(2,1)S(1)}, u32[]{:S(2)}, u32[]{:S(2)}) collective-permute-start(bf16[176,2560]{1,0:T(8,128)(2,1)} %constant_dynamic-slice_fusion.4), channel_id=1, source_target_pairs={{0,2},{2,0},{1,3},{3,1},{4,6},{6,4},{5,7},{7,5},{8,10},{10,8},{9,1... | collective-permute-start | bytes 2703368 | tf_op jit(solution)/shard_map/ppermute | solution.py:40
  254.8 144.2 %collective-permute-start.11 = (bf16[1408,2560]{1,0:T(8,128)(2,1)}, bf16[1408,2560]{1,0:T(8,128)(2,1)}, u32[]{:S(2)}, u32[]{:S(2)}) collective-permute-start(bf16[1408,2560]{1,0:T(8,128)(2,1)} %all-gather.6.cloned.1.call-done), channel_id=1, source_target_pairs={{0,1},{1,0},{2,3},{3,2},{4,5},{5,4},{6,7},{7,6},{8,9},{9,8},{10,11... | collective-permute-start | bytes 21626888 | tf_op jit(solution)/shard_map/ppermute | solution.py:36
  320.9 187.3 %collective-permute-start.13 = (bf16[704,2560]{1,0:T(8,128)(2,1)}, bf16[704,2560]{1,0:T(8,128)(2,1)}, u32[]{:S(2)}, u32[]{:S(2)}) collective-permute-start(bf16[704,2560]{1,0:T(8,128)(2,1)} %all-gather.8.cloned.1.call-done), channel_id=1, source_target_pairs={{0,1},{1,0},{2,3},{3,2},{4,5},{5,4},{6,7},{7,6},{8,9},{9,8},{10,11... | collective-permute-start | bytes 10813448 | tf_op jit(solution)/shard_map/ppermute | solution.py:36
  396.3 290.5 %collective-permute-start.31 = (bf16[3,264,1408]{2,1,0:T(8,128)(2,1)}, bf16[3,264,1408]{2,1,0:T(8,128)(2,1)}, u32[]{:S(2)}, u32[]{:S(2)}) collective-permute-start(bf16[3,264,1408]{2,1,0:T(8,128)(2,1)} %get-tuple-element.127), channel_id=1, source_target_pairs={{2,0},{3,1},{6,4},{7,5},{10,8},{11,9},{14,12},{15,13}} | collective-permute-start | bytes 6690824 | tf_op jit(solution)/shard_map/ppermute | solution.py:183
  397.6 313.5 %collective-permute-start.30 = (bf16[3,264,1408]{2,1,0:T(8,128)(2,1)}, bf16[3,264,1408]{2,1,0:T(8,128)(2,1)}, u32[]{:S(2)}, u32[]{:S(2)}) collective-permute-start(bf16[3,264,1408]{2,1,0:T(8,128)(2,1)} %get-tuple-element.127), channel_id=1, source_target_pairs={{1,0},{5,4},{9,8},{13,12}} | collective-permute-start | bytes 6690824 | tf_op jit(solution)/shard_map/ppermute | solution.py:184
  472.0 298.8 %collective-permute-start.14 = (bf16[3,264,1408]{2,1,0:T(8,128)(2,1)}, bf16[3,264,1408]{2,1,0:T(8,128)(2,1)}, u32[]{:S(2)}, u32[]{:S(2)}) collective-permute-start(bf16[3,264,1408]{2,1,0:T(8,128)(2,1)} %slice.220), channel_id=1, source_target_pairs={{0,1},{1,0},{2,3},{3,2},{4,5},{5,4},{6,7},{7,6},{8,9},{9,8},{10,11... | collective-permute-start | bytes 6690824 | tf_op jit(solution)/shard_map/ppermute | solution.py:36
  499.5 206.8 %collective-permute-start.15 = (bf16[3,264,1408]{2,1,0:T(8,128)(2,1)}, bf16[3,264,1408]{2,1,0:T(8,128)(2,1)}, u32[]{:S(2)}, u32[]{:S(2)}) collective-permute-start(bf16[3,264,1408]{2,1,0:T(8,128)(2,1)} %slice.222), channel_id=1, source_target_pairs={{0,1},{1,0},{2,3},{3,2},{4,5},{5,4},{6,7},{7,6},{8,9},{9,8},{10,11... | collective-permute-start | bytes 6690824 | tf_op jit(solution)/shard_map/ppermute | solution.py:36
  603.4 317.6 %collective-permute-start.20 = (bf16[6,264,1408]{2,1,0:T(8,128)(2,1)}, bf16[6,264,1408]{2,1,0:T(8,128)(2,1)}, u32[]{:S(2)}, u32[]{:S(2)}) collective-permute-start(bf16[6,264,1408]{2,1,0:T(8,128)(2,1)} %get-tuple-element.159), channel_id=1, source_target_pairs={{0,1},{1,0},{2,3},{3,2},{4,5},{5,4},{6,7},{7,6},{8,9},{9,8},{10,11... | collective-permute-start | bytes 13381640 | tf_op jit(solution)/shard_map/ppermute | solution.py:36
  706.3 227.7 %collective-permute-start.21 = (bf16[6,264,1408]{2,1,0:T(8,128)(2,1)}, bf16[6,264,1408]{2,1,0:T(8,128)(2,1)}, u32[]{:S(2)}, u32[]{:S(2)}) collective-permute-start(bf16[6,264,1408]{2,1,0:T(8,128)(2,1)} %get-tuple-element.161), channel_id=1, source_target_pairs={{0,1},{1,0},{2,3},{3,2},{4,5},{5,4},{6,7},{7,6},{8,9},{9,8},{10,11... | collective-permute-start | bytes 13381640 | tf_op jit(solution)/shard_map/ppermute | solution.py:36
  711.1 222.9 %collective-permute-start.22 = (bf16[6,264,1408]{2,1,0:T(8,128)(2,1)}, bf16[6,264,1408]{2,1,0:T(8,128)(2,1)}, u32[]{:S(2)}, u32[]{:S(2)}) collective-permute-start(bf16[6,264,1408]{2,1,0:T(8,128)(2,1)} %get-tuple-element.163), channel_id=1, source_target_pairs={{0,1},{1,0},{2,3},{3,2},{4,5},{5,4},{6,7},{7,6},{8,9},{9,8},{10,11... | collective-permute-start | bytes 13381640 | tf_op jit(solution)/shard_map/ppermute | solution.py:36
  711.1 68.1 %collective-permute-start.16 = (bf16[3,264,1408]{2,1,0:T(8,128)(2,1)}, bf16[3,264,1408]{2,1,0:T(8,128)(2,1)}, u32[]{:S(2)}, u32[]{:S(2)}) collective-permute-start(bf16[3,264,1408]{2,1,0:T(8,128)(2,1)} %add_convert_fusion.2), channel_id=1, source_target_pairs={{0,2},{2,0},{1,3},{3,1},{4,6},{6,4},{5,7},{7,5},{8,10},{10,8},{9,1... | collective-permute-start | bytes 6690824 | tf_op jit(solution)/shard_map/ppermute | solution.py:40
  770.8 173.3 %collective-permute-start.23 = (bf16[6,264,1408]{2,1,0:T(8,128)(2,1)}, bf16[6,264,1408]{2,1,0:T(8,128)(2,1)}, u32[]{:S(2)}, u32[]{:S(2)}) collective-permute-start(bf16[6,264,1408]{2,1,0:T(8,128)(2,1)} %get-tuple-element.165), channel_id=1, source_target_pairs={{0,1},{1,0},{2,3},{3,2},{4,5},{5,4},{6,7},{7,6},{8,9},{9,8},{10,11... | collective-permute-start | bytes 13381640 | tf_op jit(solution)/shard_map/ppermute | solution.py:36
  921.0 67.0 %collective-permute-start.24 = (bf16[6,264,1408]{2,1,0:T(8,128)(2,1)}, bf16[6,264,1408]{2,1,0:T(8,128)(2,1)}, u32[]{:S(2)}, u32[]{:S(2)}) collective-permute-start(bf16[6,264,1408]{2,1,0:T(8,128)(2,1)} %get-tuple-element.167), channel_id=1, source_target_pairs={{0,1},{1,0},{2,3},{3,2},{4,5},{5,4},{6,7},{7,6},{8,9},{9,8},{10,11... | collective-permute-start | bytes 13381640 | tf_op jit(solution)/shard_map/ppermute | solution.py:36
  927.1 51.5 %collective-permute-start.18 = (bf16[3,264,1408]{2,1,0:T(8,128)(2,1)S(1)}, bf16[3,264,1408]{2,1,0:T(8,128)(2,1)}, u32[]{:S(2)}, u32[]{:S(2)}) collective-permute-start(bf16[3,264,1408]{2,1,0:T(8,128)(2,1)S(1)} %fusion.89), channel_id=1, source_target_pairs={{0,2},{2,0},{1,3},{3,1},{4,6},{6,4},{5,7},{7,5},{8,10},{10,8},{9,1... | collective-permute-start | bytes 6690824 | tf_op jit(solution)/shard_map/ppermute | solution.py:40
  934.0 140.3 %collective-permute-start.25 = (bf16[4,4,88,1408]{3,2,1,0:T(8,128)(2,1)}, bf16[4,4,88,1408]{3,2,1,0:T(8,128)(2,1)}, u32[]{:S(2)}, u32[]{:S(2)}) collective-permute-start(bf16[4,4,88,1408]{3,2,1,0:T(8,128)(2,1)} %slice.229), channel_id=1, source_target_pairs={{0,1},{1,0},{2,3},{3,2},{4,5},{5,4},{6,7},{7,6},{8,9},{9,8},{10,11... | collective-permute-start | bytes 11894792 | tf_op jit(solution)/shard_map/ppermute | solution.py:36
  934.0 140.3 %collective-permute-start.27 = (bf16[4,4,88,1408]{3,2,1,0:T(8,128)(2,1)}, bf16[4,4,88,1408]{3,2,1,0:T(8,128)(2,1)}, u32[]{:S(2)}, u32[]{:S(2)}) collective-permute-start(bf16[4,4,88,1408]{3,2,1,0:T(8,128)(2,1)} %add_convert_fusion), channel_id=1, source_target_pairs={{0,2},{2,0},{1,3},{3,1},{4,6},{6,4},{5,7},{7,5},{8,10},{10,8},{9,1... | collective-permute-start | bytes 11894792 | tf_op jit(solution)/shard_map/ppermute | solution.py:40
  948.9 117.2 %collective-permute-start.17 = (bf16[3,264,1408]{2,1,0:T(8,128)(2,1)S(1)}, bf16[3,264,1408]{2,1,0:T(8,128)(2,1)}, u32[]{:S(2)}, u32[]{:S(2)}) collective-permute-start(bf16[3,264,1408]{2,1,0:T(8,128)(2,1)S(1)} %fusion.89), channel_id=1, source_target_pairs={{0,1},{1,0},{2,3},{3,2},{4,5},{5,4},{6,7},{7,6},{8,9},{9,8},{10,11... | collective-permute-start | bytes 6690824 | tf_op jit(solution)/shard_map/ppermute | solution.py:36
  978.6 87.5 %collective-permute-start.19 = (bf16[3,264,1408]{2,1,0:T(8,128)(2,1)}, bf16[3,264,1408]{2,1,0:T(8,128)(2,1)}, u32[]{:S(2)}, u32[]{:S(2)}) collective-permute-start(bf16[3,264,1408]{2,1,0:T(8,128)(2,1)} %collective-permute-done.18), channel_id=1, source_target_pairs={{0,1},{1,0},{2,3},{3,2},{4,5},{5,4},{6,7},{7,6},{8,9},{9,8},{10,11... | collective-permute-start | bytes 6690824 | tf_op jit(solution)/shard_map/ppermute | solution.py:36
  988.0 75.7 %collective-permute-start.29 = (f32[9602]{0:T(1024)S(1)}, f32[9602]{0:T(1024)S(1)}, u32[]{:S(2)}, u32[]{:S(2)}) collective-permute-start(f32[9602]{0:T(1024)S(1)} %add.314), channel_id=1, source_target_pairs={{0,2},{2,0},{1,3},{3,1},{4,6},{6,4},{5,7},{7,5},{8,10},{10,8},{9,1... | collective-permute-start | bytes 115232 | tf_op jit(solution)/shard_map/ppermute | solution.py:40
  (173 other events, 3267.9 us)
Sparse Core Ops, SparseCore 0:
  37.9 48.2 all-gather.3
  88.0 73.9 all-gather.5
  254.8 45.2 all-gather.7

commit v3 on v2

v3 whole, which is shorter than its diff:
```python
import functools

import jax
import jax.numpy as jnp
from jax import lax
from jax.experimental import pallas as pl
from jax.experimental.pallas import tpu as pltpu
from jax.sharding import PartitionSpec as P


LN_EPS = 1e-5
TO_F = 'btd,fd->btf'
FROM_F = 'btf,fd->btd'
WGRAD = 'btf,btd->fd'
F32 = jnp.float32
BF16 = jnp.bfloat16
SIB = [(0, 1), (1, 0), (2, 3), (3, 2)]
ACROSS = [(0, 2), (2, 0), (1, 3), (3, 1)]


def layer_norm(values, ln_gain, ln_bias):
    row_mean = jnp.mean(values, axis=-1, keepdims=True)
    centred = values - row_mean
    row_var = jnp.mean(centred * centred, axis=-1, keepdims=True)
    return (centred * lax.rsqrt(row_var + LN_EPS) * ln_gain + ln_bias).astype(BF16)


def mm(eq_form, lhs_in, rhs_in):
    return jnp.einsum(eq_form, lhs_in, rhs_in, preferred_element_type=F32)


LANES = 128


def probs_t(q_block, k_block, real_rows, scale):
    scores = lax.dot_general(k_block, q_block, (((1,), (1,)), ((), ())), preferred_element_type=F32) * scale
    key = lax.broadcasted_iota(jnp.int32, scores.shape, 0)
    scores = jnp.where(key < real_rows, scores, -1e30)
    top = jnp.max(scores, axis=0, keepdims=True)
    expd = jnp.exp(scores - top)
    return expd * (1.0 / jnp.sum(expd, axis=0, keepdims=True))


def attend_kernel(real_rows, scale, count, q_ref, k_ref, v_ref, out_ref):
    for h in range(count):
        cols = pl.ds(h * LANES, LANES)
        probs = probs_t(q_ref[0, :, cols], k_ref[0, :, cols], real_rows, scale).astype(BF16)
        out = lax.dot_general(probs, v_ref[0, :, cols], (((0,), (0,)), ((), ())), preferred_element_type=F32)
        out_ref[0, :, cols] = out.astype(BF16)


def attend_back_kernel(real_rows, scale, count, q_ref, k_ref, v_ref, g_ref, dq_ref, dk_ref, dv_ref):
    for h in range(count):
        cols = pl.ds(h * LANES, LANES)
        q_block, k_block, v_block, g_block = q_ref[0, :, cols], k_ref[0, :, cols], v_ref[0, :, cols], g_ref[0, :, cols]
        probs = probs_t(q_block, k_block, real_rows, scale)
        dv_ref[0, :, cols] = jnp.dot(probs.astype(BF16), g_block, preferred_element_type=F32).astype(BF16)
        dprobs = lax.dot_general(v_block, g_block, (((1,), (1,)), ((), ())), preferred_element_type=F32).astype(BF16).astype(F32)
        dscores = probs * (dprobs - jnp.sum(probs * dprobs, axis=0, keepdims=True))
        dscores = (dscores * scale).astype(BF16)
        dk_ref[0, :, cols] = jnp.dot(dscores, q_block, preferred_element_type=F32).astype(BF16)
        dq = lax.dot_general(dscores, k_block, (((0,), (0,)), ((), ())), preferred_element_type=F32)
        dq_ref[0, :, cols] = dq.astype(BF16)


HEADS_PER_STEP = 4


def attend(q_act, k_act, v_act, real_rows, scale):
    tiles, tokens, cols = q_act.shape
    step = HEADS_PER_STEP * LANES
    spec = pl.BlockSpec((1, tokens, step), lambda t, h: (t, 0, h))
    flops = 4 * tiles * tokens * tokens * cols
    return pl.pallas_call(
        functools.partial(attend_kernel, real_rows, scale, HEADS_PER_STEP),
        out_shape=jax.ShapeDtypeStruct(q_act.shape, BF16),
        grid=(tiles, cols // step),
        in_specs=[spec] * 3,
        out_specs=spec,
        cost_estimate=pl.CostEstimate(flops=4 * flops, bytes_accessed=8 * tiles * tokens * cols, transcendentals=0),
        compiler_params=pltpu.CompilerParams(dimension_semantics=('arbitrary', 'arbitrary')))(q_act, k_act, v_act)


def attend_back(qkv, grad, real_rows, scale):
    tiles, tokens, cols = grad.shape
    step = HEADS_PER_STEP * LANES
    spec = pl.BlockSpec((1, tokens, step), lambda t, h: (t, 0, h))
    shape = jax.ShapeDtypeStruct(grad.shape, BF16)
    flops = 10 * tiles * tokens * tokens * cols
    return pl.pallas_call(
        functools.partial(attend_back_kernel, real_rows, scale, HEADS_PER_STEP),
        out_shape=(shape, shape, shape),
        grid=(tiles, cols // step),
        in_specs=[spec] * 4,
        out_specs=(spec, spec, spec),
        cost_estimate=pl.CostEstimate(flops=4 * flops, bytes_accessed=14 * tiles * tokens * cols, transcendentals=0),
        compiler_params=pltpu.CompilerParams(dimension_semantics=('arbitrary', 'arbitrary')))(*qkv, grad)


def sib(value):
    return lax.ppermute(value, 'tp', SIB)


def across(value):
    return lax.ppermute(value, 'tp', ACROSS)


def gather_piece(quarter):
    quarter = across(quarter)
    return lax.all_gather(quarter, 'dp', axis=0, tiled=True)


def partner_shard(shard, start, count):
    rows = count // 4
    quarter = lax.dynamic_slice_in_dim(shard, start + lax.axis_index('dp') * rows, rows, axis=0)
    return gather_piece(quarter)


def reduce_own(near, far):
    n = near.shape[0] // 2
    from_sib_far = sib(far[n:])
    from_sib_own = sib(near[n:])
    chip_far = (far[:n].astype(F32) + from_sib_far.astype(F32)).astype(BF16)
    from_far = across(chip_far)
    return near[:n].astype(F32) + from_sib_own.astype(F32) + from_far.astype(F32)


def by_tp(tp, parts, builders):
    return lax.switch(tp, [lambda *p, b=b: b(*p) for b in builders], *parts)


def unfilled(shape, dtype):
    return pl.pallas_call(
        lambda out_ref: None,
        out_shape=jax.ShapeDtypeStruct(shape, dtype),
        out_specs=pl.BlockSpec(memory_space=pl.ANY),
        name='unfilled')()


def put_rows(buffer, piece, start):
    return lax.dynamic_update_slice_in_dim(buffer, piece, start, axis=0)


def whole_step(hidden, inter_feats, proj_grad, w_query, w_key, w_value, w_out, ln_params, gate_params, w_fc1, b_fc1, w_fc2, b_fc2, w_proj, b_proj):
    tiles, tokens, width = hidden.shape
    real_rows, proj_dim = proj_grad.shape[1:]
    ninter = inter_feats.shape[2]
    own_n = tiles // 4
    tp = lax.axis_index('tp')
    core = tp & 1
    first = tp * own_n
    inter_t = jnp.transpose(inter_feats, (0, 2, 1, 3))
    row_ok = (jnp.arange(tokens) < real_rows)[None, :, None]
    gate_attn = jnp.tanh(gate_params[0])
    gate_mlp = jnp.tanh(gate_params[1])

    def own(value):
        return lax.dynamic_slice_in_dim(value, first, own_n, axis=0)

    def group_of(value, other):
        return lax.dynamic_slice_in_dim(value, (tp ^ other) * own_n, own_n, axis=0)

    att_own = jnp.stack([jnp.transpose(w_query, (1, 2, 0)), jnp.transpose(w_key, (1, 2, 0)), jnp.transpose(w_value, (1, 2, 0)), w_out])
    heads, head_dim = att_own.shape[1:3]
    att_rows = att_own.reshape(4 * heads * head_dim, width)
    att_sib = sib(att_rows)
    att_far = partner_shard(att_rows, 0, att_rows.shape[0])
    att_far_sib = sib(att_far)

    score_scale = head_dim ** -0.5

    def head_group(*shards):
        group = jnp.concatenate([v.reshape(4, heads, head_dim, width) for v in shards], axis=1)
        group = jnp.pad(group, ((0, 0), (0, 0), (0, LANES - head_dim), (0, 0)))
        return group.reshape(4, -1, width)

    shard_rows = w_proj.shape[0]
    half = shard_rows - width
    wp_sib = sib(w_proj)

    def far_head(own_core):
        quarter = half // 4
        start = core * half + lax.axis_index('dp') * quarter
        piece = jnp.where(core == own_core, lax.dynamic_slice_in_dim(w_proj, start, quarter), lax.dynamic_slice_in_dim(wp_sib, start, quarter))
        mine = gather_piece(piece)
        return mine, sib(mine)

    even, even_sib = far_head(0)
    odd, odd_sib = far_head(1)
    tail = partner_shard(w_proj, width, half)
    tail_sib = sib(tail)
    far_even = 2 * (1 - tp // 2) * shard_rows
    far_odd = far_even + shard_rows
    wp_all = unfilled((4 * shard_rows, proj_dim), BF16)
    wp_all = put_rows(wp_all, w_proj, tp * shard_rows)
    wp_all = put_rows(wp_all, wp_sib, (tp ^ 1) * shard_rows)
    for start, mine, other in ((far_even, even, even_sib), (far_odd, odd, odd_sib)):
        wp_all = put_rows(wp_all, mine, start + core * half)
        wp_all = put_rows(wp_all, other, start + (1 - core) * half)
    wp_all = put_rows(wp_all, tail, (tp ^ 2) * shard_rows + width)
    wp_all = put_rows(wp_all, tail_sib, (tp ^ 3) * shard_rows + width)
    wp_planes = wp_all.reshape(ninter + 1, width, proj_dim)
    wp_first = by_tp(tp, (w_proj, wp_sib, even, even_sib), [
        lambda o, s, e, es: o[:width],
        lambda o, s, e, es: s[:width],
        lambda o, s, e, es: jnp.concatenate([e, es], axis=0),
        lambda o, s, e, es: jnp.concatenate([es, e], axis=0)])

    pg = jnp.pad(proj_grad, ((0, 0), (0, tokens - real_rows), (0, 0)))

    hid_own = own(hidden).astype(F32)
    normed, norm1_pull = jax.vjp(layer_norm, hid_own, ln_params[0], ln_params[1])

    def attention(weights):
        qkv = [mm(TO_F, normed, weights[j]).astype(BF16) for j in range(3)]
        context = attend(*qkv, real_rows, score_scale)
        return mm(FROM_F, context, weights[3]), context, qkv

    w_near = head_group(att_rows, att_sib)
    attn_near, context_near, qkv_near = attention(w_near)
    w_far = head_group(att_far, att_far_sib)
    attn_far, context_far, qkv_far = attention(w_far)
    attn_out = attn_near + attn_far
    x_one = (hid_own + gate_attn * attn_out).astype(BF16)

    x_far = across(x_one)
    x_sib = sib(x_one)
    x_far_sib = sib(x_far)
    x_all = jnp.concatenate([x_one, x_sib, x_far, x_far_sib], axis=0)

    grad_x_two = mm(TO_F, pg, wp_first).astype(BF16)
    grad_mlp_low = (gate_mlp * grad_x_two.astype(F32)).astype(BF16)
    gx_own = own(grad_x_two)
    gm_all = jnp.concatenate([own(grad_mlp_low), group_of(grad_mlp_low, 1), group_of(grad_mlp_low, 2), group_of(grad_mlp_low, 3)], axis=0)

    grad_act = mm(TO_F, gm_all, w_fc2).astype(BF16)
    normed_two = layer_norm(x_all.astype(F32), ln_params[2], ln_params[3])
    pre_act = mm('btd,df->btf', normed_two, w_fc1) + b_fc1
    cdf = 0.5 * (1.0 + lax.erf(pre_act * (0.5 ** 0.5)))
    pdf = jnp.exp(-0.5 * pre_act * pre_act) * 0.3989422804014327
    mlp_act = (pre_act * cdf).astype(BF16)
    grad_pre = grad_act.astype(F32) * (cdf + pre_act * pdf)
    grad_b_fc1 = jnp.sum(grad_pre, axis=(0, 1))
    grad_pre_low = grad_pre.astype(BF16)
    pair = 2 * own_n
    gn_far = mm(TO_F, grad_pre_low[pair:], w_fc1).astype(BF16)
    gn_near = mm(TO_F, grad_pre_low[:pair], w_fc1).astype(BF16)
    mlp_sum = mm(FROM_F, mlp_act, w_fc2).astype(BF16)
    grad_normed_two = reduce_own(gn_near, gn_far).astype(BF16)
    mlp_out = reduce_own(mlp_sum[:pair], mlp_sum[pair:]) + b_fc2
    grad_w_fc1 = mm(WGRAD, normed_two, grad_pre_low)
    grad_w_fc2 = mm(WGRAD, mlp_act, gm_all)

    x_one_wide = x_one.astype(F32)
    x_two = jnp.where(row_ok, (x_one_wide + gate_mlp * mlp_out).astype(BF16), 0)
    feats_own = jnp.concatenate([x_two[:, None], own(inter_t)], axis=1)
    proj_own = mm('bntc,ncp->btp', feats_own, wp_planes)
    proj_out = (proj_own[:, :real_rows] + b_proj).astype(BF16)
    x_two_far = lax.ppermute(x_two, 'tp', [(2, 0), (3, 1)])
    x_two_sib = lax.ppermute(x_two, 'tp', [(1, 0)])
    x_two_far_sib = lax.ppermute(x_two_far, 'tp', [(1, 0)])
    part = by_tp(tp, (inter_t,), [
        lambda i: i[:, 0, :, :half],
        lambda i: i[:, 0, :, half:],
        lambda i: i[:, 3, :, :half],
        lambda i: i[:, 3, :, half:]])
    grad_w_proj = unfilled((shard_rows, proj_dim), F32)
    grad_w_proj = put_rows(grad_w_proj, mm(WGRAD, part, pg), (1 - core) * width)
    plane = by_tp(tp, (inter_t, x_two, x_two_sib, x_two_far, x_two_far_sib), [
        lambda i, o, s, f, fs: jnp.concatenate([o, s, f, fs], axis=0),
        lambda i, o, s, f, fs: i[:, 1],
        lambda i, o, s, f, fs: i[:, 2],
        lambda i, o, s, f, fs: i[:, 4]])
    grad_w_proj = put_rows(grad_w_proj, mm(WGRAD, plane, pg), core * half)

    half_tiles = tiles // 2
    grad_inter = unfilled((tiles, ninter, tokens, width), BF16)
    gi_sib = []
    for n in range(ninter):
        pg_half = lax.dynamic_slice_in_dim(pg, core * half_tiles, half_tiles, axis=0)
        gi_half = mm(TO_F, pg_half, wp_planes[n + 1]).astype(BF16)
        grad_inter = lax.dynamic_update_slice(grad_inter, gi_half[:, None], (core * half_tiles, n, 0, 0))
        gi_sib.append(sib(gi_half))
    for n in range(ninter):
        grad_inter = lax.dynamic_update_slice(grad_inter, gi_sib[n][:, None], ((1 - core) * half_tiles, n, 0, 0))
    grad_inter = jnp.transpose(grad_inter, (0, 2, 1, 3))

    _, norm2_pull = jax.vjp(layer_norm, x_one_wide, ln_params[2], ln_params[3])
    grad_x_ln_two, grad_gain_two, grad_bias_two = norm2_pull(grad_normed_two)
    gx_own_wide = gx_own.astype(F32)
    grad_x_one = (gx_own_wide + grad_x_ln_two).astype(BF16).astype(F32)
    grad_attn_low = (gate_attn * grad_x_one).astype(BF16)

    def attention_back(weights, qkv):
        grad_context = mm(TO_F, grad_attn_low, weights[3]).astype(BF16)
        grads = attend_back(qkv, grad_context, real_rows, score_scale)
        return grads, sum(mm(FROM_F, g, weights[j]) for j, g in enumerate(grads))

    def attention_dw(grads, context):
        parts = [mm(WGRAD, g, normed) for g in grads] + [mm(WGRAD, context, grad_attn_low)]
        return jnp.stack([d.astype(BF16).reshape(-1, LANES, width)[:, :head_dim] for d in parts])

    gqkv_far, gnorm_far = attention_back(w_far, qkv_far)
    dw_far2 = attention_dw(gqkv_far, context_far)
    dw_far_from_sib = sib(dw_far2[:, heads:])
    dw_from_far = across((dw_far2[:, :heads].astype(F32) + dw_far_from_sib.astype(F32)).astype(BF16))
    gqkv_near, gnorm_near = attention_back(w_near, qkv_near)
    grad_normed = (gnorm_near + gnorm_far).astype(BF16)
    grad_x_ln, grad_gain, grad_bias = norm1_pull(grad_normed)
    gh_own = (grad_x_one + grad_x_ln).astype(BF16)
    gh_far = across(gh_own)
    gh_sib = sib(gh_own)
    gh_far_sib = sib(gh_far)
    dw_near2 = attention_dw(gqkv_near, context_near)
    dw_near_from_sib = sib(dw_near2[:, heads:])
    grad_hidden = by_tp(tp, (gh_own, gh_sib, gh_far, gh_far_sib), [
        lambda o, s, f, fs: jnp.concatenate([o, s, f, fs], axis=0),
        lambda o, s, f, fs: jnp.concatenate([s, o, fs, f], axis=0),
        lambda o, s, f, fs: jnp.concatenate([f, fs, o, s], axis=0),
        lambda o, s, f, fs: jnp.concatenate([fs, f, s, o], axis=0)])
    dw_own = dw_near2[:, :heads].astype(F32) + dw_near_from_sib.astype(F32) + dw_from_far.astype(F32)
    grad_w_query = jnp.transpose(dw_own[0], (2, 0, 1))
    grad_w_key = jnp.transpose(dw_own[1], (2, 0, 1))
    grad_w_value = jnp.transpose(dw_own[2], (2, 0, 1))
    grad_w_out = dw_own[3]

    mlp_out_late, _ = lax.optimization_barrier((mlp_out, grad_normed))
    grad_gate_mlp = jnp.sum(gx_own_wide * mlp_out_late) * (1.0 - gate_mlp * gate_mlp)
    grad_gate_attn = jnp.sum(grad_x_one * attn_out) * (1.0 - gate_attn * gate_attn)
    small = jnp.concatenate([
        grad_gain, grad_bias, grad_gain_two, grad_bias_two,
        jnp.sum(gate_mlp * gx_own_wide, axis=(0, 1)),
        jnp.sum(own(proj_grad), axis=(0, 1), dtype=F32),
        grad_gate_attn[None], grad_gate_mlp[None]])
    small = small + sib(small)
    small = small + across(small)
    grad_ln = small[:4 * width].reshape(4, width)
    grad_b_fc2 = small[4 * width:5 * width]
    grad_b_proj = small[5 * width:5 * width + proj_dim]
    grad_gates = small[5 * width + proj_dim:]
    return (proj_out, grad_hidden, grad_inter, grad_w_query, grad_w_key, grad_w_value, grad_w_out, grad_ln, grad_gates, grad_w_fc1, grad_b_fc1, grad_w_fc2, grad_b_fc2, grad_w_proj, grad_b_proj)


def solution(mesh):
    tiles_spec = P('dp', None, None)
    inter_spec = P('dp', None, None, None)
    head_cols = P(None, 'tp', None)
    in_specs = (tiles_spec, inter_spec, tiles_spec, head_cols, head_cols, head_cols, P('tp', None, None), P(None, None), P(None), P(None, 'tp'), P('tp'), P('tp', None), P(None), P('tp', None), P(None))
    grad_heads = P('dp', 'tp', None)
    out_specs = (P(('dp', 'tp'), None, None), tiles_spec, inter_spec, grad_heads, grad_heads, grad_heads, P(('dp', 'tp'), None, None), P('dp', None), P('dp'), P('dp', 'tp'), P(('dp', 'tp')), P(('dp', 'tp'), None), P('dp'), P(('dp', 'tp'), None), P('dp'))
    return jax.shard_map(whole_step, mesh=mesh, in_specs=in_specs, out_specs=out_specs, check_vma=False)
```

time: 1100 us -> 1090 us (level)
  Pallas kernels: 0.01 us -> 55.7 us
  matrix products: 522 us -> 487 us
  other arithmetic: 145 us -> 116 us
    pallas_call x0 -> x4, Pallas kernels: none -> 55.7 us  [the longest x2 35.6 us: attend_back(): pl.pallas_call(functools.partial(attend_back_kernel, real_rows, scale, HE...]
    all_gather x3 -> x4, waiting for transfers between devices: 0.04 us -> 42 us  [gather_piece(): return lax.all_gather(quarter, 'dp', axis=0, tiled=True)]
    ppermute x9 -> x10, waiting for transfers between devices: 243 us -> 201 us  [across(): return lax.ppermute(value, 'tp', ACROSS)]
    dot_general x56 -> x40, matrix products: 522 us -> 487 us  [mm(): return jnp.einsum(eq_form, lhs_in, rhs_in, preferred_element_type=F32)]
    sub x2 -> x0, other arithmetic: 21.9 us -> none  [attend(): jax.nn.softmax(jnp.where(key_ok, scores, -1e+30), axis=-1).astype(BF16)]
    unnamed x322 -> x210, local copies, waits for them, and re-layouts: 23.6 us -> 7.93 us
    dynamic_update_slice x6 -> x8, local copies, waits for them, and re-layouts: 36.3 us -> 51.9 us  [put_rows(): return lax.dynamic_update_slice_in_dim(buffer, piece, start, axis=0)]
    mul x1 -> x0, other arithmetic: 11.3 us -> none  [attend(): scores = mm('bhqe,bhke->bhqk', q_act, k_act) * score_scale]
  transfers between devices with their start and end apart: 36 -> 39, of which waited for: 7 -> 9; matrix products, arithmetic and copies ran while one was open for 70% -> 66% of each run, Pallas kernels for 0% -> 5%
where the time goes in v3:
time: 1090 us
  matrix products  487 us (45%)
  waiting for transfers between devices  243 us (22%)
  local copies, waits for them, and re-layouts  136 us (12%)
  other arithmetic  116 us (11%)
  Pallas kernels  55.7 us (5%)
  starting transfers between devices  29.1 us (3%)
  between operations  18 us (2%)
    dot_general x40, matrix products, mm(): return jnp.einsum(eq_form, lhs_in, rhs_in, preferred_element_type=F32)  487 us
    ppermute x10, waiting for transfers between devices, across(): return lax.ppermute(value, 'tp', ACROSS)  201 us
    dynamic_update_slice x8, local copies, waits for them, and re-layouts, put_rows(): return lax.dynamic_update_slice_in_dim(buffer, piece, start, axis=0)  51.9 us
    all_gather x4, waiting for transfers between devices, gather_piece(): return lax.all_gather(quarter, 'dp', axis=0, tiled=True)  42 us
    pallas_call x2, Pallas kernels, attend_back(): pl.pallas_call(functools.partial(attend_back_kernel, real_rows, scale, HE...  35.6 us
    dynamic_update_slice x5, local copies, waits for them, and re-layouts, whole_step(): lax.dynamic_update_slice(grad_inter, gi_sib[n][:, None], ((1 - core) * ha...  23.5 us
  transfers between devices with their start and end apart: 39, of which 9 were waited for; matrix products, arithmetic and copies ran while one was open for 66% of the time, Pallas kernels for 5%

profile of v3, /device:TPU:0, one launch (start us, length us, event | category | flops | bytes accessed | tf_op | source)
XLA Modules:
  0.0 1085.2 jit_solution(4004738597157600814)
XLA Ops:
  15.0 22.0 %collective-permute-done.1 = bf16[352,1408]{1,0:T(8,128)(2,1)} collective-permute-done((bf16[352,1408]{1,0:T(8,128)(2,1)S(1)}, bf16[352,1408]{1,0:T(8,128)(2,1)}, u32[]{:S(2)}, u32[]{:S(2)}) %collective-permute-start.1) | collective-permute-done | bytes 991264 | tf_op jit(solution)/shard_map/ppermute | solution.py:105
  43.5 41.9 %all-gather.5.cloned.1.call-done = bf16[1408,1408]{1,0:T(8,128)(2,1)} async-done(((bf16[352,1408]{1,0:T(8,128)(2,1)}), bf16[1408,1408]{1,0:T(8,128)(2,1)}) %all-gather.5.cloned.1.call-update) | async-done | bytes 3964944 | tf_op jit(solution)/shard_map/all_gather | solution.py:110
  176.0 48.2 %collective-permute-done.4 = bf16[3,264,1408]{2,1,0:T(8,128)(2,1)} collective-permute-done((bf16[3,264,1408]{2,1,0:T(8,128)(2,1)S(1)}, bf16[3,264,1408]{2,1,0:T(8,128)(2,1)}, u32[]{:S(2)}, u32[]{:S(2)}) %collective-permute-start.4) | collective-permute-done | bytes 2230304 | tf_op jit(solution)/shard_map/ppermute | solution.py:105
  226.9 20.9 %constant_dynamic-update-slice_fusion.7 = bf16[8448,2560]{1,0:T(8,128)(2,1)} fusion(bf16[8448,2560]{1,0:T(8,128)(2,1)} %unfilled.3, bf16[2112,2560]{1,0:T(8,128)(2,1)} %param.44, s32[]{:T(128)S(6)} %select_n.103), kind=kLoop, calls=%fused_computation.206 | loop fusion | bytes 21626884 | tf_op jit(solution)/shard_map/dynamic_update_slice | solution.py:141
  263.7 28.3 %multiply_convert_fusion = (bf16[12,264,1536]{2,1,0:T(8,128)(2,1)S(1)}, f32[12,264,1536]{2,1,0:T(8,128)}) fusion(f32[1536]{0:T(1024)S(1)} %copy-done.65, bf16[1408,1536]{1,0:T(8,128)(2,1)} %param.40, f32[1408]{0:T(1024)S(1)} %get-tuple-element.143, f32[1408]{0:T(1024)S(1)} %get-tuple-element.144, f32[12,264]{1,0:T(8,128)S(1)} %add_rsqrt_fusion, ...), kind=kOutput, calls=%fused_computation.32 | convolution fusion | flops 13772132352 | bytes 42485504 | tf_op jit(solution)/shard_map/btd,df->btf/dot_general | solution.py:29
  292.1 15.7 %convolution_convert_fusion.2 = bf16[12,264,1408]{2,1,0:T(8,128)(2,1)S(1)} fusion(bf16[12,264,1536]{2,1,0:T(8,128)(2,1)S(1)} %get-tuple-element.178, bf16[1536,1408]{1,0:T(8,128)(2,1)S(1)} %bitcast.334), kind=kOutput, calls=%fused_computation.47 | convolution fusion | flops 13707251712 | bytes 22978560 | tf_op jit(solution)/shard_map/btf,fd->btd/dot_general | solution.py:29
  329.2 19.2 %bitcast_dynamic-update-slice_fusion.1 = f32[2112,2560]{1,0:T(8,128)} fusion(f32[2112,2560]{1,0:T(8,128)} %unfilled.5, s32[]{:T(128)S(6)} %select_n.123, bf16[12,264,704]{2,1,0:T(8,128)(2,1)} %get-tuple-element.209, bf16[12,257,2560]{2,1,0:T(8,128)(2,1)} %param.33), kind=kOutput, calls=%fused_computation.80 | convolution fusion | flops 11418992640 | bytes 28295172 | tf_op jit(solution)/shard_map/btf,btd->fd/dot_general | solution.py:29
  375.7 31.1 %collective-permute-done.8 = bf16[3,264,1408]{2,1,0:T(8,128)(2,1)} collective-permute-done((bf16[3,264,1408]{2,1,0:T(8,128)(2,1)}, bf16[3,264,1408]{2,1,0:T(8,128)(2,1)}, u32[]{:S(2)}, u32[]{:S(2)}) %collective-permute-start.8) | collective-permute-done | bytes 2230304 | tf_op jit(solution)/shard_map/ppermute | solution.py:105
  423.4 31.6 %multiply_convert_fusion.1 = (bf16[12,264,1408]{2,1,0:T(8,128)(2,1)S(1)}, bf16[12,264,1408]{2,1,0:T(8,128)(2,1)}) fusion(f32[]{:T(128)} %bitcast.35, bf16[1408,2560]{1,0:T(8,128)(2,1)} %get-tuple-element.207, bf16[12,257,2560]{2,1,0:T(8,128)(2,1)} %param.33), kind=kOutput, calls=%fused_computation.39 | convolution fusion | flops 22855827456 | bytes 40841220 | tf_op jit(solution)/shard_map/btd,fd->btf/dot_general | solution.py:29
  457.8 29.6 %fusion.118 = (f32[1536]{0:T(1024)}, bf16[12,264,1536]{2,1,0:T(8,128)(2,1)}) fusion(f32[12,264,1536]{2,1,0:T(8,128)} %get-tuple-element.179, bf16[1536,1408]{1,0:T(8,128)(2,1)} %param.42, bf16[3,264,1408]{2,1,0:T(8,128)(2,1)S(1)} %get-tuple-element.164, bf16[3,264,1408]{2,1,0:T(8,128)(2,1)} %get-tuple-element.165, ...), kind=kOutput, calls=%fused_computation.236 | convolution fusion | flops 13779429376 | bytes 42448896 | tf_op jit(solution)/shard_map/btd,fd->btf/dot_general | solution.py:29
  530.9 17.1 %bitcast_dynamic-update-slice_fusion.6 = (bf16[12,5,264,1408]{3,2,1,0:T(8,128)(2,1)}, bf16[6,264,1408]{2,1,0:T(8,128)(2,1)}) fusion(bf16[12,5,264,1408]{3,2,1,0:T(8,128)(2,1)} %unfilled.4, s32[]{:T(128)S(6)} %select_n.121, bf16[8448,2560]{1,0:T(8,128)(2,1)} %constant_dynamic-update-slice_fusion, bf16[12,257,2560]{2,1,0:T(8,128)(2,1)S(1)} %bitcast.332), kind=kOutput, calls=%fused_computation.149 | convolution fusion | flops 11421222912 | bytes 31921152 | tf_op jit(solution)/shard_map/btd,fd->btf/dot_general | solution.py:29
  548.0 17.1 %bitcast_dynamic-update-slice_fusion.5 = (bf16[12,5,264,1408]{3,2,1,0:T(8,128)(2,1)}, bf16[6,264,1408]{2,1,0:T(8,128)(2,1)}) fusion(bf16[12,5,264,1408]{3,2,1,0:T(8,128)(2,1)} %get-tuple-element.183, s32[]{:T(128)S(6)} %select_n.121, bf16[8448,2560]{1,0:T(8,128)(2,1)} %constant_dynamic-update-slice_fusion, bf16[12,257,2560]{2,1,0:T(8,128)(2,1)S(1)} %bitcast.332), kind=kOutput, calls=%fused_computation.148 | convolution fusion | flops 11421222912 | bytes 31921152 | tf_op jit(solution)/shard_map/btd,fd->btf/dot_general | solution.py:29
  565.2 19.3 %bitcast_dynamic-update-slice_fusion.4 = (bf16[12,5,264,1408]{3,2,1,0:T(8,128)(2,1)}, bf16[6,264,1408]{2,1,0:T(8,128)(2,1)}) fusion(bf16[12,5,264,1408]{3,2,1,0:T(8,128)(2,1)} %get-tuple-element.185, s32[]{:T(128)S(6)} %select_n.121, bf16[8448,2560]{1,0:T(8,128)(2,1)} %constant_dynamic-update-slice_fusion, bf16[12,257,2560]{2,1,0:T(8,128)(2,1)} %param.33), kind=kOutput, calls=%fused_computation.147 | convolution fusion | flops 11421222912 | bytes 32351232 | tf_op jit(solution)/shard_map/btd,fd->btf/dot_general | solution.py:29
  584.5 18.8 %bitcast_dynamic-update-slice_fusion.3 = (bf16[12,5,264,1408]{3,2,1,0:T(8,128)(2,1)}, bf16[6,264,1408]{2,1,0:T(8,128)(2,1)}) fusion(bf16[12,5,264,1408]{3,2,1,0:T(8,128)(2,1)} %get-tuple-element.187, s32[]{:T(128)S(6)} %select_n.121, bf16[8448,2560]{1,0:T(8,128)(2,1)} %constant_dynamic-update-slice_fusion, bf16[12,257,2560]{2,1,0:T(8,128)(2,1)} %param.33), kind=kOutput, calls=%fused_computation.146 | convolution fusion | flops 11421222912 | bytes 32351232 | tf_op jit(solution)/shard_map/btd,fd->btf/dot_general | solution.py:29
  603.4 41.2 %fusion.46 = f32[3,264,2560]{2,1,0:T(8,128)} fusion(bf16[6,1408,2560,1]{2,1,0,3:T(8,128)(2,1)} %bitcast.279, bf16[3,5,264,1408]{3,2,1,0:T(8,128)(2,1)S(1)} %bitcast.291, bf16[3,1,264,1408]{3,2,1,0:T(8,128)(2,1)} %bitcast.39), kind=kOutput, calls=%fused_computation.118 | convolution fusion | flops 34263668736 | bytes 64745472 | tf_op jit(solution)/shard_map/bntc,ncp->btp/dot_general | solution.py:29
  644.7 25.1 %convolution_bitcast_fusion.1 = f32[1408,1536]{1,0:T(8,128)} fusion(f32[1408]{0:T(1024)S(1)} %copy-done.63, f32[1408]{0:T(1024)S(1)} %copy-done.44, f32[12,264]{1,0:T(8,128)S(1)} %copy-done.56, f32[12,264]{1,0:T(8,128)S(1)} %copy-done.47, bf16[12,264,1536]{2,1,0:T(8,128)(2,1)} %get-tuple-element.194, bf16[3,264,1408]{2,1,0:T(8,128)(2,1)} %collective-permute-done.5, ...), kind=kOutput, calls=%fused_computation.62 | convolution fusion | flops 13742936064 | bytes 27340544 | tf_op jit(solution)/shard_map/btf,btd->fd/dot_general | solution.py:29
  669.8 18.8 %bitcast_dynamic-update-slice_fusion.2 = (bf16[12,5,264,1408]{3,2,1,0:T(8,128)(2,1)}, bf16[6,264,1408]{2,1,0:T(8,128)(2,1)}) fusion(bf16[12,5,264,1408]{3,2,1,0:T(8,128)(2,1)} %get-tuple-element.189, s32[]{:T(128)S(6)} %select_n.121, bf16[8448,2560]{1,0:T(8,128)(2,1)} %constant_dynamic-update-slice_fusion, bf16[12,257,2560]{2,1,0:T(8,128)(2,1)} %param.33), kind=kOutput, calls=%fused_computation.145 | convolution fusion | flops 11421222912 | bytes 32351232 | tf_op jit(solution)/shard_map/btd,fd->btf/dot_general | solution.py:29
  699.6 23.1 %convolution_bitcast_fusion = f32[1536,1408]{1,0:T(8,128)} fusion(bf16[12,264,1536]{2,1,0:T(8,128)(2,1)} %copy-done.75, bf16[3,264,1408]{2,1,0:T(8,128)(2,1)} %copy-done.32, bf16[3,264,1408]{2,1,0:T(8,128)(2,1)} %get-tuple-element.165, bf16[3,264,1408]{2,1,0:T(8,128)(2,1)} %get-tuple-element.166, bf16[3,264,1408]{2,1,0:T(8,128)(2,1)S(1)} %copy-done.31), kind=kOutput, calls=%fused_computation.61 | convolution fusion | flops 13716172800 | bytes 27303936 | tf_op jit(solution)/shard_map/btf,btd->fd/dot_general | solution.py:29
  731.6 14.6 %collective-permute-done.18 = bf16[3,264,1408]{2,1,0:T(8,128)(2,1)} collective-permute-done((bf16[3,264,1408]{2,1,0:T(8,128)(2,1)}, bf16[3,264,1408]{2,1,0:T(8,128)(2,1)}, u32[]{:S(2)}, u32[]{:S(2)}) %collective-permute-start.18) | collective-permute-done | bytes 2230304 | tf_op jit(solution)/shard_map/ppermute | solution.py:105
  778.2 17.8 %shard_map.268 = (bf16[3,264,1024]{2,1,0:T(8,128)(2,1)}, bf16[3,264,1024]{2,1,0:T(8,128)(2,1)}, bf16[3,264,1024]{2,1,0:T(8,128)(2,1)}) custom-call(bf16[3,264,1024]{2,1,0:T(8,128)(2,1)} %convolution_convert_fusion.9.q_ref, bf16[3,264,1024]{2,1,0:T(8,128)(2,1)} %convolution_convert_fusion.8.k_ref, bf16[3,264,1024]{2,1,0:T(8,128)(2,1)} %convolution_convert_fusion.7.v_ref, ...), custom_call_target="tpu_custom_call" | custom-call | flops 8564244480 | bytes 11354112 | tf_op jit(solution)/shard_map/pallas_call | solution.py:90
  821.8 17.8 %shard_map.267 = (bf16[3,264,1024]{2,1,0:T(8,128)(2,1)}, bf16[3,264,1024]{2,1,0:T(8,128)(2,1)}, bf16[3,264,1024]{2,1,0:T(8,128)(2,1)}) custom-call(bf16[3,264,1024]{2,1,0:T(8,128)(2,1)} %convolution_convert_fusion.12.q_ref, bf16[3,264,1024]{2,1,0:T(8,128)(2,1)} %convolution_convert_fusion.11.k_ref, bf16[3,264,1024]{2,1,0:T(8,128)(2,1)} %convolution_convert_fusion.10.v_ref, ...), custom_call_target="tpu_custom_call" | custom-call | flops 8564244480 | bytes 11354112 | tf_op jit(solution)/shard_map/pallas_call | solution.py:90
  874.5 11.3 %convert_reduce_fusion.2 = (f32[1408]{0:T(1024)S(1)}, f32[3,264]{1,0:T(4,128)S(1)}, bf16[3,264,1408]{2,1,0:T(8,128)(2,1)S(1)}) fusion(f32[1408]{0:T(1024)S(1)} %copy-done.42, f32[3,264]{1,0:T(4,128)S(1)} %copy-done.40, bf16[12,264,1408]{2,1,0:T(8,128)(2,1)S(1)} %bitcast.287, s32[]{:T(128)S(6)} %select_n.100, bf16[3,264,1024]{2,1,0:T(8,128)(2,1)S(1)} %copy-done.33, ...), kind=kOutput, calls=%fused_computation.83 | convolution fusion | flops 2298292992 | bytes 31286468 | tf_op jit(solution)/shard_map/btf,fd->btd/dot_general | solution.py:29
  924.2 29.0 %bitcast_dynamic-update-slice_fusion = f32[2112,2560]{1,0:T(8,128)} fusion(f32[2112,2560]{1,0:T(8,128)} %bitcast_dynamic-update-slice_fusion.1, s32[]{:T(128)S(6)} %select_n.124, bf16[12,264,1408]{2,1,0:T(8,128)(2,1)S(1)} %bitcast.293, bf16[12,257,2560]{2,1,0:T(8,128)(2,1)} %param.33), kind=kOutput, calls=%fused_computation.40 | convolution fusion | flops 22837985280 | bytes 39559172 | tf_op jit(solution)/shard_map/btf,btd->fd/dot_general | solution.py:29
  989.4 69.4 %collective-permute-done.31 = f32[9602]{0:T(1024)S(1)} collective-permute-done((f32[9602]{0:T(1024)S(1)}, f32[9602]{0:T(1024)S(1)}, u32[]{:S(2)}, u32[]{:S(2)}) %collective-permute-start.31) | collective-permute-done | bytes 38440 | tf_op jit(solution)/shard_map/ppermute | solution.py:105
  (404 shorter events, 465.8 us)
Async XLA Ops:
  7.2 78.3 %all-gather.5.cloned.1.call-start = ((), (), s32[]{:S(2)}) async-start(), calls=%async_computation | async-start | bytes 4956160 | tf_op jit(solution)/shard_map/all_gather | solution.py:110
  37.0 314.3 %all-gather.7.cloned.1.call-start = ((), (), s32[]{:S(2)}) async-start(), calls=%async_computation.1 | async-start | bytes 4505600 | tf_op jit(solution)/shard_map/all_gather | solution.py:110
  37.2 66.2 %collective-permute-start.9 = (bf16[2112,2560]{1,0:T(8,128)(2,1)}, bf16[2112,2560]{1,0:T(8,128)(2,1)}, u32[]{:S(2)}, u32[]{:S(2)}) collective-permute-start(bf16[2112,2560]{1,0:T(8,128)(2,1)} %param.44), channel_id=1, source_target_pairs={{0,1},{1,0},{2,3},{3,2},{4,5},{5,4},{6,7},{7,6},{8,9},{9,8},{10,11... | collective-permute-start | bytes 32440328 | tf_op jit(solution)/shard_map/ppermute | solution.py:101
  129.6 241.5 %all-gather.11.cloned.1.call-start = ((), (), s32[]{:S(2)}) async-start(), calls=%async_computation.3 | async-start | bytes 4505600 | tf_op jit(solution)/shard_map/all_gather | solution.py:110
  163.2 208.1 %all-gather.9.cloned.1.call-start = ((), (), s32[]{:S(2)}) async-start(), calls=%async_computation.2 | async-start | bytes 4505600 | tf_op jit(solution)/shard_map/all_gather | solution.py:110
  176.0 72.0 %collective-permute-start.3 = (bf16[3,264,1408]{2,1,0:T(8,128)(2,1)S(1)}, bf16[3,264,1408]{2,1,0:T(8,128)(2,1)}, u32[]{:S(2)}, u32[]{:S(2)}) collective-permute-start(bf16[3,264,1408]{2,1,0:T(8,128)(2,1)S(1)} %get-tuple-element.149), channel_id=1, source_target_pairs={{0,1},{1,0},{2,3},{3,2},{4,5},{5,4},{6,7},{7,6},{8,9},{9,8},{10,11... | collective-permute-start | bytes 6690824 | tf_op jit(solution)/shard_map/ppermute | solution.py:101
  351.3 65.4 %collective-permute-start.11 = (bf16[704,2560]{1,0:T(8,128)(2,1)}, bf16[704,2560]{1,0:T(8,128)(2,1)}, u32[]{:S(2)}, u32[]{:S(2)}) collective-permute-start(bf16[704,2560]{1,0:T(8,128)(2,1)} %all-gather.7.cloned.1.call-done), channel_id=1, source_target_pairs={{0,1},{1,0},{2,3},{3,2},{4,5},{5,4},{6,7},{7,6},{8,9},{9,8},{10,11... | collective-permute-start | bytes 10813448 | tf_op jit(solution)/shard_map/ppermute | solution.py:101
  371.0 155.8 %collective-permute-start.15 = (bf16[704,2560]{1,0:T(8,128)(2,1)}, bf16[704,2560]{1,0:T(8,128)(2,1)}, u32[]{:S(2)}, u32[]{:S(2)}) collective-permute-start(bf16[704,2560]{1,0:T(8,128)(2,1)} %all-gather.11.cloned.1.call-done), channel_id=1, source_target_pairs={{0,1},{1,0},{2,3},{3,2},{4,5},{5,4},{6,7},{7,6},{8,9},{9,8},{10,11... | collective-permute-start | bytes 10813448 | tf_op jit(solution)/shard_map/ppermute | solution.py:101
  371.3 148.4 %collective-permute-start.13 = (bf16[704,2560]{1,0:T(8,128)(2,1)}, bf16[704,2560]{1,0:T(8,128)(2,1)}, u32[]{:S(2)}, u32[]{:S(2)}) collective-permute-start(bf16[704,2560]{1,0:T(8,128)(2,1)} %all-gather.9.cloned.1.call-done), channel_id=1, source_target_pairs={{0,1},{1,0},{2,3},{3,2},{4,5},{5,4},{6,7},{7,6},{8,9},{9,8},{10,11... | collective-permute-start | bytes 10813448 | tf_op jit(solution)/shard_map/ppermute | solution.py:101
  414.1 274.5 %collective-permute-start.33 = (bf16[3,264,1408]{2,1,0:T(8,128)(2,1)}, bf16[3,264,1408]{2,1,0:T(8,128)(2,1)}, u32[]{:S(2)}, u32[]{:S(2)}) collective-permute-start(bf16[3,264,1408]{2,1,0:T(8,128)(2,1)} %get-tuple-element.150), channel_id=1, source_target_pairs={{2,0},{3,1},{6,4},{7,5},{10,8},{11,9},{14,12},{15,13}} | collective-permute-start | bytes 6690824 | tf_op jit(solution)/shard_map/ppermute | solution.py:259
  415.4 307.3 %collective-permute-start.32 = (bf16[3,264,1408]{2,1,0:T(8,128)(2,1)}, bf16[3,264,1408]{2,1,0:T(8,128)(2,1)}, u32[]{:S(2)}, u32[]{:S(2)}) collective-permute-start(bf16[3,264,1408]{2,1,0:T(8,128)(2,1)} %get-tuple-element.150), channel_id=1, source_target_pairs={{1,0},{5,4},{9,8},{13,12}} | collective-permute-start | bytes 6690824 | tf_op jit(solution)/shard_map/ppermute | solution.py:260
  511.1 178.9 %collective-permute-start.17 = (bf16[3,264,1408]{2,1,0:T(8,128)(2,1)}, bf16[3,264,1408]{2,1,0:T(8,128)(2,1)}, u32[]{:S(2)}, u32[]{:S(2)}) collective-permute-start(bf16[3,264,1408]{2,1,0:T(8,128)(2,1)} %slice.271), channel_id=1, source_target_pairs={{0,1},{1,0},{2,3},{3,2},{4,5},{5,4},{6,7},{7,6},{8,9},{9,8},{10,11... | collective-permute-start | bytes 6690824 | tf_op jit(solution)/shard_map/ppermute | solution.py:101
  519.7 211.8 %collective-permute-start.16 = (bf16[3,264,1408]{2,1,0:T(8,128)(2,1)}, bf16[3,264,1408]{2,1,0:T(8,128)(2,1)}, u32[]{:S(2)}, u32[]{:S(2)}) collective-permute-start(bf16[3,264,1408]{2,1,0:T(8,128)(2,1)} %slice.269), channel_id=1, source_target_pairs={{0,1},{1,0},{2,3},{3,2},{4,5},{5,4},{6,7},{7,6},{8,9},{9,8},{10,11... | collective-permute-start | bytes 6690824 | tf_op jit(solution)/shard_map/ppermute | solution.py:101
  603.3 318.7 %collective-permute-start.25 = (bf16[6,264,1408]{2,1,0:T(8,128)(2,1)}, bf16[6,264,1408]{2,1,0:T(8,128)(2,1)}, u32[]{:S(2)}, u32[]{:S(2)}) collective-permute-start(bf16[6,264,1408]{2,1,0:T(8,128)(2,1)} %get-tuple-element.190), channel_id=1, source_target_pairs={{0,1},{1,0},{2,3},{3,2},{4,5},{5,4},{6,7},{7,6},{8,9},{9,8},{10,11... | collective-permute-start | bytes 13381640 | tf_op jit(solution)/shard_map/ppermute | solution.py:101
  694.2 52.0 %collective-permute-start.18 = (bf16[3,264,1408]{2,1,0:T(8,128)(2,1)}, bf16[3,264,1408]{2,1,0:T(8,128)(2,1)}, u32[]{:S(2)}, u32[]{:S(2)}) collective-permute-start(bf16[3,264,1408]{2,1,0:T(8,128)(2,1)} %add_convert_fusion.3), channel_id=1, source_target_pairs={{0,2},{2,0},{1,3},{3,1},{4,6},{6,4},{5,7},{7,5},{8,10},{10,8},{9,1... | collective-permute-start | bytes 6690824 | tf_op jit(solution)/shard_map/ppermute | solution.py:105
  722.7 199.5 %collective-permute-start.24 = (bf16[6,264,1408]{2,1,0:T(8,128)(2,1)}, bf16[6,264,1408]{2,1,0:T(8,128)(2,1)}, u32[]{:S(2)}, u32[]{:S(2)}) collective-permute-start(bf16[6,264,1408]{2,1,0:T(8,128)(2,1)} %get-tuple-element.188), channel_id=1, source_target_pairs={{0,1},{1,0},{2,3},{3,2},{4,5},{5,4},{6,7},{7,6},{8,9},{9,8},{10,11... | collective-permute-start | bytes 13381640 | tf_op jit(solution)/shard_map/ppermute | solution.py:101
  722.9 236.4 %collective-permute-start.23 = (bf16[6,264,1408]{2,1,0:T(8,128)(2,1)}, bf16[6,264,1408]{2,1,0:T(8,128)(2,1)}, u32[]{:S(2)}, u32[]{:S(2)}) collective-permute-start(bf16[6,264,1408]{2,1,0:T(8,128)(2,1)} %get-tuple-element.186), channel_id=1, source_target_pairs={{0,1},{1,0},{2,3},{3,2},{4,5},{5,4},{6,7},{7,6},{8,9},{9,8},{10,11... | collective-permute-start | bytes 13381640 | tf_op jit(solution)/shard_map/ppermute | solution.py:101
  731.5 192.3 %collective-permute-start.22 = (bf16[6,264,1408]{2,1,0:T(8,128)(2,1)}, bf16[6,264,1408]{2,1,0:T(8,128)(2,1)}, u32[]{:S(2)}, u32[]{:S(2)}) collective-permute-start(bf16[6,264,1408]{2,1,0:T(8,128)(2,1)} %get-tuple-element.184), channel_id=1, source_target_pairs={{0,1},{1,0},{2,3},{3,2},{4,5},{5,4},{6,7},{7,6},{8,9},{9,8},{10,11... | collective-permute-start | bytes 13381640 | tf_op jit(solution)/shard_map/ppermute | solution.py:101
  915.8 67.2 %collective-permute-start.26 = (bf16[6,264,1408]{2,1,0:T(8,128)(2,1)}, bf16[6,264,1408]{2,1,0:T(8,128)(2,1)}, u32[]{:S(2)}, u32[]{:S(2)}) collective-permute-start(bf16[6,264,1408]{2,1,0:T(8,128)(2,1)} %get-tuple-element.192), channel_id=1, source_target_pairs={{0,1},{1,0},{2,3},{3,2},{4,5},{5,4},{6,7},{7,6},{8,9},{9,8},{10,11... | collective-permute-start | bytes 13381640 | tf_op jit(solution)/shard_map/ppermute | solution.py:101
  922.0 147.3 %collective-permute-start.27 = (bf16[4,4,88,1408]{3,2,1,0:T(8,128)(2,1)}, bf16[4,4,88,1408]{3,2,1,0:T(8,128)(2,1)}, u32[]{:S(2)}, u32[]{:S(2)}) collective-permute-start(bf16[4,4,88,1408]{3,2,1,0:T(8,128)(2,1)} %slice.282), channel_id=1, source_target_pairs={{0,1},{1,0},{2,3},{3,2},{4,5},{5,4},{6,7},{7,6},{8,9},{9,8},{10,11... | collective-permute-start | bytes 11894792 | tf_op jit(solution)/shard_map/ppermute | solution.py:101
  923.8 145.6 %collective-permute-start.29 = (bf16[4,4,88,1408]{3,2,1,0:T(8,128)(2,1)}, bf16[4,4,88,1408]{3,2,1,0:T(8,128)(2,1)}, u32[]{:S(2)}, u32[]{:S(2)}) collective-permute-start(bf16[4,4,88,1408]{3,2,1,0:T(8,128)(2,1)} %add_convert_fusion), channel_id=1, source_target_pairs={{0,2},{2,0},{1,3},{3,1},{4,6},{6,4},{5,7},{7,5},{8,10},{10,8},{9,1... | collective-permute-start | bytes 11894792 | tf_op jit(solution)/shard_map/ppermute | solution.py:105
  964.1 97.1 %collective-permute-start.19 = (bf16[3,264,1408]{2,1,0:T(8,128)(2,1)S(1)}, bf16[3,264,1408]{2,1,0:T(8,128)(2,1)}, u32[]{:S(2)}, u32[]{:S(2)}) collective-permute-start(bf16[3,264,1408]{2,1,0:T(8,128)(2,1)S(1)} %fusion.74), channel_id=1, source_target_pairs={{0,1},{1,0},{2,3},{3,2},{4,5},{5,4},{6,7},{7,6},{8,9},{9,8},{10,11... | collective-permute-start | bytes 6690824 | tf_op jit(solution)/shard_map/ppermute | solution.py:101
  973.6 87.5 %collective-permute-start.21 = (bf16[3,264,1408]{2,1,0:T(8,128)(2,1)}, bf16[3,264,1408]{2,1,0:T(8,128)(2,1)}, u32[]{:S(2)}, u32[]{:S(2)}) collective-permute-start(bf16[3,264,1408]{2,1,0:T(8,128)(2,1)} %collective-permute-done.20), channel_id=1, source_target_pairs={{0,1},{1,0},{2,3},{3,2},{4,5},{5,4},{6,7},{7,6},{8,9},{9,8},{10,11... | collective-permute-start | bytes 6690824 | tf_op jit(solution)/shard_map/ppermute | solution.py:101
  983.0 75.7 %collective-permute-start.31 = (f32[9602]{0:T(1024)S(1)}, f32[9602]{0:T(1024)S(1)}, u32[]{:S(2)}, u32[]{:S(2)}) collective-permute-start(f32[9602]{0:T(1024)S(1)} %add.329), channel_id=1, source_target_pairs={{0,2},{2,0},{1,3},{3,1},{4,6},{6,4},{5,7},{7,5},{8,10},{10,8},{9,1... | collective-permute-start | bytes 115232 | tf_op jit(solution)/shard_map/ppermute | solution.py:105
  (120 other events, 3281.7 us)
Sparse Core Ops, SparseCore 0:
  37.2 48.2 all-gather.4
  129.7 43.9 all-gather.6
  175.5 43.9 all-gather.10
  248.1 43.8 all-gather.8

commit v4 on v3

--- a/solution.py
+++ b/solution.py
@@ -194,9 +194,10 @@
     wp_all = unfilled((4 * shard_rows, proj_dim), BF16)
     wp_all = put_rows(wp_all, w_proj, tp * shard_rows)
     wp_all = put_rows(wp_all, wp_sib, (tp ^ 1) * shard_rows)
-    for start, mine, other in ((far_even, even, even_sib), (far_odd, odd, odd_sib)):
-        wp_all = put_rows(wp_all, mine, start + core * half)
-        wp_all = put_rows(wp_all, other, start + (1 - core) * half)
+    wp_all = put_rows(wp_all, even, far_even + core * half)
+    wp_all = put_rows(wp_all, even_sib, far_even + (1 - core) * half)
+    wp_all = put_rows(wp_all, odd, far_odd + core * half)
+    wp_all = put_rows(wp_all, odd_sib, far_odd + (1 - core) * half)
     wp_all = put_rows(wp_all, tail, (tp ^ 2) * shard_rows + width)
     wp_all = put_rows(wp_all, tail_sib, (tp ^ 3) * shard_rows + width)
     wp_planes = wp_all.reshape(ninter + 1, width, proj_dim)
@@ -223,10 +224,12 @@
     attn_out = attn_near + attn_far
     x_one = (hid_own + gate_attn * attn_out).astype(BF16)
 
-    x_far = across(x_one)
-    x_sib = sib(x_one)
-    x_far_sib = sib(x_far)
-    x_all = jnp.concatenate([x_one, x_sib, x_far, x_far_sib], axis=0)
+    x_one_wide = x_one.astype(F32)
+    normed_own, norm2_pull = jax.vjp(layer_norm, x_one_wide, ln_params[2], ln_params[3])
+    n2_far = across(normed_own)
+    n2_sib = sib(normed_own)
+    n2_far_sib = sib(n2_far)
+    normed_two = jnp.concatenate([normed_own, n2_sib, n2_far, n2_far_sib], axis=0)
 
     grad_x_two = mm(TO_F, pg, wp_first).astype(BF16)
     grad_mlp_low = (gate_mlp * grad_x_two.astype(F32)).astype(BF16)
@@ -234,7 +237,6 @@
     gm_all = jnp.concatenate([own(grad_mlp_low), group_of(grad_mlp_low, 1), group_of(grad_mlp_low, 2), group_of(grad_mlp_low, 3)], axis=0)
 
     grad_act = mm(TO_F, gm_all, w_fc2).astype(BF16)
-    normed_two = layer_norm(x_all.astype(F32), ln_params[2], ln_params[3])
     pre_act = mm('btd,df->btf', normed_two, w_fc1) + b_fc1
     cdf = 0.5 * (1.0 + lax.erf(pre_act * (0.5 ** 0.5)))
     pdf = jnp.exp(-0.5 * pre_act * pre_act) * 0.3989422804014327
@@ -251,11 +253,10 @@
     grad_w_fc1 = mm(WGRAD, normed_two, grad_pre_low)
     grad_w_fc2 = mm(WGRAD, mlp_act, gm_all)
 
-    x_one_wide = x_one.astype(F32)
     x_two = jnp.where(row_ok, (x_one_wide + gate_mlp * mlp_out).astype(BF16), 0)
-    feats_own = jnp.concatenate([x_two[:, None], own(inter_t)], axis=1)
+    feats_own = jnp.concatenate([x_two[:, None, :real_rows], own(inter_t)[:, :, :real_rows]], axis=1)
     proj_own = mm('bntc,ncp->btp', feats_own, wp_planes)
-    proj_out = (proj_own[:, :real_rows] + b_proj).astype(BF16)
+    proj_out = (proj_own + b_proj).astype(BF16)
     x_two_far = lax.ppermute(x_two, 'tp', [(2, 0), (3, 1)])
     x_two_sib = lax.ppermute(x_two, 'tp', [(1, 0)])
     x_two_far_sib = lax.ppermute(x_two_far, 'tp', [(1, 0)])
@@ -285,7 +286,6 @@
         grad_inter = lax.dynamic_update_slice(grad_inter, gi_sib[n][:, None], ((1 - core) * half_tiles, n, 0, 0))
     grad_inter = jnp.transpose(grad_inter, (0, 2, 1, 3))
 
-    _, norm2_pull = jax.vjp(layer_norm, x_one_wide, ln_params[2], ln_params[3])
     grad_x_ln_two, grad_gain_two, grad_bias_two = norm2_pull(grad_normed_two)
     gx_own_wide = gx_own.astype(F32)
     grad_x_one = (gx_own_wide + grad_x_ln_two).astype(BF16).astype(F32)

time: 1090 us -> 1050 us (0.963)
  other arithmetic: 116 us -> 100 us
  local copies, waits for them, and re-layouts: 136 us -> 123 us
    dynamic_update_slice x8, local copies, waits for them, and re-layouts: 51.9 us -> 35.9 us  [put_rows(): return lax.dynamic_update_slice_in_dim(buffer, piece, start, axis=0)]
    reduce_sum x3 -> x2, other arithmetic: 16.8 us -> 3.16 us  [layer_norm(): row_var = jnp.mean(centred * centred, axis=-1, keepdims=True)]
  transfers between devices with their start and end apart: 39 -> 39, of which waited for: 9 -> 8; matrix products, arithmetic and copies ran while one was open for 66% -> 66% of each run, Pallas kernels for 5% -> 5%
where the time goes in v4:
time: 1050 us
  matrix products  482 us (46%)
  waiting for transfers between devices  240 us (23%)
  local copies, waits for them, and re-layouts  123 us (12%)
  other arithmetic  100 us (10%)
  Pallas kernels  55.7 us (5%)
  starting transfers between devices  27.9 us (3%)
  between operations  17.9 us (2%)
    dot_general x40, matrix products, mm(): return jnp.einsum(eq_form, lhs_in, rhs_in, preferred_element_type=F32)  482 us
    ppermute x10, waiting for transfers between devices, across(): return lax.ppermute(value, 'tp', ACROSS)  198 us
    all_gather x4, waiting for transfers between devices, gather_piece(): return lax.all_gather(quarter, 'dp', axis=0, tiled=True)  42 us
    dynamic_update_slice x8, local copies, waits for them, and re-layouts, put_rows(): return lax.dynamic_update_slice_in_dim(buffer, piece, start, axis=0)  35.9 us
    pallas_call x2, Pallas kernels, attend_back(): pl.pallas_call(functools.partial(attend_back_kernel, real_rows, scale, HE...  35.6 us
    dynamic_update_slice x5, local copies, waits for them, and re-layouts, whole_step(): lax.dynamic_update_slice(grad_inter, gi_sib[n][:, None], ((1 - core) * ha...  23.5 us
  transfers between devices with their start and end apart: 39, of which 8 were waited for; matrix products, arithmetic and copies ran while one was open for 66% of the time, Pallas kernels for 5%

profile of v4, /device:TPU:0, one launch (start us, length us, event | category | flops | bytes accessed | tf_op | source)
XLA Modules:
  0.0 1047.0 jit_solution(4187483968539529795)
XLA Ops:
  15.0 22.0 %collective-permute-done.1 = bf16[352,1408]{1,0:T(8,128)(2,1)} collective-permute-done((bf16[352,1408]{1,0:T(8,128)(2,1)S(1)}, bf16[352,1408]{1,0:T(8,128)(2,1)}, u32[]{:S(2)}, u32[]{:S(2)}) %collective-permute-start.1) | collective-permute-done | bytes 991264 | tf_op jit(solution)/shard_map/ppermute | solution.py:105
  43.5 42.0 %all-gather.5.cloned.1.call-done = bf16[1408,1408]{1,0:T(8,128)(2,1)} async-done(((bf16[352,1408]{1,0:T(8,128)(2,1)}), bf16[1408,1408]{1,0:T(8,128)(2,1)}) %all-gather.5.cloned.1.call-update) | async-done | bytes 3964944 | tf_op jit(solution)/shard_map/all_gather | solution.py:110
  179.6 48.5 %collective-permute-done.4 = bf16[3,264,1408]{2,1,0:T(8,128)(2,1)} collective-permute-done((bf16[3,264,1408]{2,1,0:T(8,128)(2,1)}, bf16[3,264,1408]{2,1,0:T(8,128)(2,1)}, u32[]{:S(2)}, u32[]{:S(2)}) %collective-permute-start.4) | collective-permute-done | bytes 2230304 | tf_op jit(solution)/shard_map/ppermute | solution.py:105
  229.5 21.1 %collective-permute-done.12 = bf16[176,2560]{1,0:T(8,128)(2,1)} collective-permute-done((bf16[176,2560]{1,0:T(8,128)(2,1)S(1)}, bf16[176,2560]{1,0:T(8,128)(2,1)}, u32[]{:S(2)}, u32[]{:S(2)}) %collective-permute-start.12) | collective-permute-done | bytes 901152 | tf_op jit(solution)/shard_map/ppermute | solution.py:105
  250.7 24.4 %multiply_convert_fusion = (bf16[12,264,1536]{2,1,0:T(8,128)(2,1)}, f32[12,264,1536]{2,1,0:T(8,128)}) fusion(f32[1536]{0:T(1024)S(1)} %copy-done.69, bf16[1408,1536]{1,0:T(8,128)(2,1)} %param.40, bf16[3,264,1408]{2,1,0:T(8,128)(2,1)} %collective-permute-done.5, bf16[3,264,1408]{2,1,0:T(8,128)(2,1)} %collective-permute-done.4, ...), kind=kOutput, calls=%fused_computation.28 | convolution fusion | flops 13745369088 | bytes 42448896 | tf_op jit(solution)/shard_map/btd,df->btf/dot_general | solution.py:29
  275.1 18.9 %convolution_convert_fusion.2 = bf16[12,264,1408]{2,1,0:T(8,128)(2,1)S(1)} fusion(bf16[12,264,1536]{2,1,0:T(8,128)(2,1)} %get-tuple-element.175, bf16[1536,1408]{1,0:T(8,128)(2,1)} %param.42), kind=kOutput, calls=%fused_computation.39 | convolution fusion | flops 13707251712 | bytes 22978560 | tf_op jit(solution)/shard_map/btf,fd->btd/dot_general | solution.py:29
  309.2 19.2 %bitcast_dynamic-update-slice_fusion.1 = f32[2112,2560]{1,0:T(8,128)} fusion(f32[2112,2560]{1,0:T(8,128)} %unfilled.5, s32[]{:T(128)S(6)} %select_n.123, bf16[12,264,704]{2,1,0:T(8,128)(2,1)} %get-tuple-element.206, bf16[12,257,2560]{2,1,0:T(8,128)(2,1)} %param.33), kind=kOutput, calls=%fused_computation.72 | convolution fusion | flops 11418992640 | bytes 28295172 | tf_op jit(solution)/shard_map/btf,btd->fd/dot_general | solution.py:29
  366.1 20.0 %collective-permute-done.8 = bf16[3,264,1408]{2,1,0:T(8,128)(2,1)} collective-permute-done((bf16[3,264,1408]{2,1,0:T(8,128)(2,1)}, bf16[3,264,1408]{2,1,0:T(8,128)(2,1)}, u32[]{:S(2)}, u32[]{:S(2)}) %collective-permute-start.8) | collective-permute-done | bytes 2230304 | tf_op jit(solution)/shard_map/ppermute | solution.py:105
  405.8 31.6 %multiply_convert_fusion.1 = (bf16[12,264,1408]{2,1,0:T(8,128)(2,1)S(1)}, bf16[12,264,1408]{2,1,0:T(8,128)(2,1)}) fusion(f32[]{:T(128)} %bitcast.35, bf16[1408,2560]{1,0:T(8,128)(2,1)} %get-tuple-element.204, bf16[12,257,2560]{2,1,0:T(8,128)(2,1)} %param.33), kind=kOutput, calls=%fused_computation.31 | convolution fusion | flops 22855827456 | bytes 40841220 | tf_op jit(solution)/shard_map/btd,fd->btf/dot_general | solution.py:29
  440.3 29.7 %fusion.114 = (f32[1536]{0:T(1024)}, bf16[12,264,1536]{2,1,0:T(8,128)(2,1)}) fusion(f32[12,264,1536]{2,1,0:T(8,128)} %get-tuple-element.176, bf16[1536,1408]{1,0:T(8,128)(2,1)} %param.42, bf16[3,264,1408]{2,1,0:T(8,128)(2,1)S(1)} %get-tuple-element.163, bf16[3,264,1408]{2,1,0:T(8,128)(2,1)} %get-tuple-element.164, ...), kind=kOutput, calls=%fused_computation.231 | convolution fusion | flops 13779429376 | bytes 42448896 | tf_op jit(solution)/shard_map/btd,fd->btf/dot_general | solution.py:29
  481.5 10.5 convolution_convert_fusion.3
  513.5 17.1 %bitcast_dynamic-update-slice_fusion.6 = (bf16[12,5,264,1408]{3,2,1,0:T(8,128)(2,1)}, bf16[6,264,1408]{2,1,0:T(8,128)(2,1)}) fusion(bf16[12,5,264,1408]{3,2,1,0:T(8,128)(2,1)} %unfilled.4, s32[]{:T(128)S(6)} %select_n.121, bf16[8448,2560]{1,0:T(8,128)(2,1)} %constant_dynamic-update-slice_fusion, bf16[12,257,2560]{2,1,0:T(8,128)(2,1)S(1)} %bitcast.333), kind=kOutput, calls=%fused_computation.143 | convolution fusion | flops 11421222912 | bytes 31921152 | tf_op jit(solution)/shard_map/btd,fd->btf/dot_general | solution.py:29
  530.7 17.1 %bitcast_dynamic-update-slice_fusion.5 = (bf16[12,5,264,1408]{3,2,1,0:T(8,128)(2,1)}, bf16[6,264,1408]{2,1,0:T(8,128)(2,1)}) fusion(bf16[12,5,264,1408]{3,2,1,0:T(8,128)(2,1)} %get-tuple-element.180, s32[]{:T(128)S(6)} %select_n.121, bf16[8448,2560]{1,0:T(8,128)(2,1)} %constant_dynamic-update-slice_fusion, bf16[12,257,2560]{2,1,0:T(8,128)(2,1)S(1)} %bitcast.333), kind=kOutput, calls=%fused_computation.142 | convolution fusion | flops 11421222912 | bytes 31921152 | tf_op jit(solution)/shard_map/btd,fd->btf/dot_general | solution.py:29
  547.8 17.5 %bitcast_dynamic-update-slice_fusion.4 = (bf16[12,5,264,1408]{3,2,1,0:T(8,128)(2,1)}, bf16[6,264,1408]{2,1,0:T(8,128)(2,1)}) fusion(bf16[12,5,264,1408]{3,2,1,0:T(8,128)(2,1)} %get-tuple-element.182, s32[]{:T(128)S(6)} %select_n.121, bf16[8448,2560]{1,0:T(8,128)(2,1)} %constant_dynamic-update-slice_fusion, bf16[12,257,2560]{2,1,0:T(8,128)(2,1)S(1)} %bitcast.333), kind=kOutput, calls=%fused_computation.141 | convolution fusion | flops 11421222912 | bytes 31921152 | tf_op jit(solution)/shard_map/btd,fd->btf/dot_general | solution.py:29
  565.3 18.8 %bitcast_dynamic-update-slice_fusion.3 = (bf16[12,5,264,1408]{3,2,1,0:T(8,128)(2,1)}, bf16[6,264,1408]{2,1,0:T(8,128)(2,1)}) fusion(bf16[12,5,264,1408]{3,2,1,0:T(8,128)(2,1)} %get-tuple-element.184, s32[]{:T(128)S(6)} %select_n.121, bf16[8448,2560]{1,0:T(8,128)(2,1)} %constant_dynamic-update-slice_fusion, bf16[12,257,2560]{2,1,0:T(8,128)(2,1)} %param.33), kind=kOutput, calls=%fused_computation.140 | convolution fusion | flops 11421222912 | bytes 32351232 | tf_op jit(solution)/shard_map/btd,fd->btf/dot_general | solution.py:29
  584.2 43.2 %fusion.25 = bf16[3,257,2560]{2,1,0:T(8,128)(2,1)} fusion(bf16[6,1408,2560,1]{2,1,0,3:T(8,128)(2,1)} %bitcast.283, bf16[3,5,257,1408]{3,2,1,0:T(8,128)(2,1)} %bitcast.296, bf16[3,1,257,1408]{3,2,1,0:T(8,128)(2,1)S(1)} %copy-done.31, f32[2560]{0:T(1024)S(1)} %copy-done.68), kind=kOutput, calls=%fused_computation.56 | convolution fusion | flops 33359110144 | bytes 60238336 | tf_op jit(solution)/shard_map/bntc,ncp->btp/dot_general | solution.py:29
  627.4 19.0 %bitcast_dynamic-update-slice_fusion.2 = (bf16[12,5,264,1408]{3,2,1,0:T(8,128)(2,1)}, bf16[6,264,1408]{2,1,0:T(8,128)(2,1)}) fusion(bf16[12,5,264,1408]{3,2,1,0:T(8,128)(2,1)} %get-tuple-element.186, s32[]{:T(128)S(6)} %select_n.121, bf16[8448,2560]{1,0:T(8,128)(2,1)} %constant_dynamic-update-slice_fusion, bf16[12,257,2560]{2,1,0:T(8,128)(2,1)} %param.33), kind=kOutput, calls=%fused_computation.139 | convolution fusion | flops 11421222912 | bytes 32351232 | tf_op jit(solution)/shard_map/btd,fd->btf/dot_general | solution.py:29
  653.9 23.1 %convolution_bitcast_fusion.1 = f32[1408,1536]{1,0:T(8,128)} fusion(bf16[3,264,1408]{2,1,0:T(8,128)(2,1)} %collective-permute-done.5, bf16[3,264,1408]{2,1,0:T(8,128)(2,1)} %collective-permute-done.4, bf16[3,264,1408]{2,1,0:T(8,128)(2,1)} %collective-permute-done.3, bf16[3,264,1408]{2,1,0:T(8,128)(2,1)} %fusion.54, ...), kind=kOutput, calls=%fused_computation.54 | convolution fusion | flops 13716172800 | bytes 27303936 | tf_op jit(solution)/shard_map/btf,btd->fd/dot_general | solution.py:29
  677.0 21.3 %convolution_bitcast_fusion = f32[1536,1408]{1,0:T(8,128)} fusion(bf16[12,264,1536]{2,1,0:T(8,128)(2,1)} %get-tuple-element.175, bf16[3,264,1408]{2,1,0:T(8,128)(2,1)S(1)} %copy-done.35, bf16[3,264,1408]{2,1,0:T(8,128)(2,1)S(1)} %copy-done.36, bf16[3,264,1408]{2,1,0:T(8,128)(2,1)S(1)} %copy-done.37, bf16[3,264,1408]{2,1,0:T(8,128)(2,1)S(1)} %copy-done.33), kind=kOutput, calls=%fused_computation.53 | convolution fusion | flops 13716172800 | bytes 27303936 | tf_op jit(solution)/shard_map/btf,btd->fd/dot_general | solution.py:29
  739.8 17.8 %shard_map.268 = (bf16[3,264,1024]{2,1,0:T(8,128)(2,1)}, bf16[3,264,1024]{2,1,0:T(8,128)(2,1)}, bf16[3,264,1024]{2,1,0:T(8,128)(2,1)}) custom-call(bf16[3,264,1024]{2,1,0:T(8,128)(2,1)} %convolution_convert_fusion.9.q_ref, bf16[3,264,1024]{2,1,0:T(8,128)(2,1)} %convolution_convert_fusion.8.k_ref, bf16[3,264,1024]{2,1,0:T(8,128)(2,1)} %convolution_convert_fusion.7.v_ref, ...), custom_call_target="tpu_custom_call" | custom-call | flops 8564244480 | bytes 11354112 | tf_op jit(solution)/shard_map/pallas_call | solution.py:90
  783.5 17.8 %shard_map.267 = (bf16[3,264,1024]{2,1,0:T(8,128)(2,1)}, bf16[3,264,1024]{2,1,0:T(8,128)(2,1)}, bf16[3,264,1024]{2,1,0:T(8,128)(2,1)}) custom-call(bf16[3,264,1024]{2,1,0:T(8,128)(2,1)} %convolution_convert_fusion.12.q_ref, bf16[3,264,1024]{2,1,0:T(8,128)(2,1)} %convolution_convert_fusion.11.k_ref, bf16[3,264,1024]{2,1,0:T(8,128)(2,1)} %convolution_convert_fusion.10.v_ref, ...), custom_call_target="tpu_custom_call" | custom-call | flops 8564244480 | bytes 11354112 | tf_op jit(solution)/shard_map/pallas_call | solution.py:90
  835.9 11.3 %convert_reduce_fusion.1 = (f32[1408]{0:T(1024)S(1)}, f32[3,264]{1,0:T(4,128)S(1)}, bf16[3,264,1408]{2,1,0:T(8,128)(2,1)S(1)}) fusion(f32[1408]{0:T(1024)S(1)} %copy-done.47, f32[3,264]{1,0:T(4,128)S(1)} %copy-done.45, bf16[12,264,1408]{2,1,0:T(8,128)(2,1)S(1)} %bitcast.293, s32[]{:T(128)S(6)} %select_n.100, bf16[3,264,1024]{2,1,0:T(8,128)(2,1)S(1)} %copy-done.38, ...), kind=kOutput, calls=%fused_computation.75 | convolution fusion | flops 2298292992 | bytes 31286468 | tf_op jit(solution)/shard_map/btf,fd->btd/dot_general | solution.py:29
  886.3 29.0 %bitcast_dynamic-update-slice_fusion = f32[2112,2560]{1,0:T(8,128)} fusion(f32[2112,2560]{1,0:T(8,128)} %bitcast_dynamic-update-slice_fusion.1, s32[]{:T(128)S(6)} %select_n.124, bf16[12,264,1408]{2,1,0:T(8,128)(2,1)S(1)} %bitcast.298, bf16[12,257,2560]{2,1,0:T(8,128)(2,1)} %param.33), kind=kOutput, calls=%fused_computation.32 | convolution fusion | flops 22837985280 | bytes 39559172 | tf_op jit(solution)/shard_map/btf,btd->fd/dot_general | solution.py:29
  949.9 70.7 %collective-permute-done.31 = f32[9602]{0:T(1024)S(1)} collective-permute-done((f32[9602]{0:T(1024)S(1)}, f32[9602]{0:T(1024)S(1)}, u32[]{:S(2)}, u32[]{:S(2)}) %collective-permute-start.31) | collective-permute-done | bytes 38440 | tf_op jit(solution)/shard_map/ppermute | solution.py:105
  (394 shorter events, 445.5 us)
Async XLA Ops:
  7.2 78.3 %all-gather.5.cloned.1.call-start = ((), (), s32[]{:S(2)}) async-start(), calls=%async_computation | async-start | bytes 4956160 | tf_op jit(solution)/shard_map/all_gather | solution.py:110
  37.0 310.1 %all-gather.7.cloned.1.call-start = ((), (), s32[]{:S(2)}) async-start(), calls=%async_computation.1 | async-start | bytes 4505600 | tf_op jit(solution)/shard_map/all_gather | solution.py:110
  37.2 66.2 %collective-permute-start.9 = (bf16[2112,2560]{1,0:T(8,128)(2,1)}, bf16[2112,2560]{1,0:T(8,128)(2,1)}, u32[]{:S(2)}, u32[]{:S(2)}) collective-permute-start(bf16[2112,2560]{1,0:T(8,128)(2,1)} %param.44), channel_id=1, source_target_pairs={{0,1},{1,0},{2,3},{3,2},{4,5},{5,4},{6,7},{7,6},{8,9},{9,8},{10,11... | collective-permute-start | bytes 32440328 | tf_op jit(solution)/shard_map/ppermute | solution.py:101
  129.5 231.9 %all-gather.11.cloned.1.call-start = ((), (), s32[]{:S(2)}) async-start(), calls=%async_computation.3 | async-start | bytes 4505600 | tf_op jit(solution)/shard_map/all_gather | solution.py:110
  174.0 187.9 %all-gather.9.cloned.1.call-start = ((), (), s32[]{:S(2)}) async-start(), calls=%async_computation.2 | async-start | bytes 4505600 | tf_op jit(solution)/shard_map/all_gather | solution.py:110
  179.6 71.1 %collective-permute-start.3 = (bf16[3,264,1408]{2,1,0:T(8,128)(2,1)}, bf16[3,264,1408]{2,1,0:T(8,128)(2,1)}, u32[]{:S(2)}, u32[]{:S(2)}) collective-permute-start(bf16[3,264,1408]{2,1,0:T(8,128)(2,1)} %fusion.54), channel_id=1, source_target_pairs={{0,1},{1,0},{2,3},{3,2},{4,5},{5,4},{6,7},{7,6},{8,9},{9,8},{10,11... | collective-permute-start | bytes 6690824 | tf_op jit(solution)/shard_map/ppermute | solution.py:101
  347.1 52.0 %collective-permute-start.11 = (bf16[704,2560]{1,0:T(8,128)(2,1)}, bf16[704,2560]{1,0:T(8,128)(2,1)}, u32[]{:S(2)}, u32[]{:S(2)}) collective-permute-start(bf16[704,2560]{1,0:T(8,128)(2,1)} %all-gather.7.cloned.1.call-done), channel_id=1, source_target_pairs={{0,1},{1,0},{2,3},{3,2},{4,5},{5,4},{6,7},{7,6},{8,9},{9,8},{10,11... | collective-permute-start | bytes 10813448 | tf_op jit(solution)/shard_map/ppermute | solution.py:101
  361.4 148.1 %collective-permute-start.15 = (bf16[704,2560]{1,0:T(8,128)(2,1)}, bf16[704,2560]{1,0:T(8,128)(2,1)}, u32[]{:S(2)}, u32[]{:S(2)}) collective-permute-start(bf16[704,2560]{1,0:T(8,128)(2,1)} %all-gather.11.cloned.1.call-done), channel_id=1, source_target_pairs={{0,1},{1,0},{2,3},{3,2},{4,5},{5,4},{6,7},{7,6},{8,9},{9,8},{10,11... | collective-permute-start | bytes 10813448 | tf_op jit(solution)/shard_map/ppermute | solution.py:101
  361.9 140.5 %collective-permute-start.13 = (bf16[704,2560]{1,0:T(8,128)(2,1)}, bf16[704,2560]{1,0:T(8,128)(2,1)}, u32[]{:S(2)}, u32[]{:S(2)}) collective-permute-start(bf16[704,2560]{1,0:T(8,128)(2,1)} %all-gather.9.cloned.1.call-done), channel_id=1, source_target_pairs={{0,1},{1,0},{2,3},{3,2},{4,5},{5,4},{6,7},{7,6},{8,9},{9,8},{10,11... | collective-permute-start | bytes 10813448 | tf_op jit(solution)/shard_map/ppermute | solution.py:101
  393.4 253.0 %collective-permute-start.33 = (bf16[3,264,1408]{2,1,0:T(8,128)(2,1)}, bf16[3,264,1408]{2,1,0:T(8,128)(2,1)}, u32[]{:S(2)}, u32[]{:S(2)}) collective-permute-start(bf16[3,264,1408]{2,1,0:T(8,128)(2,1)} %get-tuple-element.147), channel_id=1, source_target_pairs={{2,0},{3,1},{6,4},{7,5},{10,8},{11,9},{14,12},{15,13}} | collective-permute-start | bytes 6690824 | tf_op jit(solution)/shard_map/ppermute | solution.py:260
  394.7 303.5 %collective-permute-start.32 = (bf16[3,264,1408]{2,1,0:T(8,128)(2,1)}, bf16[3,264,1408]{2,1,0:T(8,128)(2,1)}, u32[]{:S(2)}, u32[]{:S(2)}) collective-permute-start(bf16[3,264,1408]{2,1,0:T(8,128)(2,1)} %get-tuple-element.147), channel_id=1, source_target_pairs={{1,0},{5,4},{9,8},{13,12}} | collective-permute-start | bytes 6690824 | tf_op jit(solution)/shard_map/ppermute | solution.py:261
  493.6 154.1 %collective-permute-start.17 = (bf16[3,264,1408]{2,1,0:T(8,128)(2,1)}, bf16[3,264,1408]{2,1,0:T(8,128)(2,1)}, u32[]{:S(2)}, u32[]{:S(2)}) collective-permute-start(bf16[3,264,1408]{2,1,0:T(8,128)(2,1)} %slice.275), channel_id=1, source_target_pairs={{0,1},{1,0},{2,3},{3,2},{4,5},{5,4},{6,7},{7,6},{8,9},{9,8},{10,11... | collective-permute-start | bytes 6690824 | tf_op jit(solution)/shard_map/ppermute | solution.py:101
  502.4 204.7 %collective-permute-start.16 = (bf16[3,264,1408]{2,1,0:T(8,128)(2,1)}, bf16[3,264,1408]{2,1,0:T(8,128)(2,1)}, u32[]{:S(2)}, u32[]{:S(2)}) collective-permute-start(bf16[3,264,1408]{2,1,0:T(8,128)(2,1)} %slice.273), channel_id=1, source_target_pairs={{0,1},{1,0},{2,3},{3,2},{4,5},{5,4},{6,7},{7,6},{8,9},{9,8},{10,11... | collective-permute-start | bytes 6690824 | tf_op jit(solution)/shard_map/ppermute | solution.py:101
  584.2 299.6 %collective-permute-start.25 = (bf16[6,264,1408]{2,1,0:T(8,128)(2,1)}, bf16[6,264,1408]{2,1,0:T(8,128)(2,1)}, u32[]{:S(2)}, u32[]{:S(2)}) collective-permute-start(bf16[6,264,1408]{2,1,0:T(8,128)(2,1)} %get-tuple-element.187), channel_id=1, source_target_pairs={{0,1},{1,0},{2,3},{3,2},{4,5},{5,4},{6,7},{7,6},{8,9},{9,8},{10,11... | collective-permute-start | bytes 13381640 | tf_op jit(solution)/shard_map/ppermute | solution.py:101
  651.3 55.9 %collective-permute-start.18 = (bf16[3,264,1408]{2,1,0:T(8,128)(2,1)}, bf16[3,264,1408]{2,1,0:T(8,128)(2,1)}, u32[]{:S(2)}, u32[]{:S(2)}) collective-permute-start(bf16[3,264,1408]{2,1,0:T(8,128)(2,1)} %add_convert_fusion.3), channel_id=1, source_target_pairs={{0,2},{2,0},{1,3},{3,1},{4,6},{6,4},{5,7},{7,5},{8,10},{10,8},{9,1... | collective-permute-start | bytes 6690824 | tf_op jit(solution)/shard_map/ppermute | solution.py:105
  698.2 186.1 %collective-permute-start.24 = (bf16[6,264,1408]{2,1,0:T(8,128)(2,1)}, bf16[6,264,1408]{2,1,0:T(8,128)(2,1)}, u32[]{:S(2)}, u32[]{:S(2)}) collective-permute-start(bf16[6,264,1408]{2,1,0:T(8,128)(2,1)} %get-tuple-element.185), channel_id=1, source_target_pairs={{0,1},{1,0},{2,3},{3,2},{4,5},{5,4},{6,7},{7,6},{8,9},{9,8},{10,11... | collective-permute-start | bytes 13381640 | tf_op jit(solution)/shard_map/ppermute | solution.py:101
  698.4 223.1 %collective-permute-start.23 = (bf16[6,264,1408]{2,1,0:T(8,128)(2,1)}, bf16[6,264,1408]{2,1,0:T(8,128)(2,1)}, u32[]{:S(2)}, u32[]{:S(2)}) collective-permute-start(bf16[6,264,1408]{2,1,0:T(8,128)(2,1)} %get-tuple-element.183), channel_id=1, source_target_pairs={{0,1},{1,0},{2,3},{3,2},{4,5},{5,4},{6,7},{7,6},{8,9},{9,8},{10,11... | collective-permute-start | bytes 13381640 | tf_op jit(solution)/shard_map/ppermute | solution.py:101
  707.1 177.2 %collective-permute-start.22 = (bf16[6,264,1408]{2,1,0:T(8,128)(2,1)}, bf16[6,264,1408]{2,1,0:T(8,128)(2,1)}, u32[]{:S(2)}, u32[]{:S(2)}) collective-permute-start(bf16[6,264,1408]{2,1,0:T(8,128)(2,1)} %get-tuple-element.181), channel_id=1, source_target_pairs={{0,1},{1,0},{2,3},{3,2},{4,5},{5,4},{6,7},{7,6},{8,9},{9,8},{10,11... | collective-permute-start | bytes 13381640 | tf_op jit(solution)/shard_map/ppermute | solution.py:101
  878.0 67.2 %collective-permute-start.26 = (bf16[6,264,1408]{2,1,0:T(8,128)(2,1)}, bf16[6,264,1408]{2,1,0:T(8,128)(2,1)}, u32[]{:S(2)}, u32[]{:S(2)}) collective-permute-start(bf16[6,264,1408]{2,1,0:T(8,128)(2,1)} %get-tuple-element.189), channel_id=1, source_target_pairs={{0,1},{1,0},{2,3},{3,2},{4,5},{5,4},{6,7},{7,6},{8,9},{9,8},{10,11... | collective-permute-start | bytes 13381640 | tf_op jit(solution)/shard_map/ppermute | solution.py:101
  883.8 147.4 %collective-permute-start.27 = (bf16[4,4,88,1408]{3,2,1,0:T(8,128)(2,1)}, bf16[4,4,88,1408]{3,2,1,0:T(8,128)(2,1)}, u32[]{:S(2)}, u32[]{:S(2)}) collective-permute-start(bf16[4,4,88,1408]{3,2,1,0:T(8,128)(2,1)} %slice.286), channel_id=1, source_target_pairs={{0,1},{1,0},{2,3},{3,2},{4,5},{5,4},{6,7},{7,6},{8,9},{9,8},{10,11... | collective-permute-start | bytes 11894792 | tf_op jit(solution)/shard_map/ppermute | solution.py:101
  884.3 146.8 %collective-permute-start.29 = (bf16[4,4,88,1408]{3,2,1,0:T(8,128)(2,1)}, bf16[4,4,88,1408]{3,2,1,0:T(8,128)(2,1)}, u32[]{:S(2)}, u32[]{:S(2)}) collective-permute-start(bf16[4,4,88,1408]{3,2,1,0:T(8,128)(2,1)} %add_convert_fusion), channel_id=1, source_target_pairs={{0,2},{2,0},{1,3},{3,1},{4,6},{6,4},{5,7},{7,5},{8,10},{10,8},{9,1... | collective-permute-start | bytes 11894792 | tf_op jit(solution)/shard_map/ppermute | solution.py:105
  926.2 96.7 %collective-permute-start.19 = (bf16[3,264,1408]{2,1,0:T(8,128)(2,1)S(1)}, bf16[3,264,1408]{2,1,0:T(8,128)(2,1)}, u32[]{:S(2)}, u32[]{:S(2)}) collective-permute-start(bf16[3,264,1408]{2,1,0:T(8,128)(2,1)S(1)} %fusion.68), channel_id=1, source_target_pairs={{0,1},{1,0},{2,3},{3,2},{4,5},{5,4},{6,7},{7,6},{8,9},{9,8},{10,11... | collective-permute-start | bytes 6690824 | tf_op jit(solution)/shard_map/ppermute | solution.py:101
  935.7 87.2 %collective-permute-start.21 = (bf16[3,264,1408]{2,1,0:T(8,128)(2,1)}, bf16[3,264,1408]{2,1,0:T(8,128)(2,1)}, u32[]{:S(2)}, u32[]{:S(2)}) collective-permute-start(bf16[3,264,1408]{2,1,0:T(8,128)(2,1)} %collective-permute-done.20), channel_id=1, source_target_pairs={{0,1},{1,0},{2,3},{3,2},{4,5},{5,4},{6,7},{7,6},{8,9},{9,8},{10,11... | collective-permute-start | bytes 6690824 | tf_op jit(solution)/shard_map/ppermute | solution.py:101
  945.1 75.4 %collective-permute-start.31 = (f32[9602]{0:T(1024)S(1)}, f32[9602]{0:T(1024)S(1)}, u32[]{:S(2)}, u32[]{:S(2)}) collective-permute-start(f32[9602]{0:T(1024)S(1)} %add.316), channel_id=1, source_target_pairs={{0,2},{2,0},{1,3},{3,1},{4,6},{6,4},{5,7},{7,5},{8,10},{10,8},{9,1... | collective-permute-start | bytes 115232 | tf_op jit(solution)/shard_map/ppermute | solution.py:105
  (117 other events, 2857.8 us)
Sparse Core Ops, SparseCore 0:
  37.2 48.2 all-gather.4
  129.6 43.9 all-gather.6
  175.5 43.9 all-gather.10
  250.8 43.8 all-gather.8
